TPU v7x, 256 devices: a whole 4x4x8 slice. The times are simulated.
256 devices in a mesh: px: 32 (over y, z_lo, core), py: 8 (over x, z_hi).
Axes of the slice: x: 4, y: 4, z: 8 (z_hi: 2, z_lo: 4; z = z_hi * 4 + z_lo), core: 2. Of those that a mesh axis runs over, the one named last changes fastest.
Arguments:
- spectrum: float32 [2, 3, 128, 128, 512], P(None, None, 'px', 'py'), may hold values from -3 to 3
- scalar: float32 [1024, 256, 256], P('px', 'py'), may hold values from -6 to 6
Outputs:
- tendency: float32 [2, 3, 128, 128, 512], P(None, None, 'px', 'py')
- advanced: float32 [1024, 256, 256], P('px', 'py')
All inputs are finite; a program needn't handle non-finite values.
Results may differ from a plain program's by a relative error of at most 0.0003.
Values sent between devices are 32-bit elements; how exact they have to be, the bound alone decides.
No kernel may reach another device: no remote copies, remote signals or barrier semaphores. Data moves between devices by JAX's collectives and lax.ppermute only.
A program may use at most 128 MiB of HBM per device.

v0:
```python
import math

import jax
import jax.numpy as jnp
import numpy as np
from jax import lax
from jax.experimental import pallas as pl
from jax.experimental.pallas import tpu as pltpu
from jax.sharding import PartitionSpec as P

NSUB = 3
STEP_RATIO = 0.08
DIFFUSION_RATIO = 1.0
INTERPRET = False

N1, N2, N3 = 512, 128, 128
GX, GY = 32, 8
Q2, Q3 = N2 // GX, N3 // GY
C1, C2 = N1 // GX, N2 // GY
FACTOR = 1.0 / math.sqrt(N1 * N2 * N3)
BF = jnp.bfloat16
F32 = jnp.float32


def halves(table):
    high = table.astype(np.float32).astype(BF)
    low = (table - high.astype(np.float64)).astype(np.float32).astype(BF)
    return np.asarray(high), np.asarray(low)


def waves_np(n):
    index = np.arange(n)
    return 2.0 * math.pi / n * np.where(index < n // 2, index, index - n)


def angles(n):
    index = np.arange(n)
    return 2.0 * math.pi / n * (np.outer(index, index) % n)


def first_table():
    a = angles(N1)
    return halves(np.concatenate([np.cos(a), np.sin(a)], axis=1))


def second_forward():
    a = angles(N2)
    plain = np.zeros((2, N2, N2, 2))
    plain[0, :, :, 0] = np.cos(a)
    plain[0, :, :, 1] = -np.sin(a)
    plain[1, :, :, 0] = np.sin(a)
    plain[1, :, :, 1] = np.cos(a)
    turned = np.zeros_like(plain)
    turned[0] = -plain[1]
    turned[1] = plain[0]
    both = np.stack([plain, turned]).reshape(2, 2 * N2, 2 * N2)
    return halves(both)


def third_forward():
    a = angles(N3)
    return halves(FACTOR * np.concatenate([np.cos(a), -np.sin(a)], axis=0))


def third_back():
    a = angles(N3)
    return halves(FACTOR * np.concatenate([np.cos(a), -np.sin(a)], axis=1))


def second_back():
    a = angles(N2)
    table = np.zeros((N2, 2, 2, N2))
    table[:, 0, 0] = np.cos(a)
    table[:, 0, 1] = np.sin(a)
    table[:, 1, 0] = -np.sin(a)
    table[:, 1, 1] = np.cos(a)
    return halves(table.reshape(2 * N2, 2 * N2))


def split(x):
    high = x.astype(BF)
    return high, (x - high.astype(F32)).astype(BF)


def dots(pairs, dims):
    total = None
    for left, right in pairs:
        part = lax.dot_general(left, right, (dims, ((), ())), preferred_element_type=F32)
        total = part if total is None else total + part
    return total


def dot3(left, right, dims=((1,), (0,))):
    lh, ll = left
    rh, rl = right
    return dots([(lh, rl), (ll, rh), (lh, rh)], dims)


def swap_groups(v):
    lane = lax.broadcasted_iota(jnp.int32, v[0].shape, len(v[0].shape) - 1) // 16
    axis = len(v[0].shape) - 1
    v = list(v)
    for s in (1, 2, 4):
        upper = (lane // s) % 2 == 1
        for i in range(8):
            if i & s:
                continue
            a, b = v[i], v[i + s]
            v[i] = jnp.where(upper, pltpu.roll(b, 16 * s, axis), a)
            v[i + s] = jnp.where(upper, b, pltpu.roll(a, 128 - 16 * s, axis))
    return v


def first_kernel(spec, wave, th, tl, out, y):
    rows = []
    for f in (0, 1, 2, 1, 2):
        plain, turned = [], []
        for r in range(Q2):
            re, im = spec[0, f, r], spec[1, f, r]
            plain += [re, im]
            turned += [-im, re]
        piece = jnp.concatenate(
            [jnp.concatenate(plain, axis=0), jnp.concatenate(turned, axis=0)], axis=1
        )
        rows.append(piece if len(rows) < 3 else piece * wave[...])
    table = (th[...], tl[...])
    z = dot3(table, split(jnp.concatenate(rows, axis=0)), ((1,), (1,)))
    for f in range(5):
        y[N1 * f : N1 * f + N1, :] = z[:, 128 * f : 128 * f + 128]
    for f in range(5):
        w = swap_groups([y[pl.ds(N1 * f + i, N1 // 8, stride=8), :] for i in range(8)])
        for g in range(8):
            y[pl.ds(N1 * f + g, N1 // 8, stride=8), :] = w[g]
        out[:, 16 * f : 16 * f + 16, :] = y[N1 * f : N1 * f + N1, :].reshape(GX, 16, 128)


def second_kernel(got, wave2, wave3, th, tl, out):
    c = []
    for f in range(5):
        halves_ = [got[:, 16 * f + 8 * h : 16 * f + 8 * h + 8, :].reshape(256, 128) for h in range(2)]
        c.append(jnp.concatenate(halves_, axis=1))
    k2 = wave2[...]
    k3 = wave3[...]
    curl = [k2 * c[2] - k3 * c[1], k3 * c[0] - c[4], c[3] - k2 * c[0]]
    z = []
    for group, fields in enumerate((c[:3], curl)):
        data = split(jnp.concatenate(fields, axis=1))
        z.append(dot3((th[group], tl[group]), data))
    for f in range(6):
        for ri in range(2):
            for h in range(2):
                at = ((f * 2 + ri) * 2 + h) * 16
                col = (f % 3) * 256 + h * 128
                piece = z[f // 3][ri * 128 : ri * 128 + 128, col : col + 128]
                out[:, at : at + 16, :] = piece.reshape(GY, 16, 128)


def third_kernel(got, th, tl, velocity, vorticity):
    for f in range(6):
        lines = []
        for ri in range(2):
            blocks = []
            for h in range(2):
                at = ((f * 2 + ri) * 2 + h) * 16
                blocks += swap_groups([got[q, at : at + 16, :] for q in range(GY)])
            lines.append(jnp.concatenate(blocks, axis=0))
        u = dot3(split(jnp.concatenate(lines, axis=1)), (th[...], tl[...]))
        out = velocity if f < 3 else vorticity
        out[f % 3] = u.reshape(C1, C2, N3)


def force_lines(velocity, vorticity, b, th, tl, out):
    u = [velocity[i].reshape(C1 * C2, N3) for i in range(3)]
    w = [vorticity[i].reshape(C1 * C2, N3) for i in range(3)]
    force = [u[1] * w[2] - u[2] * w[1], u[2] * w[0] - u[0] * w[2], u[0] * w[1] - u[1] * w[0] + b]
    for f in range(3):
        lines = dot3(split(force[f]), (th[...], tl[...]))
        for ri in range(2):
            for h in range(2):
                at = ((f * 2 + ri) * 2 + h) * 16
                v = [
                    lines[(h * 8 + i) * 16 : (h * 8 + i) * 16 + 16, ri * 128 : ri * 128 + 128]
                    for i in range(8)
                ]
                w8 = swap_groups(v)
                for q in range(GY):
                    out[q, at : at + 16, :] = w8[q]


def rise_tables():
    plain = np.zeros((N3, 2 * N3))
    for i in range(N3):
        plain[i, 2 * i] += 1.0
        for near in (i, (i + 1) % N3):
            plain[near, 2 * i + 1] += 9.0 / 16.0
        for far in ((i - 1) % N3, (i + 2) % N3):
            plain[far, 2 * i + 1] -= 1.0 / 16.0
    face = 0.5 * (plain + np.roll(plain, -1, axis=1))
    return np.stack([plain, face]).astype(np.float32).astype(BF)


def pair_table():
    cols = np.arange(2 * N3)[:, None] // 2
    return np.where(cols == np.arange(N3)[None], 0.125, 0.0).astype(np.float32).astype(BF)


def middle(a, b, c, d):
    return (9.0 * (b + c) - (a + d)) * (1.0 / 16.0)


def limited(first, second):
    return jnp.maximum(jnp.minimum(second, 0.0), jnp.minimum(first, jnp.maximum(second, 0.0)))


def upwind(face, left, right, jump):
    return face * jnp.where(face > 0.0, left, right) - DIFFUSION_RATIO * jump


def rolled_divergence(theta, face, axis):
    count = theta.shape[axis]
    jump = pltpu.roll(theta, count - 1, axis) - theta
    half = 0.5 * limited(pltpu.roll(jump, 1, axis), jump)
    flux = upwind(face, theta + half, pltpu.roll(theta - half, count - 1, axis), jump)
    return flux - pltpu.roll(flux, 1, axis)


EDGE = 6
SLABS = 2 * C1 + 2 * EDGE
ROWS = 2 * C2 + 16
PTS = C1 + 8
PROWS = C2 + 16


def scalar_kernel(
    scalar, x_low, x_high, y_low, y_high,
    velocity, vx_low, vx_high, vy_low, vy_high, vorticity,
    rise, pair, th, tl,
    advanced, out,
    ta, tb, vw, su, sf, f1, f2, f3, bs,
):
    for c in range(3):
        vw[c * PTS : c * PTS + 4, 8:24, :] = vx_low[c]
        vw[c * PTS + 4 : c * PTS + 20, 8:24, :] = velocity[c]
        vw[c * PTS + 20 : c * PTS + 24, 8:24, :] = vx_high[c]
        vw[c * PTS : c * PTS + 24, 4:8, :] = vy_low[c]
        vw[c * PTS : c * PTS + 24, 24:28, :] = vy_high[c]
    total = 3 * PTS * PROWS
    for c in range(3):
        table = rise[1 if c == 2 else 0]

        def third(n, carry, c=c, table=table):
            lines = vw[pl.ds(c * PTS + 8 * n, 8)].reshape(8 * PROWS, N3)
            high, low = split(lines)
            z = dots([(low, table), (high, table)], ((1,), (0,)))
            at = pl.multiple_of((c * PTS + 8 * n) * PROWS, 8)
            for h in range(2):
                su[pl.ds(h * total + at, 8 * PROWS), :] = z[:, h * 128 : h * 128 + 128]
            return carry

        lax.fori_loop(0, PTS // 8, third, 0)

    def second(n, carry, c):
        for h in range(2):
            at = pl.multiple_of(h * total + (c * PTS + n) * PROWS, 8)
            p = su[pl.ds(at, PROWS), :]
            a, b, cc, d = (p[4 + o : 25 + o] for o in range(4))
            odd, even = middle(a, b, cc, d), cc
            to = (h * 3 * PTS + c * PTS + n) * ROWS
            if c == 1:
                sf[pl.ds(to + 3, 21, stride=2), :] = 0.5 * (odd + even)
                sf[pl.ds(to + 2, 21, stride=2), :] = 0.5 * (b + odd)
            else:
                sf[pl.ds(to + 3, 21, stride=2), :] = odd
                sf[pl.ds(to + 4, 21, stride=2), :] = even
        return carry

    for c in range(3):
        lax.fori_loop(0, PTS, lambda n, k, c=c: second(n, k, c), 0)

    def first(k, carry):
        for c, face in enumerate((f1, f2, f3)):
            for h in range(2):
                cols = pl.ds(h * 128, 128)
                a, b, cc, d = (
                    sf[pl.ds(pl.multiple_of((h * 3 * PTS + c * PTS + k + o) * ROWS, 8), ROWS), :]
                    for o in range(4)
                )
                odd = middle(a, b, cc, d)
                if c == 0:
                    face[2 * k + 1, :, cols] = 0.5 * (odd + cc)
                    face[2 * k, :, cols] = 0.5 * (b + odd)
                else:
                    face[2 * k + 1, :, cols] = odd
                    face[2 * k + 2, :, cols] = cc
        return carry

    lax.fori_loop(0, 21, first, 0)

    ta[0:EDGE, 8:40, :] = x_low[...]
    ta[EDGE : EDGE + 2 * C1, 8:40, :] = scalar[...]
    ta[EDGE + 2 * C1 :, 8:40, :] = x_high[...]
    ta[:, 0:8, :] = y_low[...]
    ta[:, 40:48, :] = y_high[...]

    for turn, (source, target) in enumerate(((ta, tb), (tb, ta), (ta, tb))):
        low = 2 + 2 * turn
        t0, t1, t2, t3 = (source[low - 2 + o] for o in range(4))
        j0, j1, j2 = t1 - t0, t2 - t1, t3 - t2
        h1, h2 = 0.5 * limited(j0, j1), 0.5 * limited(j1, j2)
        flux = upwind(f1[low - 1], t1 + h1, t2 - h2, j1)

        def step(i, carry, source=source, target=target, turn=turn):
            left, jump, before = carry
            here, ahead = source[i], source[i + 1]
            next_jump = source[i + 2] - ahead
            half = 0.5 * limited(jump, next_jump)
            flux = upwind(f1[i], left, ahead - half, jump)
            change = flux - before
            change += rolled_divergence(here, f2[i], 0)
            change += rolled_divergence(here, f3[i], 1)
            fresh = here - STEP_RATIO * change
            if turn < NSUB - 1:
                target[i] = fresh
            else:
                advanced[i - EDGE] = fresh[8:40]
            return ahead + half, next_jump, flux

        lax.fori_loop(low, SLABS - low, step, (t2 + h2, j2, flux))

    def pairs(n, carry):
        lines = (advanced[pl.ds(4 * n, 4)]).reshape(2, 2, 32, 256)
        both = (lines[:, 0] + lines[:, 1]).reshape(64, 256)
        high, low = split(both)
        bs[pl.ds(pl.multiple_of(64 * n, 8), 64), :] = dots([(low, pair[...]), (high, pair[...])], ((1,), (0,)))
        return carry

    lax.fori_loop(0, C1 // 2, pairs, 0)
    buoyancy = bs[pl.ds(0, C1 * C2, stride=2), :] + bs[pl.ds(1, C1 * C2, stride=2), :]
    force_lines(velocity, vorticity, buoyancy, th, tl, out)


def second_back_kernel(got, th, tl, out):
    columns = []
    for f in range(3):
        for h in range(2):
            parts = []
            for ri in range(2):
                at = ((f * 2 + ri) * 2 + h) * 16
                parts.append(got[:, at : at + 16, :].reshape(128, 128))
            columns.append(jnp.concatenate(parts, axis=0))
    z = dot3((th[...], tl[...]), split(jnp.concatenate(columns, axis=1)))
    for f in range(3):
        for h in range(2):
            at = f * 16 + h * 8
            col = (f * 2 + h) * 128
            out[:, at : at + 8, :] = z[:, col : col + 128].reshape(GX, 8, 128)


def first_back_kernel(got, th, tl, out, y):
    rows = []
    for f in range(3):
        y[...] = got[:, 16 * f : 16 * f + 16, :].reshape(N1, 128)
        w = swap_groups([y[pl.ds(g, N1 // 8, stride=8), :] for g in range(8)])
        for i in range(8):
            y[pl.ds(i, N1 // 8, stride=8), :] = w[i]
        rows.append(y[...].T)
    z = dot3(split(jnp.concatenate(rows, axis=0)), (th[...], tl[...]))
    for f in range(3):
        for r in range(Q2):
            at = f * 128 + r * 32
            cr, ci = z[at : at + 16, :N1], z[at + 16 : at + 32, :N1]
            sr, si = z[at : at + 16, N1:], z[at + 16 : at + 32, N1:]
            out[0, f, r] = cr + si
            out[1, f, r] = ci - sr


def call(kernel, out_shape, *args, scratch=()):
    return pl.pallas_call(
        kernel,
        out_shape=out_shape,
        scratch_shapes=list(scratch),
        interpret=INTERPRET,
        name=kernel.__name__,
        compiler_params=pltpu.CompilerParams(vmem_limit_bytes=48 * 1024 * 1024),
    )(*args)


def shape(*dims):
    return jax.ShapeDtypeStruct(dims, F32)


def ring(axis):
    count = lax.axis_size(axis)
    up = [(i, (i + 1) % count) for i in range(count)]
    return up, [(b, a) for a, b in up]


def edges(axis, first, last):
    up, down = ring(axis)
    return lax.ppermute(last, axis, up), lax.ppermute(first, axis, down)


def body(spectrum, scalar):
    wave_first = np.tile(waves_np(N1).astype(np.float32), 2)[None]
    wave_second = np.repeat(waves_np(N2).astype(np.float32), 2)[:, None]
    blocks = np.tile(waves_np(N3).astype(np.float32).reshape(GY, 1, Q3), (1, 16, 1)).reshape(GY, 1, 256)
    wave_third = lax.dynamic_index_in_dim(jnp.asarray(blocks), lax.axis_index("py"), 0, keepdims=False)
    first = [jnp.asarray(t) for t in first_table()]
    second = [jnp.asarray(t) for t in second_forward()]
    third = [jnp.asarray(t) for t in third_forward()]
    x_low, x_high = edges("px", scalar[:EDGE], scalar[-EDGE:])
    strips = [
        jnp.concatenate([part[:, cut] for part in (x_low, scalar, x_high)], axis=0)
        for cut in (slice(0, 8), slice(2 * C2 - 8, 2 * C2))
    ]
    y_low, y_high = edges("py", *strips)
    sent = call(
        first_kernel, shape(GX, 80, 128), spectrum, jnp.asarray(wave_first), *first,
        scratch=(pltpu.VMEM((5 * N1, 128), F32),),
    )
    got = lax.all_to_all(sent, "px", split_axis=0, concat_axis=0, tiled=True)
    sent = call(second_kernel, shape(GY, 384, 128), got, jnp.asarray(wave_second), wave_third, *second)
    got = lax.all_to_all(sent, "py", split_axis=0, concat_axis=0, tiled=True)
    velocity, vorticity = call(
        third_kernel, (shape(3, C1, C2, N3), shape(3, C1, C2, N3)), got, *third
    )
    vx_low, vx_high = edges("px", velocity[:, :4], velocity[:, -4:])
    strips = [
        jnp.concatenate([part[:, :, cut] for part in (vx_low, velocity, vx_high)], axis=1)
        for cut in (slice(0, 4), slice(C2 - 4, C2))
    ]
    vy_low, vy_high = edges("py", *strips)
    theta, sent = call(
        scalar_kernel, (shape(2 * C1, 2 * C2, 2 * N3), shape(GY, 192, 128)),
        scalar, x_low, x_high, y_low, y_high,
        velocity, vx_low, vx_high, vy_low, vy_high, vorticity,
        jnp.asarray(rise_tables()), jnp.asarray(pair_table()), *[jnp.asarray(t) for t in third_back()],
        scratch=(
            pltpu.VMEM((SLABS, ROWS, 256), F32),
            pltpu.VMEM((SLABS, ROWS, 256), F32),
            pltpu.VMEM((3 * PTS, PROWS, N3), F32),
            pltpu.VMEM((2 * 3 * PTS * PROWS, 128), F32),
            pltpu.VMEM((2 * 3 * PTS * ROWS, 128), F32),
            pltpu.VMEM((SLABS, ROWS, 256), F32),
            pltpu.VMEM((SLABS, ROWS, 256), F32),
            pltpu.VMEM((SLABS, ROWS, 256), F32),
            pltpu.VMEM((2 * C1 * C2, 128), F32),
        ),
    )
    got = lax.all_to_all(sent, "py", split_axis=0, concat_axis=0, tiled=True)
    sent = call(
        second_back_kernel, shape(GX, 48, 128), got, *[jnp.asarray(t) for t in second_back()]
    )
    got = lax.all_to_all(sent, "px", split_axis=0, concat_axis=0, tiled=True)
    tendency = call(
        first_back_kernel, shape(2, 3, Q2, Q3, N1), got, *first,
        scratch=(pltpu.VMEM((N1, 128), F32),),
    )
    return tendency, theta


def solution(mesh):
    in_specs = (P(None, None, "px", "py", None), P("px", "py", None))
    out_specs = (P(None, None, "px", "py", None), P("px", "py", None))
    return jax.shard_map(body, mesh=mesh, in_specs=in_specs, out_specs=out_specs, check_vma=False)
```

profile of v0, /device:TPU:1, one launch (start us, length us, event | category | flops | bytes accessed | tf_op | source)
XLA Modules:
  0.0 263.7 jit_solution(16670514815747129000)
XLA Ops:
  0.6 0.0 copy-start
  0.6 1.2 copy-done
  1.9 1.2 copy-done.2
  3.1 1.1 copy-done.5
  4.2 0.7 copy-done.17
  4.9 4.4 %first_kernel.1 = f32[32,80,128]{2,1,0:T(8,128)} custom-call(f32[2,3,4,16,512]{4,3,2,1,0:T(8,128)S(1)} %copy-done.5, f32[1,1024]{1,0:T(1,128)S(1)} %copy-done.17, bf16[512,1024]{1,0:T(8,128)(2,1)S(1)} %copy-done, bf16[512,1024]{1,0:T(8,128)(2,1)S(1)} %copy-done.2), custom_call_target="tpu_custom_call" | custom-call | tf_op jit(solution)/shard_map/first_kernel/pallas_call | solution.py:378
  9.3 10.3 %all-to-all-start = ((f32[32,80,128]{2,1,0:T(8,128)}), f32[32,80,128]{2,1,0:T(8,128)S(1)}, u32[]{:S(2)}, u32[]{:S(2)}) async-start(f32[32,80,128]{2,1,0:T(8,128)} %first_kernel.1), calls=%async_computation | async-start | bytes 2621440 | tf_op jit(solution)/shard_map/all_to_all | solution.py:421
  19.7 0.7 dynamic-slice_bitcast_fusion.wave3
  20.4 32.7 %all-to-all-done.got = f32[32,80,128]{2,1,0:T(8,128)S(1)} async-done(((f32[32,80,128]{2,1,0:T(8,128)}), f32[32,80,128]{2,1,0:T(8,128)S(1)}, u32[]{:S(2)}, u32[]{:S(2)}) %all-to-all-start) | async-done | bytes 1310752 | tf_op jit(solution)/shard_map/all_to_all | solution.py:421
  53.0 0.0 copy-done.6
  53.0 0.0 copy-done.7
  53.0 0.0 copy-done.11
  53.0 2.1 second_kernel.1
  55.1 8.1 %all-to-all-start.1 = ((f32[8,384,128]{2,1,0:T(8,128)}), f32[8,384,128]{2,1,0:T(8,128)S(1)}, u32[]{:S(2)}, u32[]{:S(2)}) async-start(f32[8,384,128]{2,1,0:T(8,128)} %second_kernel.1), calls=%async_computation.1 | async-start | bytes 3145728 | tf_op jit(solution)/shard_map/all_to_all | solution.py:423
  63.2 0.0 copy-done.4
  63.2 0.1 collective-permute-start
  63.3 0.7 collective-permute-start.1
  64.0 37.7 %collective-permute-done.x_low = f32[6,32,256]{2,1,0:T(8,128)S(1)} collective-permute-done((f32[6,32,256]{2,1,0:T(8,128)S(1)}, f32[6,32,256]{2,1,0:T(8,128)S(1)}, u32[]{:S(2)}, u32[]{:S(2)}) %collective-permute-start) | collective-permute-done | bytes 196640 | tf_op jit(solution)/shard_map/ppermute | solution.py:400
  101.7 0.0 collective-permute-done.1.x_high
  101.7 0.8 pad_maximum_fusion.1
  102.5 5.4 %collective-permute-start.3 = (f32[44,8,256]{2,1,0:T(8,128)}, f32[44,8,256]{2,1,0:T(8,128)S(1)}, u32[]{:S(2)}, u32[]{:S(2)}) collective-permute-start(f32[44,8,256]{2,1,0:T(8,128)} %pad_maximum_fusion.1), channel_id=1, source_target_pairs={{1,0},{2,1},{3,2},{4,3},{5,4},{6,5},{7,6},{0,7},{9,8},{10,9},{11,1... | collective-permute-start | bytes 1081352 | tf_op jit(solution)/shard_map/ppermute | solution.py:400
  107.9 0.8 pad_maximum_fusion
  108.7 0.0 collective-permute-start.2
  108.7 0.0 all-to-all-done.1.got
  108.7 0.0 copy-start.15
  108.7 0.9 copy-done.15
  109.6 0.8 copy-done.16
  110.4 3.0 %third_kernel.1 = (f32[3,16,16,128]{3,2,1,0:T(8,128)S(1)}, f32[3,16,16,128]{3,2,1,0:T(8,128)S(1)}) custom-call(f32[8,384,128]{2,1,0:T(8,128)S(1)} %all-to-all-done.1.got, bf16[256,128]{1,0:T(8,128)(2,1)S(1)} %copy-done.15, bf16[256,128]{1,0:T(8,128)(2,1)S(1)} %copy-done.16), custom_call_target="tpu_custom_call" | custom-call | tf_op jit(solution)/shard_map/third_kernel/pallas_call | solution.py:378
  113.5 3.0 %collective-permute-start.4 = (f32[3,4,16,128]{3,2,1,0:T(8,128)S(1)}, f32[3,4,16,128]{3,2,1,0:T(8,128)S(1)}, u32[]{:S(2)}, u32[]{:S(2)}) collective-permute-start(f32[3,4,16,128]{3,2,1,0:T(8,128)S(1)} %get-tuple-element.17), channel_id=1, source_target_pairs={{0,8},{8,16},{16,24},{24,32},{32,40},{40,48},{48,56},{56,64},{64,7... | collective-permute-start | bytes 294920 | tf_op jit(solution)/shard_map/ppermute | solution.py:400
  116.5 0.1 collective-permute-start.5
  116.6 19.1 %collective-permute-done.4.vx_low = f32[3,4,16,128]{3,2,1,0:T(8,128)S(1)} collective-permute-done((f32[3,4,16,128]{3,2,1,0:T(8,128)S(1)}, f32[3,4,16,128]{3,2,1,0:T(8,128)S(1)}, u32[]{:S(2)}, u32[]{:S(2)}) %collective-permute-start.4) | collective-permute-done | bytes 98336 | tf_op jit(solution)/shard_map/ppermute | solution.py:400
  135.7 5.7 %collective-permute-done.5.vx_high = f32[3,4,16,128]{3,2,1,0:T(8,128)S(1)} collective-permute-done((f32[3,4,16,128]{3,2,1,0:T(8,128)S(1)}, f32[3,4,16,128]{3,2,1,0:T(8,128)S(1)}, u32[]{:S(2)}, u32[]{:S(2)}) %collective-permute-start.5) | collective-permute-done | bytes 98336 | tf_op jit(solution)/shard_map/ppermute | solution.py:400
  141.5 2.4 collective-permute-start.7
  143.9 3.3 %collective-permute-start.6 = (f32[3,24,4,128]{3,2,1,0:T(4,128)S(1)}, f32[3,24,4,128]{3,2,1,0:T(4,128)S(1)}, u32[]{:S(2)}, u32[]{:S(2)}) collective-permute-start(f32[3,24,4,128]{3,2,1,0:T(4,128)S(1)} %pad_maximum_fusion.2), channel_id=1, source_target_pairs={{0,1},{1,2},{2,3},{3,4},{4,5},{5,6},{6,7},{7,0},{8,9},{9,10},{10,1... | collective-permute-start | bytes 442376 | tf_op jit(solution)/shard_map/ppermute | solution.py:400
  147.2 0.0 collective-permute-done.3.y_high
  147.2 0.0 collective-permute-done.2.y_low
  147.2 4.5 %collective-permute-done.7.vy_high = f32[3,24,4,128]{3,2,1,0:T(4,128)S(1)} collective-permute-done((f32[3,24,4,128]{3,2,1,0:T(4,128)S(1)}, f32[3,24,4,128]{3,2,1,0:T(4,128)S(1)}, u32[]{:S(2)}, u32[]{:S(2)}) %collective-permute-start.7) | collective-permute-done | bytes 147488 | tf_op jit(solution)/shard_map/ppermute | solution.py:400
  151.7 6.6 %collective-permute-done.6.vy_low = f32[3,24,4,128]{3,2,1,0:T(4,128)S(1)} collective-permute-done((f32[3,24,4,128]{3,2,1,0:T(4,128)S(1)}, f32[3,24,4,128]{3,2,1,0:T(4,128)S(1)}, u32[]{:S(2)}, u32[]{:S(2)}) %collective-permute-start.6) | collective-permute-done | bytes 147488 | tf_op jit(solution)/shard_map/ppermute | solution.py:400
  158.3 0.0 copy-done.10
  158.3 0.0 copy-done.12
  158.3 41.9 %scalar_kernel.1 = (f32[32,32,256]{2,1,0:T(8,128)}, f32[8,192,128]{2,1,0:T(8,128)S(1)}) custom-call(f32[32,32,256]{2,1,0:T(8,128)S(1)} %copy-done.4, f32[6,32,256]{2,1,0:T(8,128)S(1)} %collective-permute-done.x_low, f32[6,32,256]{2,1,0:T(8,128)S(1)} %collective-permute-done.1.x_high, f32[44,8,256]{2,1,0:T(8,128)} %collective-permute-done.2.y_low, ...), custom_call_target="tpu_custom_call" | custom-call | tf_op jit(solution)/shard_map/scalar_kernel/pallas_call | solution.py:378
  200.2 0.0 copy-start.8
  200.2 0.0 copy-start.9
  200.2 19.0 %all_to_all.20.got = f32[8,192,128]{2,1,0:T(8,128)S(1)} all-to-all(f32[8,192,128]{2,1,0:T(8,128)S(1)} %get-tuple-element.8), channel_id=1, replica_groups=mesh['px'=32,'py'=8] {'py'}, dimensions={0} | all-to-all | bytes 1572864 | tf_op jit(solution)/shard_map/all_to_all | solution.py:450
  219.2 0.0 copy-done.9
  219.2 0.5 second_back_kernel.1
  219.7 40.7 %all_to_all.21.got = f32[32,48,128]{2,1,0:T(8,128)S(1)} all-to-all(f32[32,48,128]{2,1,0:T(8,128)S(1)} %second_back_kernel.1), channel_id=1, replica_groups=mesh['px'=32,'py'=8] {'px'}, dimensions={0} | all-to-all | bytes 1572864 | tf_op jit(solution)/shard_map/all_to_all | solution.py:454
  260.4 3.3 %first_back_kernel.1 = f32[2,3,4,16,512]{4,3,2,1,0:T(8,128)} custom-call(f32[32,48,128]{2,1,0:T(8,128)S(1)} %all_to_all.21.got, bf16[512,1024]{1,0:T(8,128)(2,1)S(1)} %copy-done.1, bf16[512,1024]{1,0:T(8,128)(2,1)S(1)} %copy-done.3), custom_call_target="tpu_custom_call" | custom-call | tf_op jit(solution)/shard_map/first_back_kernel/pallas_call | solution.py:378
  (29 shorter events, 0.3 us)
Async XLA Ops:
  0.6 1.2 copy-start
  1.9 1.2 copy-start.2
  3.1 1.1 copy-start.5
  4.2 0.7 copy-start.17
  9.3 43.7 %copy-start.6 = (bf16[2,256,256]{2,1,0:T(8,128)(2,1)S(1)}, bf16[2,256,256]{2,1,0:T(8,128)(2,1)}, u32[]{:S(2)}) copy-start(bf16[2,256,256]{2,1,0:T(8,128)(2,1)} %constant.43.clone.th) | copy-start | bytes 786436
  9.3 43.7 %copy-start.7 = (bf16[2,256,256]{2,1,0:T(8,128)(2,1)S(1)}, bf16[2,256,256]{2,1,0:T(8,128)(2,1)}, u32[]{:S(2)}) copy-start(bf16[2,256,256]{2,1,0:T(8,128)(2,1)} %constant.44.clone.tl) | copy-start | bytes 786436
  9.3 43.7 %copy-start.11 = (f32[256,1]{1,0:T(8,128)S(1)}, f32[256,1]{1,0:T(8,128)}, u32[]{:S(2)}) copy-start(f32[256,1]{1,0:T(8,128)} %constant.48.clone.wave2) | copy-start | bytes 3076
  9.3 43.7 %all-to-all-start = ((f32[32,80,128]{2,1,0:T(8,128)}), f32[32,80,128]{2,1,0:T(8,128)S(1)}, u32[]{:S(2)}, u32[]{:S(2)}) async-start(f32[32,80,128]{2,1,0:T(8,128)} %first_kernel.1), calls=%async_computation | async-start | bytes 2621440 | tf_op jit(solution)/shard_map/all_to_all | solution.py:421
  55.1 8.1 %copy-start.4 = (f32[32,32,256]{2,1,0:T(8,128)S(1)}, f32[32,32,256]{2,1,0:T(8,128)}, u32[]{:S(2)}) copy-start(f32[32,32,256]{2,1,0:T(8,128)} %scalar.1) | copy-start | bytes 3145732
  55.1 53.6 %all-to-all-start.1 = ((f32[8,384,128]{2,1,0:T(8,128)}), f32[8,384,128]{2,1,0:T(8,128)S(1)}, u32[]{:S(2)}, u32[]{:S(2)}) async-start(f32[8,384,128]{2,1,0:T(8,128)} %second_kernel.1), calls=%async_computation.1 | async-start | bytes 3145728 | tf_op jit(solution)/shard_map/all_to_all | solution.py:423
  63.2 38.5 %collective-permute-start = (f32[6,32,256]{2,1,0:T(8,128)S(1)}, f32[6,32,256]{2,1,0:T(8,128)S(1)}, u32[]{:S(2)}, u32[]{:S(2)}) collective-permute-start(f32[6,32,256]{2,1,0:T(8,128)S(1)} %get-tuple-element.13), channel_id=1, source_target_pairs={{0,8},{8,16},{16,24},{24,32},{32,40},{40,48},{48,56},{56,64},{64,7... | collective-permute-start | bytes 589832 | tf_op jit(solution)/shard_map/ppermute | solution.py:400
  63.3 38.4 %collective-permute-start.1 = (f32[6,32,256]{2,1,0:T(8,128)S(1)}, f32[6,32,256]{2,1,0:T(8,128)S(1)}, u32[]{:S(2)}, u32[]{:S(2)}) collective-permute-start(f32[6,32,256]{2,1,0:T(8,128)S(1)} %get-tuple-element.12), channel_id=1, source_target_pairs={{8,0},{16,8},{24,16},{32,24},{40,32},{48,40},{56,48},{64,56},{72,6... | collective-permute-start | bytes 589832 | tf_op jit(solution)/shard_map/ppermute | solution.py:400
  102.5 44.7 %collective-permute-start.3 = (f32[44,8,256]{2,1,0:T(8,128)}, f32[44,8,256]{2,1,0:T(8,128)S(1)}, u32[]{:S(2)}, u32[]{:S(2)}) collective-permute-start(f32[44,8,256]{2,1,0:T(8,128)} %pad_maximum_fusion.1), channel_id=1, source_target_pairs={{1,0},{2,1},{3,2},{4,3},{5,4},{6,5},{7,6},{0,7},{9,8},{10,9},{11,1... | collective-permute-start | bytes 1081352 | tf_op jit(solution)/shard_map/ppermute | solution.py:400
  108.7 49.6 %copy-start.10 = (bf16[2,128,256]{2,1,0:T(8,128)(2,1)S(1)}, bf16[2,128,256]{2,1,0:T(8,128)(2,1)}, u32[]{:S(2)}) copy-start(bf16[2,128,256]{2,1,0:T(8,128)(2,1)} %constant.49.clone.rise) | copy-start | bytes 393220
  108.7 38.5 %collective-permute-start.2 = (f32[44,8,256]{2,1,0:T(8,128)}, f32[44,8,256]{2,1,0:T(8,128)}, u32[]{:S(2)}, u32[]{:S(2)}) collective-permute-start(f32[44,8,256]{2,1,0:T(8,128)} %pad_maximum_fusion), channel_id=1, source_target_pairs={{0,1},{1,2},{2,3},{3,4},{4,5},{5,6},{6,7},{7,0},{8,9},{9,10},{10,1... | collective-permute-start | bytes 1081352 | tf_op jit(solution)/shard_map/ppermute | solution.py:400
  108.7 0.9 copy-start.15
  109.6 0.8 copy-start.16
  110.4 47.9 %copy-start.12 = (bf16[256,128]{1,0:T(8,128)(2,1)S(1)}, bf16[256,128]{1,0:T(8,128)(2,1)}, u32[]{:S(2)}) copy-start(bf16[256,128]{1,0:T(8,128)(2,1)} %constant.50.clone.pair) | copy-start | bytes 196612
  110.4 47.9 %copy-start.13 = (bf16[128,256]{1,0:T(8,128)(2,1)S(1)}, bf16[128,256]{1,0:T(8,128)(2,1)}, u32[]{:S(2)}) copy-start(bf16[128,256]{1,0:T(8,128)(2,1)} %constant.51.clone.th) | copy-start | bytes 196612
  110.4 47.9 %copy-start.14 = (bf16[128,256]{1,0:T(8,128)(2,1)S(1)}, bf16[128,256]{1,0:T(8,128)(2,1)}, u32[]{:S(2)}) copy-start(bf16[128,256]{1,0:T(8,128)(2,1)} %constant.52.clone.tl) | copy-start | bytes 196612
  113.5 22.3 %collective-permute-start.4 = (f32[3,4,16,128]{3,2,1,0:T(8,128)S(1)}, f32[3,4,16,128]{3,2,1,0:T(8,128)S(1)}, u32[]{:S(2)}, u32[]{:S(2)}) collective-permute-start(f32[3,4,16,128]{3,2,1,0:T(8,128)S(1)} %get-tuple-element.17), channel_id=1, source_target_pairs={{0,8},{8,16},{16,24},{24,32},{32,40},{40,48},{48,56},{56,64},{64,7... | collective-permute-start | bytes 294920 | tf_op jit(solution)/shard_map/ppermute | solution.py:400
  116.5 24.9 %collective-permute-start.5 = (f32[3,4,16,128]{3,2,1,0:T(8,128)S(1)}, f32[3,4,16,128]{3,2,1,0:T(8,128)S(1)}, u32[]{:S(2)}, u32[]{:S(2)}) collective-permute-start(f32[3,4,16,128]{3,2,1,0:T(8,128)S(1)} %get-tuple-element.16), channel_id=1, source_target_pairs={{8,0},{16,8},{24,16},{32,24},{40,32},{48,40},{56,48},{64,56},{72,6... | collective-permute-start | bytes 294920 | tf_op jit(solution)/shard_map/ppermute | solution.py:400
  141.5 10.2 %collective-permute-start.7 = (f32[3,24,4,128]{3,2,1,0:T(4,128)S(1)}, f32[3,24,4,128]{3,2,1,0:T(4,128)S(1)}, u32[]{:S(2)}, u32[]{:S(2)}) collective-permute-start(f32[3,24,4,128]{3,2,1,0:T(4,128)S(1)} %pad_maximum_fusion.3), channel_id=1, source_target_pairs={{1,0},{2,1},{3,2},{4,3},{5,4},{6,5},{7,6},{0,7},{9,8},{10,9},{11,1... | collective-permute-start | bytes 442376 | tf_op jit(solution)/shard_map/ppermute | solution.py:400
  143.9 14.4 %collective-permute-start.6 = (f32[3,24,4,128]{3,2,1,0:T(4,128)S(1)}, f32[3,24,4,128]{3,2,1,0:T(4,128)S(1)}, u32[]{:S(2)}, u32[]{:S(2)}) collective-permute-start(f32[3,24,4,128]{3,2,1,0:T(4,128)S(1)} %pad_maximum_fusion.2), channel_id=1, source_target_pairs={{0,1},{1,2},{2,3},{3,4},{4,5},{5,6},{6,7},{7,0},{8,9},{9,10},{10,1... | collective-permute-start | bytes 442376 | tf_op jit(solution)/shard_map/ppermute | solution.py:400
  200.2 19.0 %copy-start.8 = (bf16[256,256]{1,0:T(8,128)(2,1)S(1)}, bf16[256,256]{1,0:T(8,128)(2,1)}, u32[]{:S(2)}) copy-start(bf16[256,256]{1,0:T(8,128)(2,1)} %constant.53.clone.th) | copy-start | bytes 393220
  200.2 19.0 %copy-start.9 = (bf16[256,256]{1,0:T(8,128)(2,1)S(1)}, bf16[256,256]{1,0:T(8,128)(2,1)}, u32[]{:S(2)}) copy-start(bf16[256,256]{1,0:T(8,128)(2,1)} %constant.54.clone.tl) | copy-start | bytes 393220
  219.2 41.2 %copy-start.1 = (bf16[512,1024]{1,0:T(8,128)(2,1)S(1)}, bf16[512,1024]{1,0:T(8,128)(2,1)}, u32[]{:S(2)}) copy-start(bf16[512,1024]{1,0:T(8,128)(2,1)} %constant.41.clone.th) | copy-start | bytes 3145732
  219.2 41.2 %copy-start.3 = (bf16[512,1024]{1,0:T(8,128)(2,1)S(1)}, bf16[512,1024]{1,0:T(8,128)(2,1)}, u32[]{:S(2)}) copy-start(bf16[512,1024]{1,0:T(8,128)(2,1)} %constant.42.clone.tl) | copy-start | bytes 3145732
where the time goes:
time: 264 us
  waiting for transfers between devices  106 us (40%)
  blocking collectives  59.7 us (23%)
  Pallas kernels  55.1 us (21%)
  starting transfers between devices  33.4 us (13%)
  local copies, waits for them, and re-layouts  6.86 us (3%)
    ppermute x8, waiting for transfers between devices, edges(): return (lax.ppermute(last, axis, up), lax.ppermute(first, axis, down))  73.5 us
    pallas_call x6, Pallas kernels, call(): pl.pallas_call(kernel, out_shape=out_shape, scratch_shapes=list(scratch),...  55.1 us
    all_to_all x1, blocking collectives, body(): got = lax.all_to_all(sent, 'px', split_axis=0, concat_axis=0, tiled=True)  40.7 us
    all_to_all x1, waiting for transfers between devices, body(): got = lax.all_to_all(sent, 'px', split_axis=0, concat_axis=0, tiled=True)  32.7 us
    all_to_all x1, blocking collectives, body(): got = lax.all_to_all(sent, 'py', split_axis=0, concat_axis=0, tiled=True)  19 us
    ppermute x8, starting transfers between devices, edges(): return (lax.ppermute(last, axis, up), lax.ppermute(first, axis, down))  15 us
    all_to_all x1, starting transfers between devices, body(): got = lax.all_to_all(sent, 'px', split_axis=0, concat_axis=0, tiled=True)  10.3 us
    all_to_all x1, starting transfers between devices, body(): got = lax.all_to_all(sent, 'py', split_axis=0, concat_axis=0, tiled=True)  8.08 us
  transfers between devices with their start and end apart: 10, of which 6 were waited for; matrix products, arithmetic and copies ran while one was open for 1% of the time, Pallas kernels for 1%

commit v1 on v0

--- a/solution.py
+++ b/solution.py
@@ -111,7 +111,7 @@
     return v
 
 
-def first_kernel(spec, wave, th, tl, out, y):
+def first_kernel(spec, wave, th, tl, x_low, x_high, out, y):
     rows = []
     for f in (0, 1, 2, 1, 2):
         plain, turned = [], []
@@ -134,7 +134,7 @@
         out[:, 16 * f : 16 * f + 16, :] = y[N1 * f : N1 * f + N1, :].reshape(GX, 16, 128)
 
 
-def second_kernel(got, wave2, wave3, th, tl, out):
+def second_kernel(got, wave2, wave3, th, tl, brick, out):
     c = []
     for f in range(5):
         halves_ = [got[:, 16 * f + 8 * h : 16 * f + 8 * h + 8, :].reshape(256, 128) for h in range(2)]
@@ -187,6 +187,10 @@
                     out[q, at : at + 16, :] = w8[q]
 
 
+def parted(table):
+    return np.concatenate([table[:, 0::2], table[:, 1::2]], axis=1).astype(np.float32).astype(BF)
+
+
 def rise_tables():
     plain = np.zeros((N3, 2 * N3))
     for i in range(N3):
@@ -196,12 +200,23 @@
         for far in ((i - 1) % N3, (i + 2) % N3):
             plain[far, 2 * i + 1] -= 1.0 / 16.0
     face = 0.5 * (plain + np.roll(plain, -1, axis=1))
-    return np.stack([plain, face]).astype(np.float32).astype(BF)
-
-
-def pair_table():
-    cols = np.arange(2 * N3)[:, None] // 2
-    return np.where(cols == np.arange(N3)[None], 0.125, 0.0).astype(np.float32).astype(BF)
+    return np.stack([parted(plain), parted(face)])
+
+
+def parity_tables():
+    part = parted(np.eye(2 * N3))
+    return part, np.ascontiguousarray(part.T)
+
+
+def three(x):
+    high, rest = x.astype(BF), None
+    rest = x - high.astype(F32)
+    mid = rest.astype(BF)
+    return (rest - mid.astype(F32)).astype(BF), mid, high
+
+
+def permuted(x, table):
+    return dots([(part, table) for part in three(x)], ((1,), (0,)))
 
 
 def middle(a, b, c, d):
@@ -216,12 +231,22 @@
     return face * jnp.where(face > 0.0, left, right) - DIFFUSION_RATIO * jump
 
 
-def rolled_divergence(theta, face, axis):
-    count = theta.shape[axis]
-    jump = pltpu.roll(theta, count - 1, axis) - theta
-    half = 0.5 * limited(pltpu.roll(jump, 1, axis), jump)
-    flux = upwind(face, theta + half, pltpu.roll(theta - half, count - 1, axis), jump)
-    return flux - pltpu.roll(flux, 1, axis)
+def row_divergence(theta, face):
+    count = theta.shape[0]
+    jump = pltpu.roll(theta, count - 1, 0) - theta
+    half = 0.5 * limited(pltpu.roll(jump, 1, 0), jump)
+    flux = upwind(face, theta + half, pltpu.roll(theta - half, count - 1, 0), jump)
+    return flux - pltpu.roll(flux, 1, 0)
+
+
+def lane_divergence(even, odd, face_even, face_odd):
+    jump_even = odd - even
+    jump_odd = pltpu.roll(even, N3 - 1, 1) - odd
+    half_even = 0.5 * limited(even - pltpu.roll(odd, 1, 1), jump_even)
+    half_odd = 0.5 * limited(jump_even, jump_odd)
+    flux_even = upwind(face_even, even + half_even, odd - half_odd, jump_even)
+    flux_odd = upwind(face_odd, odd + half_odd, pltpu.roll(even - half_even, N3 - 1, 1), jump_odd)
+    return flux_even - pltpu.roll(flux_odd, 1, 1), flux_odd - flux_even
 
 
 EDGE = 6
@@ -231,12 +256,31 @@
 PROWS = C2 + 16
 
 
+def brick_kernel(scalar, x_low, x_high, y_low, y_high, table, brick, raw):
+    raw[0:EDGE, 8:40, :] = x_low[...]
+    raw[EDGE : EDGE + 2 * C1, 8:40, :] = scalar[...]
+    raw[EDGE + 2 * C1 :, 8:40, :] = x_high[...]
+    at = 0
+    for layer in range(3):
+        first, count = 2 + 2 * layer, 40 - 4 * layer
+        raw[first : first + count, 6 - 2 * layer : 8 - 2 * layer, :] = y_low[at : at + count]
+        raw[first : first + count, 40 + 2 * layer : 42 + 2 * layer, :] = y_high[at : at + count]
+        at += count
+
+    def part(n, carry):
+        z = permuted(raw[pl.ds(4 * n, 4)].reshape(4 * ROWS, 256), table[...])
+        for h in range(2):
+            brick[pl.ds(4 * n, 4), h] = z[:, h * 128 : h * 128 + 128].reshape(4, ROWS, 128)
+        return carry
+
+    lax.fori_loop(0, SLABS // 4, part, 0)
+
+
 def scalar_kernel(
-    scalar, x_low, x_high, y_low, y_high,
-    velocity, vx_low, vx_high, vy_low, vy_high, vorticity,
-    rise, pair, th, tl,
+    brick, velocity, vx_low, vx_high, vy_low, vy_high, vorticity,
+    rise, join, th, tl,
     advanced, out,
-    ta, tb, vw, su, sf, f1, f2, f3, bs,
+    ta, tb, last, vw, su, sf, f1, f2, f3, bs,
 ):
     for c in range(3):
         vw[c * PTS : c * PTS + 4, 8:24, :] = vx_low[c]
@@ -280,61 +324,60 @@
     def first(k, carry):
         for c, face in enumerate((f1, f2, f3)):
             for h in range(2):
-                cols = pl.ds(h * 128, 128)
                 a, b, cc, d = (
                     sf[pl.ds(pl.multiple_of((h * 3 * PTS + c * PTS + k + o) * ROWS, 8), ROWS), :]
                     for o in range(4)
                 )
                 odd = middle(a, b, cc, d)
                 if c == 0:
-                    face[2 * k + 1, :, cols] = 0.5 * (odd + cc)
-                    face[2 * k, :, cols] = 0.5 * (b + odd)
+                    face[2 * k + 1, h] = 0.5 * (odd + cc)
+                    face[2 * k, h] = 0.5 * (b + odd)
                 else:
-                    face[2 * k + 1, :, cols] = odd
-                    face[2 * k + 2, :, cols] = cc
+                    face[2 * k + 1, h] = odd
+                    face[2 * k + 2, h] = cc
         return carry
 
     lax.fori_loop(0, 21, first, 0)
 
-    ta[0:EDGE, 8:40, :] = x_low[...]
-    ta[EDGE : EDGE + 2 * C1, 8:40, :] = scalar[...]
-    ta[EDGE + 2 * C1 :, 8:40, :] = x_high[...]
-    ta[:, 0:8, :] = y_low[...]
-    ta[:, 40:48, :] = y_high[...]
-
-    for turn, (source, target) in enumerate(((ta, tb), (tb, ta), (ta, tb))):
+    for turn, (source, target) in enumerate(((brick, ta), (ta, tb), (tb, last))):
         low = 2 + 2 * turn
-        t0, t1, t2, t3 = (source[low - 2 + o] for o in range(4))
-        j0, j1, j2 = t1 - t0, t2 - t1, t3 - t2
-        h1, h2 = 0.5 * limited(j0, j1), 0.5 * limited(j1, j2)
-        flux = upwind(f1[low - 1], t1 + h1, t2 - h2, j1)
+        begin = []
+        for h in range(2):
+            t0, t1, t2, t3 = (source[low - 2 + o, h] for o in range(4))
+            j0, j1, j2 = t1 - t0, t2 - t1, t3 - t2
+            h1, h2 = 0.5 * limited(j0, j1), 0.5 * limited(j1, j2)
+            begin.append((t2 + h2, j2, upwind(f1[low - 1, h], t1 + h1, t2 - h2, j1)))
 
         def step(i, carry, source=source, target=target, turn=turn):
-            left, jump, before = carry
-            here, ahead = source[i], source[i + 1]
-            next_jump = source[i + 2] - ahead
-            half = 0.5 * limited(jump, next_jump)
-            flux = upwind(f1[i], left, ahead - half, jump)
-            change = flux - before
-            change += rolled_divergence(here, f2[i], 0)
-            change += rolled_divergence(here, f3[i], 1)
-            fresh = here - STEP_RATIO * change
-            if turn < NSUB - 1:
-                target[i] = fresh
-            else:
-                advanced[i - EDGE] = fresh[8:40]
-            return ahead + half, next_jump, flux
-
-        lax.fori_loop(low, SLABS - low, step, (t2 + h2, j2, flux))
-
-    def pairs(n, carry):
-        lines = (advanced[pl.ds(4 * n, 4)]).reshape(2, 2, 32, 256)
-        both = (lines[:, 0] + lines[:, 1]).reshape(64, 256)
-        high, low = split(both)
-        bs[pl.ds(pl.multiple_of(64 * n, 8), 64), :] = dots([(low, pair[...]), (high, pair[...])], ((1,), (0,)))
+            here = [source[i, h] for h in range(2)]
+            change = list(lane_divergence(*here, f3[i, 0], f3[i, 1]))
+            done = []
+            for h in range(2):
+                left, jump, before = carry[h]
+                ahead = source[i + 1, h]
+                next_jump = source[i + 2, h] - ahead
+                half = 0.5 * limited(jump, next_jump)
+                flux = upwind(f1[i, h], left, ahead - half, jump)
+                total = change[h] + (flux - before) + row_divergence(here[h], f2[i, h])
+                fresh = here[h] - STEP_RATIO * total
+                if turn < NSUB - 1:
+                    target[i, h] = fresh
+                else:
+                    target[i - EDGE, :, h * 128 : h * 128 + 128] = fresh[8:40]
+                done.append((ahead + half, next_jump, flux))
+            return tuple(done)
+
+        lax.fori_loop(low, SLABS - low, step, tuple(begin))
+
+    def finish(n, carry):
+        lines = last[pl.ds(4 * n, 4)]
+        advanced[pl.ds(4 * n, 4)] = permuted(lines.reshape(128, 256), join[...]).reshape(4, 32, 256)
+        both = lines[:, :, :128] + lines[:, :, 128:]
+        bs[pl.ds(pl.multiple_of(64 * n, 8), 32), :] = 0.125 * (both[0] + both[1])
+        bs[pl.ds(pl.multiple_of(64 * n + 32, 8), 32), :] = 0.125 * (both[2] + both[3])
         return carry
 
-    lax.fori_loop(0, C1 // 2, pairs, 0)
+    lax.fori_loop(0, C1 // 2, finish, 0)
     buoyancy = bs[pl.ds(0, C1 * C2, stride=2), :] + bs[pl.ds(1, C1 * C2, stride=2), :]
     force_lines(velocity, vorticity, buoyancy, th, tl, out)
 
@@ -374,9 +417,12 @@
             out[1, f, r] = ci - sr
 
 
-def call(kernel, out_shape, *args, scratch=()):
+def call(kernel, out_shape, *args, scratch=(), late=0):
+    specs = [pl.BlockSpec(memory_space=pltpu.VMEM)] * (len(args) - late)
+    specs += [pl.BlockSpec(memory_space=pl.ANY)] * late
     return pl.pallas_call(
         kernel,
+        in_specs=specs,
         out_shape=out_shape,
         scratch_shapes=list(scratch),
         interpret=INTERPRET,
@@ -409,17 +455,23 @@
     second = [jnp.asarray(t) for t in second_forward()]
     third = [jnp.asarray(t) for t in third_forward()]
     x_low, x_high = edges("px", scalar[:EDGE], scalar[-EDGE:])
+    around = jnp.concatenate([x_low[2:], scalar, x_high[:4]], axis=0)
     strips = [
-        jnp.concatenate([part[:, cut] for part in (x_low, scalar, x_high)], axis=0)
-        for cut in (slice(0, 8), slice(2 * C2 - 8, 2 * C2))
+        jnp.concatenate([around[2 * n : 40 - 2 * n, at : at + 2] for n, at in enumerate(starts)], axis=0)
+        for starts in ((0, 2, 4), (2 * C2 - 2, 2 * C2 - 4, 2 * C2 - 6))
     ]
     y_low, y_high = edges("py", *strips)
+    part, join = (jnp.asarray(t) for t in parity_tables())
+    brick = call(
+        brick_kernel, shape(SLABS, 2, ROWS, 128), scalar, x_low, x_high, y_low, y_high, part,
+        scratch=(pltpu.VMEM((SLABS, ROWS, 256), F32),),
+    )
     sent = call(
-        first_kernel, shape(GX, 80, 128), spectrum, jnp.asarray(wave_first), *first,
-        scratch=(pltpu.VMEM((5 * N1, 128), F32),),
+        first_kernel, shape(GX, 80, 128), spectrum, jnp.asarray(wave_first), *first, x_low, x_high,
+        scratch=(pltpu.VMEM((5 * N1, 128), F32),), late=2,
     )
     got = lax.all_to_all(sent, "px", split_axis=0, concat_axis=0, tiled=True)
-    sent = call(second_kernel, shape(GY, 384, 128), got, jnp.asarray(wave_second), wave_third, *second)
+    sent = call(second_kernel, shape(GY, 384, 128), got, jnp.asarray(wave_second), wave_third, *second, brick, late=1)
     got = lax.all_to_all(sent, "py", split_axis=0, concat_axis=0, tiled=True)
     velocity, vorticity = call(
         third_kernel, (shape(3, C1, C2, N3), shape(3, C1, C2, N3)), got, *third
@@ -432,18 +484,18 @@
     vy_low, vy_high = edges("py", *strips)
     theta, sent = call(
         scalar_kernel, (shape(2 * C1, 2 * C2, 2 * N3), shape(GY, 192, 128)),
-        scalar, x_low, x_high, y_low, y_high,
-        velocity, vx_low, vx_high, vy_low, vy_high, vorticity,
-        jnp.asarray(rise_tables()), jnp.asarray(pair_table()), *[jnp.asarray(t) for t in third_back()],
+        brick, velocity, vx_low, vx_high, vy_low, vy_high, vorticity,
+        jnp.asarray(rise_tables()), join, *[jnp.asarray(t) for t in third_back()],
         scratch=(
-            pltpu.VMEM((SLABS, ROWS, 256), F32),
-            pltpu.VMEM((SLABS, ROWS, 256), F32),
+            pltpu.VMEM((SLABS, 2, ROWS, 128), F32),
+            pltpu.VMEM((SLABS, 2, ROWS, 128), F32),
+            pltpu.VMEM((2 * C1, 2 * C2, 256), F32),
             pltpu.VMEM((3 * PTS, PROWS, N3), F32),
             pltpu.VMEM((2 * 3 * PTS * PROWS, 128), F32),
             pltpu.VMEM((2 * 3 * PTS * ROWS, 128), F32),
-            pltpu.VMEM((SLABS, ROWS, 256), F32),
-            pltpu.VMEM((SLABS, ROWS, 256), F32),
-            pltpu.VMEM((SLABS, ROWS, 256), F32),
+            pltpu.VMEM((SLABS, 2, ROWS, 128), F32),
+            pltpu.VMEM((SLABS, 2, ROWS, 128), F32),
+            pltpu.VMEM((SLABS, 2, ROWS, 128), F32),
             pltpu.VMEM((2 * C1 * C2, 128), F32),
         ),
     )

time: 264 us -> 257 us (0.973)
  waiting for transfers between devices: 106 us -> 54.2 us
  blocking collectives: 59.7 us -> 108 us
  Pallas kernels: 55.1 us -> 48.6 us
  local copies, waits for them, and re-layouts: 6.86 us -> 13.2 us
    all_to_all x1 -> x2, blocking collectives: 19 us -> 65.8 us  [body(): got = lax.all_to_all(sent, 'py', split_axis=0, concat_axis=0, tiled=True)]
    all_to_all x1, waiting for transfers between devices: 32.7 us -> 0.01 us  [body(): got = lax.all_to_all(sent, 'px', split_axis=0, concat_axis=0, tiled=True)]
    ppermute x8, waiting for transfers between devices: 73.5 us -> 54.2 us  [edges(): return (lax.ppermute(last, axis, up), lax.ppermute(first, axis, down))]
    all_to_all x1 -> x0, starting transfers between devices: 8.08 us -> none  [body(): got = lax.all_to_all(sent, 'py', split_axis=0, concat_axis=0, tiled=True)]
    pallas_call x6 -> x7, Pallas kernels: 55.1 us -> 48.6 us  [call(): pl.pallas_call(kernel, in_specs=specs, out_shape=out_shape, scratch_shape...]
    unnamed x36 -> x50, local copies, waits for them, and re-layouts: 6.02 us -> 11.3 us
    ppermute x8, starting transfers between devices: 15 us -> 19.5 us  [edges(): return (lax.ppermute(last, axis, up), lax.ppermute(first, axis, down))]
  transfers between devices with their start and end apart: 10 -> 9, of which waited for: 6 -> 7; matrix products, arithmetic and copies ran while one was open for 1% -> 0% of each run, Pallas kernels for 1% -> 1%
where the time goes in v1:
time: 257 us
  blocking collectives  108 us (42%)
  waiting for transfers between devices  54.2 us (21%)
  Pallas kernels  48.6 us (19%)
  starting transfers between devices  31.9 us (12%)
  local copies, waits for them, and re-layouts  13.2 us (5%)
    all_to_all x2, blocking collectives, body(): got = lax.all_to_all(sent, 'py', split_axis=0, concat_axis=0, tiled=True)  65.8 us
    ppermute x8, waiting for transfers between devices, edges(): return (lax.ppermute(last, axis, up), lax.ppermute(first, axis, down))  54.2 us
    pallas_call x7, Pallas kernels, call(): pl.pallas_call(kernel, in_specs=specs, out_shape=out_shape, scratch_shape...  48.6 us
    all_to_all x1, blocking collectives, body(): got = lax.all_to_all(sent, 'px', split_axis=0, concat_axis=0, tiled=True)  41.7 us
    ppermute x8, starting transfers between devices, edges(): return (lax.ppermute(last, axis, up), lax.ppermute(first, axis, down))  19.5 us
    all_to_all x1, starting transfers between devices, body(): got = lax.all_to_all(sent, 'px', split_axis=0, concat_axis=0, tiled=True)  12.4 us
    unnamed x50, local copies, waits for them, and re-layouts  11.3 us
  transfers between devices with their start and end apart: 9, of which 7 were waited for; matrix products, arithmetic and copies ran while one was open for 0% of the time, Pallas kernels for 1%

profile of v1, /device:TPU:1, one launch (start us, length us, event | category | flops | bytes accessed | tf_op | source)
XLA Modules:
  0.0 256.5 jit_solution(2672105972133047179)
XLA Ops:
  0.6 1.1 fusion.5
  1.7 3.3 %collective-permute-start.1 = (f32[6,32,256]{2,1,0:T(8,128)S(1)}, f32[6,32,256]{2,1,0:T(8,128)S(1)}, u32[]{:S(2)}, u32[]{:S(2)}) collective-permute-start(f32[6,32,256]{2,1,0:T(8,128)S(1)} %get-tuple-element.14), channel_id=1, source_target_pairs={{8,0},{16,8},{24,16},{32,24},{40,32},{48,40},{56,48},{64,56},{72,6... | collective-permute-start | bytes 589832 | tf_op jit(solution)/shard_map/ppermute | solution.py:446
  5.0 0.0 collective-permute-start
  5.0 3.2 %collective-permute-done.1.x_high = f32[6,32,256]{2,1,0:T(8,128)S(1)} collective-permute-done((f32[6,32,256]{2,1,0:T(8,128)S(1)}, f32[6,32,256]{2,1,0:T(8,128)S(1)}, u32[]{:S(2)}, u32[]{:S(2)}) %collective-permute-start.1) | collective-permute-done | bytes 196640 | tf_op jit(solution)/shard_map/ppermute | solution.py:446
  8.1 2.6 %collective-permute-done.x_low = f32[6,32,256]{2,1,0:T(8,128)S(1)} collective-permute-done((f32[6,32,256]{2,1,0:T(8,128)S(1)}, f32[6,32,256]{2,1,0:T(8,128)S(1)}, u32[]{:S(2)}, u32[]{:S(2)}) %collective-permute-start) | collective-permute-done | bytes 196640 | tf_op jit(solution)/shard_map/ppermute | solution.py:446
  10.7 1.2 copy-done.1
  11.9 1.2 copy-done.3
  13.2 1.1 copy-done.7
  14.3 0.7 copy-done.24
  15.0 4.4 %first_kernel.1 = f32[32,80,128]{2,1,0:T(8,128)} custom-call(f32[2,3,4,16,512]{4,3,2,1,0:T(8,128)S(1)} %copy-done.7, f32[1,1024]{1,0:T(1,128)S(1)} %copy-done.24, bf16[512,1024]{1,0:T(8,128)(2,1)S(1)} %copy-done.3, bf16[512,1024]{1,0:T(8,128)(2,1)S(1)} %copy-done.1, f32[6,32,256]{2,1,0:T(8,128)S(1)} %collective-permute-done.x_low, ...), custom_call_target="tpu_custom_call" | custom-call | tf_op jit(solution)/shard_map/first_kernel/pallas_call | solution.py:423
  19.4 12.4 %all-to-all-start = ((f32[32,80,128]{2,1,0:T(8,128)}), f32[32,80,128]{2,1,0:T(8,128)}, u32[]{:S(2)}, u32[]{:S(2)}) async-start(f32[32,80,128]{2,1,0:T(8,128)} %first_kernel.1), calls=%async_computation | async-start | bytes 2621440 | tf_op jit(solution)/shard_map/all_to_all | solution.py:473
  31.9 0.1 fusion.4
  32.0 0.2 fusion.1
  32.2 6.5 %collective-permute-start.3 = (f32[108,2,256]{2,1,0:T(2,128)S(1)}, f32[108,2,256]{2,1,0:T(2,128)S(1)}, u32[]{:S(2)}, u32[]{:S(2)}) collective-permute-start(f32[108,2,256]{2,1,0:T(2,128)S(1)} %get-tuple-element.10), channel_id=1, source_target_pairs={{1,0},{2,1},{3,2},{4,3},{5,4},{6,5},{7,6},{0,7},{9,8},{10,9},{11,1... | collective-permute-start | bytes 663560 | tf_op jit(solution)/shard_map/ppermute | solution.py:446
  38.7 0.0 collective-permute-start.2
  38.7 0.7 dynamic-slice_bitcast_fusion.wave3
  39.3 32.9 %collective-permute-done.3.y_high = f32[108,2,256]{2,1,0:T(2,128)S(1)} collective-permute-done((f32[108,2,256]{2,1,0:T(2,128)S(1)}, f32[108,2,256]{2,1,0:T(2,128)S(1)}, u32[]{:S(2)}, u32[]{:S(2)}) %collective-permute-start.3) | collective-permute-done | bytes 221216 | tf_op jit(solution)/shard_map/ppermute | solution.py:446
  72.2 0.7 copy-done.10
  72.9 6.2 %collective-permute-done.2.y_low = f32[108,2,256]{2,1,0:T(2,128)S(1)} collective-permute-done((f32[108,2,256]{2,1,0:T(2,128)S(1)}, f32[108,2,256]{2,1,0:T(2,128)S(1)}, u32[]{:S(2)}, u32[]{:S(2)}) %collective-permute-start.2) | collective-permute-done | bytes 221216 | tf_op jit(solution)/shard_map/ppermute | solution.py:446
  79.2 0.7 copy-done.12
  79.9 0.9 copy-done.6
  80.8 0.9 copy-done.11
  81.7 0.9 copy-done.13
  82.7 0.9 copy-done.17
  83.6 3.0 %brick_kernel.1.brick = f32[44,2,48,128]{3,2,1,0:T(8,128)S(1)} custom-call(f32[32,32,256]{2,1,0:T(8,128)S(1)} %copy-done, f32[6,32,256]{2,1,0:T(8,128)S(1)} %copy-done.6, f32[6,32,256]{2,1,0:T(8,128)S(1)} %collective-permute-done.1.x_high, f32[108,2,256]{2,1,0:T(2,128)S(1)} %copy-done.13, f32[108,2,256]{2,1,0:T(2,128)S(1)} %copy-done.11, ...), custom_call_target="tpu_custom_call" | custom-call | tf_op jit(solution)/shard_map/brick_kernel/pallas_call | solution.py:423
  86.6 0.0 all-to-all-done.got
  86.6 0.0 copy-start.8
  86.6 0.9 copy-done.8
  87.5 0.9 copy-done.9
  88.5 2.2 second_kernel.1
  90.7 0.0 copy-start.20
  90.7 0.0 copy-start.21
  90.7 44.0 %all_to_all.20.got = f32[8,384,128]{2,1,0:T(8,128)S(1)} all-to-all(f32[8,384,128]{2,1,0:T(8,128)S(1)} %second_kernel.1), channel_id=1, replica_groups=mesh['px'=32,'py'=8] {'py'}, dimensions={0} | all-to-all | bytes 3145728 | tf_op jit(solution)/shard_map/all_to_all | solution.py:475
  134.8 0.0 copy-start.22
  134.8 0.0 copy-start.23
  134.8 3.0 %third_kernel.1 = (f32[3,16,16,128]{3,2,1,0:T(8,128)S(1)}, f32[3,16,16,128]{3,2,1,0:T(8,128)S(1)}) custom-call(f32[8,384,128]{2,1,0:T(8,128)S(1)} %all_to_all.20.got, bf16[256,128]{1,0:T(8,128)(2,1)S(1)} %copy-done.21, bf16[256,128]{1,0:T(8,128)(2,1)S(1)} %copy-done.20), custom_call_target="tpu_custom_call" | custom-call | tf_op jit(solution)/shard_map/third_kernel/pallas_call | solution.py:423
  137.8 1.7 collective-permute-start.5
  139.6 0.2 collective-permute-start.4
  139.8 2.2 collective-permute-done.5.vx_high
  142.1 3.7 %collective-permute-start.6 = (f32[3,24,4,128]{3,2,1,0:T(4,128)S(1)}, f32[3,24,4,128]{3,2,1,0:T(4,128)S(1)}, u32[]{:S(2)}, u32[]{:S(2)}) collective-permute-start(f32[3,24,4,128]{3,2,1,0:T(4,128)S(1)} %pad_maximum_fusion.6), channel_id=1, source_target_pairs={{0,1},{1,2},{2,3},{3,4},{4,5},{5,6},{6,7},{7,0},{8,9},{9,10},{10,1... | collective-permute-start | bytes 442376 | tf_op jit(solution)/shard_map/ppermute | solution.py:446
  145.8 4.1 %collective-permute-start.7 = (f32[3,24,4,128]{3,2,1,0:T(4,128)S(1)}, f32[3,24,4,128]{3,2,1,0:T(4,128)S(1)}, u32[]{:S(2)}, u32[]{:S(2)}) collective-permute-start(f32[3,24,4,128]{3,2,1,0:T(4,128)S(1)} %pad_maximum_fusion.7), channel_id=1, source_target_pairs={{1,0},{2,1},{3,2},{4,3},{5,4},{6,5},{7,6},{0,7},{9,8},{10,9},{11,1... | collective-permute-start | bytes 442376 | tf_op jit(solution)/shard_map/ppermute | solution.py:446
  149.9 4.3 %collective-permute-done.6.vy_low = f32[3,24,4,128]{3,2,1,0:T(4,128)S(1)} collective-permute-done((f32[3,24,4,128]{3,2,1,0:T(4,128)S(1)}, f32[3,24,4,128]{3,2,1,0:T(4,128)S(1)}, u32[]{:S(2)}, u32[]{:S(2)}) %collective-permute-start.6) | collective-permute-done | bytes 147488 | tf_op jit(solution)/shard_map/ppermute | solution.py:446
  154.3 2.8 %collective-permute-done.7.vy_high = f32[3,24,4,128]{3,2,1,0:T(4,128)S(1)} collective-permute-done((f32[3,24,4,128]{3,2,1,0:T(4,128)S(1)}, f32[3,24,4,128]{3,2,1,0:T(4,128)S(1)}, u32[]{:S(2)}, u32[]{:S(2)}) %collective-permute-start.7) | collective-permute-done | bytes 147488 | tf_op jit(solution)/shard_map/ppermute | solution.py:446
  157.1 32.2 %scalar_kernel.1 = (f32[32,32,256]{2,1,0:T(8,128)}, f32[8,192,128]{2,1,0:T(8,128)S(1)}) custom-call(f32[44,2,48,128]{3,2,1,0:T(8,128)S(1)} %brick_kernel.1.brick, f32[3,16,16,128]{3,2,1,0:T(8,128)S(1)} %get-tuple-element.6.velocity, f32[3,4,16,128]{3,2,1,0:T(8,128)S(1)} %collective-permute-done.4.vx_low, ...), custom_call_target="tpu_custom_call" | custom-call | tf_op jit(solution)/shard_map/scalar_kernel/pallas_call | solution.py:423
  189.2 21.7 %all_to_all.21.got = f32[8,192,128]{2,1,0:T(8,128)S(1)} all-to-all(f32[8,192,128]{2,1,0:T(8,128)S(1)} %get-tuple-element.8), channel_id=1, replica_groups=mesh['px'=32,'py'=8] {'py'}, dimensions={0} | all-to-all | bytes 1572864 | tf_op jit(solution)/shard_map/all_to_all | solution.py:502
  211.0 0.5 second_back_kernel.1
  211.5 41.7 %all_to_all.22.got = f32[32,48,128]{2,1,0:T(8,128)S(1)} all-to-all(f32[32,48,128]{2,1,0:T(8,128)S(1)} %second_back_kernel.1), channel_id=1, replica_groups=mesh['px'=32,'py'=8] {'px'}, dimensions={0} | all-to-all | bytes 1572864 | tf_op jit(solution)/shard_map/all_to_all | solution.py:506
  253.2 3.3 %first_back_kernel.1 = f32[2,3,4,16,512]{4,3,2,1,0:T(8,128)} custom-call(f32[32,48,128]{2,1,0:T(8,128)S(1)} %all_to_all.22.got, bf16[512,1024]{1,0:T(8,128)(2,1)S(1)} %copy-done.4, bf16[512,1024]{1,0:T(8,128)(2,1)S(1)} %copy-done.2), custom_call_target="tpu_custom_call" | custom-call | tf_op jit(solution)/shard_map/first_back_kernel/pallas_call | solution.py:423
  (42 shorter events, 0.2 us)
Async XLA Ops:
  1.7 6.4 %collective-permute-start.1 = (f32[6,32,256]{2,1,0:T(8,128)S(1)}, f32[6,32,256]{2,1,0:T(8,128)S(1)}, u32[]{:S(2)}, u32[]{:S(2)}) collective-permute-start(f32[6,32,256]{2,1,0:T(8,128)S(1)} %get-tuple-element.14), channel_id=1, source_target_pairs={{8,0},{16,8},{24,16},{32,24},{40,32},{48,40},{56,48},{64,56},{72,6... | collective-permute-start | bytes 589832 | tf_op jit(solution)/shard_map/ppermute | solution.py:446
  5.0 5.7 %collective-permute-start = (f32[6,32,256]{2,1,0:T(8,128)S(1)}, f32[6,32,256]{2,1,0:T(8,128)S(1)}, u32[]{:S(2)}, u32[]{:S(2)}) collective-permute-start(f32[6,32,256]{2,1,0:T(8,128)S(1)} %get-tuple-element.15), channel_id=1, source_target_pairs={{0,8},{8,16},{16,24},{24,32},{32,40},{40,48},{48,56},{56,64},{64,7... | collective-permute-start | bytes 589832 | tf_op jit(solution)/shard_map/ppermute | solution.py:446
  10.7 1.2 copy-start.1
  11.9 1.2 copy-start.3
  13.2 1.1 copy-start.7
  14.3 0.7 copy-start.24
  15.0 17.0 %copy-start.5 = (f32[6,32,256]{2,1,0:T(8,128)}, f32[6,32,256]{2,1,0:T(8,128)S(1)}, u32[]{:S(2)}) copy-start(f32[6,32,256]{2,1,0:T(8,128)S(1)} %collective-permute-done.x_low) | copy-start | bytes 589828
  19.4 12.5 %copy-start = (f32[32,32,256]{2,1,0:T(8,128)S(1)}, f32[32,32,256]{2,1,0:T(8,128)}, u32[]{:S(2)}) copy-start(f32[32,32,256]{2,1,0:T(8,128)} %scalar.1) | copy-start | bytes 3145732
  19.4 67.2 %all-to-all-start = ((f32[32,80,128]{2,1,0:T(8,128)}), f32[32,80,128]{2,1,0:T(8,128)}, u32[]{:S(2)}, u32[]{:S(2)}) async-start(f32[32,80,128]{2,1,0:T(8,128)} %first_kernel.1), calls=%async_computation | async-start | bytes 2621440 | tf_op jit(solution)/shard_map/all_to_all | solution.py:473
  32.2 40.1 %collective-permute-start.3 = (f32[108,2,256]{2,1,0:T(2,128)S(1)}, f32[108,2,256]{2,1,0:T(2,128)S(1)}, u32[]{:S(2)}, u32[]{:S(2)}) collective-permute-start(f32[108,2,256]{2,1,0:T(2,128)S(1)} %get-tuple-element.10), channel_id=1, source_target_pairs={{1,0},{2,1},{3,2},{4,3},{5,4},{6,5},{7,6},{0,7},{9,8},{10,9},{11,1... | collective-permute-start | bytes 663560 | tf_op jit(solution)/shard_map/ppermute | solution.py:446
  38.7 40.5 %collective-permute-start.2 = (f32[108,2,256]{2,1,0:T(2,128)S(1)}, f32[108,2,256]{2,1,0:T(2,128)S(1)}, u32[]{:S(2)}, u32[]{:S(2)}) collective-permute-start(f32[108,2,256]{2,1,0:T(2,128)S(1)} %get-tuple-element.11), channel_id=1, source_target_pairs={{0,1},{1,2},{2,3},{3,4},{4,5},{5,6},{6,7},{7,0},{8,9},{9,10},{10,1... | collective-permute-start | bytes 663560 | tf_op jit(solution)/shard_map/ppermute | solution.py:446
  72.2 0.7 copy-start.10
  79.2 0.7 copy-start.12
  79.9 0.9 copy-start.6
  80.8 0.9 copy-start.11
  81.7 0.9 copy-start.13
  82.7 0.9 copy-start.17
  83.6 3.0 %copy-start.16 = (f32[256,1]{1,0:T(8,128)S(1)}, f32[256,1]{1,0:T(8,128)}, u32[]{:S(2)}) copy-start(f32[256,1]{1,0:T(8,128)} %constant.52.clone.wave2) | copy-start | bytes 3076
  86.6 1.0 copy-start.8
  87.5 0.9 copy-start.9
  90.7 44.1 %copy-start.20 = (bf16[256,128]{1,0:T(8,128)(2,1)S(1)}, bf16[256,128]{1,0:T(8,128)(2,1)}, u32[]{:S(2)}) copy-start(bf16[256,128]{1,0:T(8,128)(2,1)} %constant.48.clone.tl) | copy-start | bytes 196612
  90.7 44.1 %copy-start.21 = (bf16[256,128]{1,0:T(8,128)(2,1)S(1)}, bf16[256,128]{1,0:T(8,128)(2,1)}, u32[]{:S(2)}) copy-start(bf16[256,128]{1,0:T(8,128)(2,1)} %constant.47.clone.th) | copy-start | bytes 196612
  134.8 22.3 %copy-start.18 = (bf16[2,128,256]{2,1,0:T(8,128)(2,1)S(1)}, bf16[2,128,256]{2,1,0:T(8,128)(2,1)}, u32[]{:S(2)}) copy-start(bf16[2,128,256]{2,1,0:T(8,128)(2,1)} %constant.53.clone.rise) | copy-start | bytes 393220
  134.8 22.3 %copy-start.19 = (bf16[256,256]{1,0:T(8,128)(2,1)S(1)}, bf16[256,256]{1,0:T(8,128)(2,1)}, u32[]{:S(2)}) copy-start(bf16[256,256]{1,0:T(8,128)(2,1)} %constant.50.clone.join) | copy-start | bytes 393220
  134.8 22.2 %copy-start.22 = (bf16[128,256]{1,0:T(8,128)(2,1)S(1)}, bf16[128,256]{1,0:T(8,128)(2,1)}, u32[]{:S(2)}) copy-start(bf16[128,256]{1,0:T(8,128)(2,1)} %constant.55.clone.tl) | copy-start | bytes 196612
  134.8 22.2 %copy-start.23 = (bf16[128,256]{1,0:T(8,128)(2,1)S(1)}, bf16[128,256]{1,0:T(8,128)(2,1)}, u32[]{:S(2)}) copy-start(bf16[128,256]{1,0:T(8,128)(2,1)} %constant.54.clone.th) | copy-start | bytes 196612
  137.8 4.1 %collective-permute-start.5 = (f32[3,4,16,128]{3,2,1,0:T(8,128)S(1)}, f32[3,4,16,128]{3,2,1,0:T(8,128)S(1)}, u32[]{:S(2)}, u32[]{:S(2)}) collective-permute-start(f32[3,4,16,128]{3,2,1,0:T(8,128)S(1)} %get-tuple-element.18), channel_id=1, source_target_pairs={{8,0},{16,8},{24,16},{32,24},{40,32},{48,40},{56,48},{64,56},{72,6... | collective-permute-start | bytes 294920 | tf_op jit(solution)/shard_map/ppermute | solution.py:446
  139.6 2.4 collective-permute-start.4
  142.1 12.2 %collective-permute-start.6 = (f32[3,24,4,128]{3,2,1,0:T(4,128)S(1)}, f32[3,24,4,128]{3,2,1,0:T(4,128)S(1)}, u32[]{:S(2)}, u32[]{:S(2)}) collective-permute-start(f32[3,24,4,128]{3,2,1,0:T(4,128)S(1)} %pad_maximum_fusion.6), channel_id=1, source_target_pairs={{0,1},{1,2},{2,3},{3,4},{4,5},{5,6},{6,7},{7,0},{8,9},{9,10},{10,1... | collective-permute-start | bytes 442376 | tf_op jit(solution)/shard_map/ppermute | solution.py:446
  145.8 11.2 %collective-permute-start.7 = (f32[3,24,4,128]{3,2,1,0:T(4,128)S(1)}, f32[3,24,4,128]{3,2,1,0:T(4,128)S(1)}, u32[]{:S(2)}, u32[]{:S(2)}) collective-permute-start(f32[3,24,4,128]{3,2,1,0:T(4,128)S(1)} %pad_maximum_fusion.7), channel_id=1, source_target_pairs={{1,0},{2,1},{3,2},{4,3},{5,4},{6,5},{7,6},{0,7},{9,8},{10,9},{11,1... | collective-permute-start | bytes 442376 | tf_op jit(solution)/shard_map/ppermute | solution.py:446
  189.2 21.7 %copy-start.14 = (bf16[256,256]{1,0:T(8,128)(2,1)S(1)}, bf16[256,256]{1,0:T(8,128)(2,1)}, u32[]{:S(2)}) copy-start(bf16[256,256]{1,0:T(8,128)(2,1)} %constant.57.clone.tl) | copy-start | bytes 393220
  189.2 21.7 %copy-start.15 = (bf16[256,256]{1,0:T(8,128)(2,1)S(1)}, bf16[256,256]{1,0:T(8,128)(2,1)}, u32[]{:S(2)}) copy-start(bf16[256,256]{1,0:T(8,128)(2,1)} %constant.56.clone.th) | copy-start | bytes 393220
  211.0 42.3 %copy-start.2 = (bf16[512,1024]{1,0:T(8,128)(2,1)S(1)}, bf16[512,1024]{1,0:T(8,128)(2,1)}, u32[]{:S(2)}) copy-start(bf16[512,1024]{1,0:T(8,128)(2,1)} %constant.44.clone.tl) | copy-start | bytes 3145732
  211.0 42.3 %copy-start.4 = (bf16[512,1024]{1,0:T(8,128)(2,1)S(1)}, bf16[512,1024]{1,0:T(8,128)(2,1)}, u32[]{:S(2)}) copy-start(bf16[512,1024]{1,0:T(8,128)(2,1)} %constant.43.clone.th) | copy-start | bytes 3145732

commit v2 on v1

--- a/solution.py
+++ b/solution.py
@@ -111,7 +111,7 @@
     return v
 
 
-def first_kernel(spec, wave, th, tl, x_low, x_high, out, y):
+def first_kernel(spec, wave, th, tl, out, y):
     rows = []
     for f in (0, 1, 2, 1, 2):
         plain, turned = [], []
@@ -134,7 +134,7 @@
         out[:, 16 * f : 16 * f + 16, :] = y[N1 * f : N1 * f + N1, :].reshape(GX, 16, 128)
 
 
-def second_kernel(got, wave2, wave3, th, tl, brick, out):
+def second_kernel(got, wave2, wave3, th, tl, x_low, x_high, out):
     c = []
     for f in range(5):
         halves_ = [got[:, 16 * f + 8 * h : 16 * f + 8 * h + 8, :].reshape(256, 128) for h in range(2)]
@@ -417,13 +417,14 @@
             out[1, f, r] = ci - sr
 
 
-def call(kernel, out_shape, *args, scratch=(), late=0):
+def call(kernel, out_shape, *args, scratch=(), late=0, hbm=False):
     specs = [pl.BlockSpec(memory_space=pltpu.VMEM)] * (len(args) - late)
     specs += [pl.BlockSpec(memory_space=pl.ANY)] * late
     return pl.pallas_call(
         kernel,
         in_specs=specs,
-        out_shape=out_shape,
+        out_shape=out_shape if not hbm else pltpu.HBM(out_shape.shape, out_shape.dtype),
+        out_specs=jax.tree.map(lambda _: pl.BlockSpec(memory_space=pltpu.VMEM), out_shape),
         scratch_shapes=list(scratch),
         interpret=INTERPRET,
         name=kernel.__name__,
@@ -467,11 +468,11 @@
         scratch=(pltpu.VMEM((SLABS, ROWS, 256), F32),),
     )
     sent = call(
-        first_kernel, shape(GX, 80, 128), spectrum, jnp.asarray(wave_first), *first, x_low, x_high,
-        scratch=(pltpu.VMEM((5 * N1, 128), F32),), late=2,
+        first_kernel, shape(GX, 80, 128), spectrum, jnp.asarray(wave_first), *first,
+        scratch=(pltpu.VMEM((5 * N1, 128), F32),),
     )
     got = lax.all_to_all(sent, "px", split_axis=0, concat_axis=0, tiled=True)
-    sent = call(second_kernel, shape(GY, 384, 128), got, jnp.asarray(wave_second), wave_third, *second, brick, late=1)
+    sent = call(second_kernel, shape(GY, 384, 128), got, jnp.asarray(wave_second), wave_third, *second, x_low, x_high, late=2, hbm=True)
     got = lax.all_to_all(sent, "py", split_axis=0, concat_axis=0, tiled=True)
     velocity, vorticity = call(
         third_kernel, (shape(3, C1, C2, N3), shape(3, C1, C2, N3)), got, *third

time: 257 us -> 237 us (0.922)
  blocking collectives: 108 us -> 61.9 us
  waiting for transfers between devices: 54.2 us -> 78.7 us
  starting transfers between devices: 31.9 us -> 38.9 us
  local copies, waits for them, and re-layouts: 13.2 us -> 6.77 us
    all_to_all x0 -> x1, waiting for transfers between devices: none -> 39.7 us  [body(): got = lax.all_to_all(sent, 'py', split_axis=0, concat_axis=0, tiled=True)]
    all_to_all x2 -> x1, blocking collectives: 65.8 us -> 29.9 us  [body(): got = lax.all_to_all(sent, 'py', split_axis=0, concat_axis=0, tiled=True)]
    ppermute x8, waiting for transfers between devices: 54.2 us -> 29.2 us  [edges(): return (lax.ppermute(last, axis, up), lax.ppermute(first, axis, down))]
    all_to_all x1, waiting for transfers between devices: 0.01 us -> 9.78 us  [body(): got = lax.all_to_all(sent, 'px', split_axis=0, concat_axis=0, tiled=True)]
    all_to_all x1, blocking collectives: 41.7 us -> 32 us  [body(): got = lax.all_to_all(sent, 'px', split_axis=0, concat_axis=0, tiled=True)]
    all_to_all x0 -> x1, starting transfers between devices: none -> 7.95 us  [body(): got = lax.all_to_all(sent, 'py', split_axis=0, concat_axis=0, tiled=True)]
    unnamed x50 -> x38, local copies, waits for them, and re-layouts: 11.3 us -> 5.17 us
  transfers between devices with their start and end apart: 9 -> 10, of which waited for: 7 -> 7; matrix products, arithmetic and copies ran while one was open for 0% -> 1% of each run, Pallas kernels for 1% -> 3%
where the time goes in v2:
time: 237 us; the launch traced here: 236 us
  waiting for transfers between devices  78.7 us (33%)
  blocking collectives  61.9 us (26%)
  Pallas kernels  48.4 us (20%)
  starting transfers between devices  38.9 us (16%)
  local copies, waits for them, and re-layouts  6.77 us (3%)
    pallas_call x7, Pallas kernels, call(): pl.pallas_call(kernel, in_specs=specs, out_shape=out_shape if not hbm els...  48.4 us
    all_to_all x1, waiting for transfers between devices, body(): got = lax.all_to_all(sent, 'py', split_axis=0, concat_axis=0, tiled=True)  39.7 us
    all_to_all x1, blocking collectives, body(): got = lax.all_to_all(sent, 'px', split_axis=0, concat_axis=0, tiled=True)  32 us
    all_to_all x1, blocking collectives, body(): got = lax.all_to_all(sent, 'py', split_axis=0, concat_axis=0, tiled=True)  29.9 us
    ppermute x8, waiting for transfers between devices, edges(): return (lax.ppermute(last, axis, up), lax.ppermute(first, axis, down))  29.2 us
    ppermute x8, starting transfers between devices, edges(): return (lax.ppermute(last, axis, up), lax.ppermute(first, axis, down))  20.6 us
    all_to_all x1, starting transfers between devices, body(): got = lax.all_to_all(sent, 'px', split_axis=0, concat_axis=0, tiled=True)  10.3 us
    all_to_all x1, waiting for transfers between devices, body(): got = lax.all_to_all(sent, 'px', split_axis=0, concat_axis=0, tiled=True)  9.78 us
  transfers between devices with their start and end apart: 10, of which 7 were waited for; matrix products, arithmetic and copies ran while one was open for 1% of the time, Pallas kernels for 3%

profile of v2, /device:TPU:1, one launch (start us, length us, event | category | flops | bytes accessed | tf_op | source)
XLA Modules:
  0.0 236.5 jit_solution(12744797301896312486)
XLA Ops:
  0.6 0.0 copy-start.1
  0.6 1.2 copy-done.1
  1.9 1.2 copy-done.3
  3.1 1.1 copy-done.5
  4.2 0.7 copy-done.18
  4.9 4.4 %first_kernel.1 = f32[32,80,128]{2,1,0:T(8,128)} custom-call(f32[2,3,4,16,512]{4,3,2,1,0:T(8,128)S(1)} %copy-done.5, f32[1,1024]{1,0:T(1,128)S(1)} %copy-done.18, bf16[512,1024]{1,0:T(8,128)(2,1)S(1)} %copy-done.3, bf16[512,1024]{1,0:T(8,128)(2,1)S(1)} %copy-done.1), custom_call_target="tpu_custom_call" | custom-call | tf_op jit(solution)/shard_map/first_kernel/pallas_call | solution.py:423
  9.3 10.3 %all-to-all-start = ((f32[32,80,128]{2,1,0:T(8,128)}), f32[32,80,128]{2,1,0:T(8,128)S(1)}, u32[]{:S(2)}, u32[]{:S(2)}) async-start(f32[32,80,128]{2,1,0:T(8,128)} %first_kernel.1), calls=%async_computation | async-start | bytes 2621440 | tf_op jit(solution)/shard_map/all_to_all | solution.py:474
  19.7 0.0 copy-done
  19.7 0.8 fusion.5
  20.4 0.2 collective-permute-start.1
  20.7 1.5 collective-permute-start
  22.2 0.7 dynamic-slice_bitcast_fusion.wave3
  22.9 14.9 %collective-permute-done.1.x_high = f32[6,32,256]{2,1,0:T(8,128)S(1)} collective-permute-done((f32[6,32,256]{2,1,0:T(8,128)}, f32[6,32,256]{2,1,0:T(8,128)S(1)}, u32[]{:S(2)}, u32[]{:S(2)}) %collective-permute-start.1) | collective-permute-done | bytes 196640 | tf_op jit(solution)/shard_map/ppermute | solution.py:447
  37.8 7.6 %collective-permute-done.x_low = f32[6,32,256]{2,1,0:T(8,128)S(1)} collective-permute-done((f32[6,32,256]{2,1,0:T(8,128)}, f32[6,32,256]{2,1,0:T(8,128)S(1)}, u32[]{:S(2)}, u32[]{:S(2)}) %collective-permute-start) | collective-permute-done | bytes 196640 | tf_op jit(solution)/shard_map/ppermute | solution.py:447
  45.4 9.8 %all-to-all-done.got = f32[32,80,128]{2,1,0:T(8,128)S(1)} async-done(((f32[32,80,128]{2,1,0:T(8,128)}), f32[32,80,128]{2,1,0:T(8,128)S(1)}, u32[]{:S(2)}, u32[]{:S(2)}) %all-to-all-start) | async-done | bytes 1310752 | tf_op jit(solution)/shard_map/all_to_all | solution.py:474
  55.1 0.0 copy-done.6
  55.1 0.0 copy-done.7
  55.1 0.0 copy-done.11
  55.1 2.1 second_kernel.1
  57.2 8.0 %all-to-all-start.1 = ((f32[8,384,128]{2,1,0:T(8,128)}), f32[8,384,128]{2,1,0:T(8,128)S(1)}, u32[]{:S(2)}, u32[]{:S(2)}) async-start(f32[8,384,128]{2,1,0:T(8,128)} %second_kernel.1), calls=%async_computation.1 | async-start | bytes 3145728 | tf_op jit(solution)/shard_map/all_to_all | solution.py:476
  65.2 0.1 fusion.4
  65.3 0.9 fusion.1
  66.2 7.5 %collective-permute-start.3 = (f32[108,2,256]{2,1,0:T(2,128)}, f32[108,2,256]{2,1,0:T(2,128)S(1)}, u32[]{:S(2)}, u32[]{:S(2)}) collective-permute-start(f32[108,2,256]{2,1,0:T(2,128)} %get-tuple-element.10), channel_id=1, source_target_pairs={{1,0},{2,1},{3,2},{4,3},{5,4},{6,5},{7,6},{0,7},{9,8},{10,9},{11,1... | collective-permute-start | bytes 663560 | tf_op jit(solution)/shard_map/ppermute | solution.py:447
  73.7 0.0 collective-permute-start.2
  73.7 39.7 %all-to-all-done.1.got = f32[8,384,128]{2,1,0:T(8,128)S(1)} async-done(((f32[8,384,128]{2,1,0:T(8,128)}), f32[8,384,128]{2,1,0:T(8,128)S(1)}, u32[]{:S(2)}, u32[]{:S(2)}) %all-to-all-start.1) | async-done | bytes 1572896 | tf_op jit(solution)/shard_map/all_to_all | solution.py:476
  113.4 0.8 copy-done.15
  114.2 3.0 %third_kernel.1 = (f32[3,16,16,128]{3,2,1,0:T(8,128)S(1)}, f32[3,16,16,128]{3,2,1,0:T(8,128)S(1)}) custom-call(f32[8,384,128]{2,1,0:T(8,128)S(1)} %all-to-all-done.1.got, bf16[256,128]{1,0:T(8,128)(2,1)S(1)} %copy-done.15, bf16[256,128]{1,0:T(8,128)(2,1)S(1)} %copy-done.14), custom_call_target="tpu_custom_call" | custom-call | tf_op jit(solution)/shard_map/third_kernel/pallas_call | solution.py:423
  117.2 2.5 %collective-permute-start.5 = (f32[3,4,16,128]{3,2,1,0:T(8,128)S(1)}, f32[3,4,16,128]{3,2,1,0:T(8,128)S(1)}, u32[]{:S(2)}, u32[]{:S(2)}) collective-permute-start(f32[3,4,16,128]{3,2,1,0:T(8,128)S(1)} %get-tuple-element.18), channel_id=1, source_target_pairs={{8,0},{16,8},{24,16},{32,24},{40,32},{48,40},{56,48},{64,56},{72,6... | collective-permute-start | bytes 294920 | tf_op jit(solution)/shard_map/ppermute | solution.py:447
  119.8 1.1 collective-permute-start.4
  120.9 2.5 %collective-permute-done.5.vx_high = f32[3,4,16,128]{3,2,1,0:T(8,128)S(1)} collective-permute-done((f32[3,4,16,128]{3,2,1,0:T(8,128)S(1)}, f32[3,4,16,128]{3,2,1,0:T(8,128)S(1)}, u32[]{:S(2)}, u32[]{:S(2)}) %collective-permute-start.5) | collective-permute-done | bytes 98336 | tf_op jit(solution)/shard_map/ppermute | solution.py:447
  123.3 0.0 collective-permute-done.4.vx_low
  123.4 4.3 %collective-permute-start.6 = (f32[3,24,4,128]{3,2,1,0:T(4,128)S(1)}, f32[3,24,4,128]{3,2,1,0:T(4,128)S(1)}, u32[]{:S(2)}, u32[]{:S(2)}) collective-permute-start(f32[3,24,4,128]{3,2,1,0:T(4,128)S(1)} %pad_maximum_fusion.6), channel_id=1, source_target_pairs={{0,1},{1,2},{2,3},{3,4},{4,5},{5,6},{6,7},{7,0},{8,9},{9,10},{10,1... | collective-permute-start | bytes 442376 | tf_op jit(solution)/shard_map/ppermute | solution.py:447
  127.7 0.0 copy-start.12
  127.7 0.0 copy-start.13
  127.8 0.0 copy-start.16
  127.8 0.0 copy-start.17
  127.8 3.5 %collective-permute-start.7 = (f32[3,24,4,128]{3,2,1,0:T(4,128)S(1)}, f32[3,24,4,128]{3,2,1,0:T(4,128)S(1)}, u32[]{:S(2)}, u32[]{:S(2)}) collective-permute-start(f32[3,24,4,128]{3,2,1,0:T(4,128)S(1)} %pad_maximum_fusion.7), channel_id=1, source_target_pairs={{1,0},{2,1},{3,2},{4,3},{5,4},{6,5},{7,6},{0,7},{9,8},{10,9},{11,1... | collective-permute-start | bytes 442376 | tf_op jit(solution)/shard_map/ppermute | solution.py:447
  131.3 0.0 collective-permute-done.3.y_high
  131.3 0.0 collective-permute-done.2.y_low
  131.3 2.9 %brick_kernel.1.brick = f32[44,2,48,128]{3,2,1,0:T(8,128)S(1)} custom-call(f32[32,32,256]{2,1,0:T(8,128)S(1)} %copy-done, f32[6,32,256]{2,1,0:T(8,128)S(1)} %collective-permute-done.x_low, f32[6,32,256]{2,1,0:T(8,128)S(1)} %collective-permute-done.1.x_high, f32[108,2,256]{2,1,0:T(2,128)S(1)} %collective-permute-done.2.y_low, ...), custom_call_target="tpu_custom_call" | custom-call | tf_op jit(solution)/shard_map/brick_kernel/pallas_call | solution.py:423
  134.3 1.1 collective-permute-done.6.vy_low
  135.3 3.2 %collective-permute-done.7.vy_high = f32[3,24,4,128]{3,2,1,0:T(4,128)S(1)} collective-permute-done((f32[3,24,4,128]{3,2,1,0:T(4,128)S(1)}, f32[3,24,4,128]{3,2,1,0:T(4,128)S(1)}, u32[]{:S(2)}, u32[]{:S(2)}) %collective-permute-start.7) | collective-permute-done | bytes 147488 | tf_op jit(solution)/shard_map/ppermute | solution.py:447
  138.5 0.0 copy-done.16
  138.5 32.2 %scalar_kernel.1 = (f32[32,32,256]{2,1,0:T(8,128)}, f32[8,192,128]{2,1,0:T(8,128)S(1)}) custom-call(f32[44,2,48,128]{3,2,1,0:T(8,128)S(1)} %brick_kernel.1.brick, f32[3,16,16,128]{3,2,1,0:T(8,128)S(1)} %get-tuple-element.6.velocity, f32[3,4,16,128]{3,2,1,0:T(8,128)S(1)} %collective-permute-done.4.vx_low, ...), custom_call_target="tpu_custom_call" | custom-call | tf_op jit(solution)/shard_map/scalar_kernel/pallas_call | solution.py:423
  170.7 29.9 %all_to_all.20.got = f32[8,192,128]{2,1,0:T(8,128)S(1)} all-to-all(f32[8,192,128]{2,1,0:T(8,128)S(1)} %get-tuple-element.8), channel_id=1, replica_groups=mesh['px'=32,'py'=8] {'py'}, dimensions={0} | all-to-all | bytes 1572864 | tf_op jit(solution)/shard_map/all_to_all | solution.py:503
  200.7 0.5 second_back_kernel.1
  201.2 32.0 %all_to_all.21.got = f32[32,48,128]{2,1,0:T(8,128)S(1)} all-to-all(f32[32,48,128]{2,1,0:T(8,128)S(1)} %second_back_kernel.1), channel_id=1, replica_groups=mesh['px'=32,'py'=8] {'px'}, dimensions={0} | all-to-all | bytes 1572864 | tf_op jit(solution)/shard_map/all_to_all | solution.py:507
  233.2 3.3 %first_back_kernel.1 = f32[2,3,4,16,512]{4,3,2,1,0:T(8,128)} custom-call(f32[32,48,128]{2,1,0:T(8,128)S(1)} %all_to_all.21.got, bf16[512,1024]{1,0:T(8,128)(2,1)S(1)} %copy-done.4, bf16[512,1024]{1,0:T(8,128)(2,1)S(1)} %copy-done.2), custom_call_target="tpu_custom_call" | custom-call | tf_op jit(solution)/shard_map/first_back_kernel/pallas_call | solution.py:423
  (31 shorter events, 0.2 us)
Async XLA Ops:
  0.6 1.2 copy-start.1
  1.9 1.2 copy-start.3
  3.1 1.1 copy-start.5
  4.2 0.7 copy-start.18
  9.3 10.3 %copy-start = (f32[32,32,256]{2,1,0:T(8,128)S(1)}, f32[32,32,256]{2,1,0:T(8,128)}, u32[]{:S(2)}) copy-start(f32[32,32,256]{2,1,0:T(8,128)} %scalar.1) | copy-start | bytes 3145732
  9.3 45.8 %copy-start.6 = (bf16[2,256,256]{2,1,0:T(8,128)(2,1)S(1)}, bf16[2,256,256]{2,1,0:T(8,128)(2,1)}, u32[]{:S(2)}) copy-start(bf16[2,256,256]{2,1,0:T(8,128)(2,1)} %constant.46.clone.tl) | copy-start | bytes 786436
  9.3 45.8 %copy-start.7 = (bf16[2,256,256]{2,1,0:T(8,128)(2,1)S(1)}, bf16[2,256,256]{2,1,0:T(8,128)(2,1)}, u32[]{:S(2)}) copy-start(bf16[2,256,256]{2,1,0:T(8,128)(2,1)} %constant.45.clone.th) | copy-start | bytes 786436
  9.3 45.8 %copy-start.11 = (f32[256,1]{1,0:T(8,128)S(1)}, f32[256,1]{1,0:T(8,128)}, u32[]{:S(2)}) copy-start(f32[256,1]{1,0:T(8,128)} %constant.52.clone.wave2) | copy-start | bytes 3076
  9.3 45.8 %all-to-all-start = ((f32[32,80,128]{2,1,0:T(8,128)}), f32[32,80,128]{2,1,0:T(8,128)S(1)}, u32[]{:S(2)}, u32[]{:S(2)}) async-start(f32[32,80,128]{2,1,0:T(8,128)} %first_kernel.1), calls=%async_computation | async-start | bytes 2621440 | tf_op jit(solution)/shard_map/all_to_all | solution.py:474
  20.4 17.3 %collective-permute-start.1 = (f32[6,32,256]{2,1,0:T(8,128)}, f32[6,32,256]{2,1,0:T(8,128)S(1)}, u32[]{:S(2)}, u32[]{:S(2)}) collective-permute-start(f32[6,32,256]{2,1,0:T(8,128)} %get-tuple-element.14), channel_id=1, source_target_pairs={{8,0},{16,8},{24,16},{32,24},{40,32},{48,40},{56,48},{64,56},{72,6... | collective-permute-start | bytes 589832 | tf_op jit(solution)/shard_map/ppermute | solution.py:447
  20.7 24.7 %collective-permute-start = (f32[6,32,256]{2,1,0:T(8,128)}, f32[6,32,256]{2,1,0:T(8,128)S(1)}, u32[]{:S(2)}, u32[]{:S(2)}) collective-permute-start(f32[6,32,256]{2,1,0:T(8,128)} %get-tuple-element.15), channel_id=1, source_target_pairs={{0,8},{8,16},{16,24},{24,32},{32,40},{40,48},{48,56},{56,64},{64,7... | collective-permute-start | bytes 589832 | tf_op jit(solution)/shard_map/ppermute | solution.py:447
  57.2 56.2 %all-to-all-start.1 = ((f32[8,384,128]{2,1,0:T(8,128)}), f32[8,384,128]{2,1,0:T(8,128)S(1)}, u32[]{:S(2)}, u32[]{:S(2)}) async-start(f32[8,384,128]{2,1,0:T(8,128)} %second_kernel.1), calls=%async_computation.1 | async-start | bytes 3145728 | tf_op jit(solution)/shard_map/all_to_all | solution.py:476
  65.2 48.2 %copy-start.14 = (bf16[256,128]{1,0:T(8,128)(2,1)S(1)}, bf16[256,128]{1,0:T(8,128)(2,1)}, u32[]{:S(2)}) copy-start(bf16[256,128]{1,0:T(8,128)(2,1)} %constant.48.clone.tl) | copy-start | bytes 196612
  66.2 65.1 %collective-permute-start.3 = (f32[108,2,256]{2,1,0:T(2,128)}, f32[108,2,256]{2,1,0:T(2,128)S(1)}, u32[]{:S(2)}, u32[]{:S(2)}) collective-permute-start(f32[108,2,256]{2,1,0:T(2,128)} %get-tuple-element.10), channel_id=1, source_target_pairs={{1,0},{2,1},{3,2},{4,3},{5,4},{6,5},{7,6},{0,7},{9,8},{10,9},{11,1... | collective-permute-start | bytes 663560 | tf_op jit(solution)/shard_map/ppermute | solution.py:447
  73.7 57.7 %collective-permute-start.2 = (f32[108,2,256]{2,1,0:T(2,128)}, f32[108,2,256]{2,1,0:T(2,128)S(1)}, u32[]{:S(2)}, u32[]{:S(2)}) collective-permute-start(f32[108,2,256]{2,1,0:T(2,128)} %get-tuple-element.11), channel_id=1, source_target_pairs={{0,1},{1,2},{2,3},{3,4},{4,5},{5,6},{6,7},{7,0},{8,9},{9,10},{10,1... | collective-permute-start | bytes 663560 | tf_op jit(solution)/shard_map/ppermute | solution.py:447
  113.4 0.8 copy-start.15
  114.2 17.1 %copy-start.10 = (bf16[256,256]{1,0:T(8,128)(2,1)S(1)}, bf16[256,256]{1,0:T(8,128)(2,1)}, u32[]{:S(2)}) copy-start(bf16[256,256]{1,0:T(8,128)(2,1)} %constant.49.clone.table) | copy-start | bytes 393220
  117.2 6.1 %collective-permute-start.5 = (f32[3,4,16,128]{3,2,1,0:T(8,128)S(1)}, f32[3,4,16,128]{3,2,1,0:T(8,128)S(1)}, u32[]{:S(2)}, u32[]{:S(2)}) collective-permute-start(f32[3,4,16,128]{3,2,1,0:T(8,128)S(1)} %get-tuple-element.18), channel_id=1, source_target_pairs={{8,0},{16,8},{24,16},{32,24},{40,32},{48,40},{56,48},{64,56},{72,6... | collective-permute-start | bytes 294920 | tf_op jit(solution)/shard_map/ppermute | solution.py:447
  119.8 3.6 %collective-permute-start.4 = (f32[3,4,16,128]{3,2,1,0:T(8,128)S(1)}, f32[3,4,16,128]{3,2,1,0:T(8,128)S(1)}, u32[]{:S(2)}, u32[]{:S(2)}) collective-permute-start(f32[3,4,16,128]{3,2,1,0:T(8,128)S(1)} %get-tuple-element.19), channel_id=1, source_target_pairs={{0,8},{8,16},{16,24},{24,32},{32,40},{40,48},{48,56},{56,64},{64,7... | collective-permute-start | bytes 294920 | tf_op jit(solution)/shard_map/ppermute | solution.py:447
  123.4 11.9 %collective-permute-start.6 = (f32[3,24,4,128]{3,2,1,0:T(4,128)S(1)}, f32[3,24,4,128]{3,2,1,0:T(4,128)S(1)}, u32[]{:S(2)}, u32[]{:S(2)}) collective-permute-start(f32[3,24,4,128]{3,2,1,0:T(4,128)S(1)} %pad_maximum_fusion.6), channel_id=1, source_target_pairs={{0,1},{1,2},{2,3},{3,4},{4,5},{5,6},{6,7},{7,0},{8,9},{9,10},{10,1... | collective-permute-start | bytes 442376 | tf_op jit(solution)/shard_map/ppermute | solution.py:447
  127.7 10.8 %copy-start.12 = (bf16[2,128,256]{2,1,0:T(8,128)(2,1)S(1)}, bf16[2,128,256]{2,1,0:T(8,128)(2,1)}, u32[]{:S(2)}) copy-start(bf16[2,128,256]{2,1,0:T(8,128)(2,1)} %constant.53.clone.rise) | copy-start | bytes 393220
  127.7 10.8 %copy-start.13 = (bf16[256,256]{1,0:T(8,128)(2,1)S(1)}, bf16[256,256]{1,0:T(8,128)(2,1)}, u32[]{:S(2)}) copy-start(bf16[256,256]{1,0:T(8,128)(2,1)} %constant.50.clone.join) | copy-start | bytes 393220
  127.8 10.8 %copy-start.16 = (bf16[128,256]{1,0:T(8,128)(2,1)S(1)}, bf16[128,256]{1,0:T(8,128)(2,1)}, u32[]{:S(2)}) copy-start(bf16[128,256]{1,0:T(8,128)(2,1)} %constant.55.clone.tl) | copy-start | bytes 196612
  127.8 10.8 %copy-start.17 = (bf16[128,256]{1,0:T(8,128)(2,1)S(1)}, bf16[128,256]{1,0:T(8,128)(2,1)}, u32[]{:S(2)}) copy-start(bf16[128,256]{1,0:T(8,128)(2,1)} %constant.54.clone.th) | copy-start | bytes 196612
  127.8 10.7 %collective-permute-start.7 = (f32[3,24,4,128]{3,2,1,0:T(4,128)S(1)}, f32[3,24,4,128]{3,2,1,0:T(4,128)S(1)}, u32[]{:S(2)}, u32[]{:S(2)}) collective-permute-start(f32[3,24,4,128]{3,2,1,0:T(4,128)S(1)} %pad_maximum_fusion.7), channel_id=1, source_target_pairs={{1,0},{2,1},{3,2},{4,3},{5,4},{6,5},{7,6},{0,7},{9,8},{10,9},{11,1... | collective-permute-start | bytes 442376 | tf_op jit(solution)/shard_map/ppermute | solution.py:447
  170.7 29.9 %copy-start.8 = (bf16[256,256]{1,0:T(8,128)(2,1)S(1)}, bf16[256,256]{1,0:T(8,128)(2,1)}, u32[]{:S(2)}) copy-start(bf16[256,256]{1,0:T(8,128)(2,1)} %constant.57.clone.tl) | copy-start | bytes 393220
  170.7 30.0 %copy-start.9 = (bf16[256,256]{1,0:T(8,128)(2,1)S(1)}, bf16[256,256]{1,0:T(8,128)(2,1)}, u32[]{:S(2)}) copy-start(bf16[256,256]{1,0:T(8,128)(2,1)} %constant.56.clone.th) | copy-start | bytes 393220
  200.7 32.5 %copy-start.2 = (bf16[512,1024]{1,0:T(8,128)(2,1)S(1)}, bf16[512,1024]{1,0:T(8,128)(2,1)}, u32[]{:S(2)}) copy-start(bf16[512,1024]{1,0:T(8,128)(2,1)} %constant.44.clone.tl) | copy-start | bytes 3145732
  200.7 32.5 %copy-start.4 = (bf16[512,1024]{1,0:T(8,128)(2,1)S(1)}, bf16[512,1024]{1,0:T(8,128)(2,1)}, u32[]{:S(2)}) copy-start(bf16[512,1024]{1,0:T(8,128)(2,1)} %constant.43.clone.th) | copy-start | bytes 3145732

commit v3 on v2

--- a/solution.py
+++ b/solution.py
@@ -7,6 +7,7 @@
 from jax.experimental import pallas as pl
 from jax.experimental.pallas import tpu as pltpu
 from jax.sharding import PartitionSpec as P
+
 
 NSUB = 3
 STEP_RATIO = 0.08
@@ -169,12 +170,9 @@
         out[f % 3] = u.reshape(C1, C2, N3)
 
 
-def force_lines(velocity, vorticity, b, th, tl, out):
-    u = [velocity[i].reshape(C1 * C2, N3) for i in range(3)]
-    w = [vorticity[i].reshape(C1 * C2, N3) for i in range(3)]
-    force = [u[1] * w[2] - u[2] * w[1], u[2] * w[0] - u[0] * w[2], u[0] * w[1] - u[1] * w[0] + b]
-    for f in range(3):
-        lines = dot3(split(force[f]), (th[...], tl[...]))
+def send_lines(force, th, tl, out):
+    for f, field in enumerate(force):
+        lines = dot3(split(field), (th[...], tl[...]))
         for ri in range(2):
             for h in range(2):
                 at = ((f * 2 + ri) * 2 + h) * 16
@@ -182,9 +180,18 @@
                     lines[(h * 8 + i) * 16 : (h * 8 + i) * 16 + 16, ri * 128 : ri * 128 + 128]
                     for i in range(8)
                 ]
-                w8 = swap_groups(v)
+                moved = swap_groups(v)
                 for q in range(GY):
-                    out[q, at : at + 16, :] = w8[q]
+                    out[q, at : at + 16, :] = moved[q]
+
+
+def flat_fields(velocity, vorticity):
+    return [[part[i].reshape(C1 * C2, N3) for i in range(3)] for part in (velocity, vorticity)]
+
+
+def force_kernel(velocity, vorticity, th, tl, out):
+    u, w = flat_fields(velocity, vorticity)
+    send_lines([u[1] * w[2] - u[2] * w[1], u[2] * w[0] - u[0] * w[2]], th, tl, out)
 
 
 def parted(table):
@@ -276,11 +283,41 @@
     lax.fori_loop(0, SLABS // 4, part, 0)
 
 
-def scalar_kernel(
-    brick, velocity, vx_low, vx_high, vy_low, vy_high, vorticity,
-    rise, join, th, tl,
-    advanced, out,
-    ta, tb, last, vw, su, sf, f1, f2, f3, bs,
+def substep(source, target, turn, f1, f2, f3):
+    low = 2 + 2 * turn
+    begin = []
+    for h in range(2):
+        t0, t1, t2, t3 = (source[low - 2 + o, h] for o in range(4))
+        j0, j1, j2 = t1 - t0, t2 - t1, t3 - t2
+        h1, h2 = 0.5 * limited(j0, j1), 0.5 * limited(j1, j2)
+        begin.append((t2 + h2, j2, upwind(f1[low - 1, h], t1 + h1, t2 - h2, j1)))
+
+    def step(i, carry):
+        here = [source[i, h] for h in range(2)]
+        change = list(lane_divergence(*here, f3[i, 0], f3[i, 1]))
+        done = []
+        for h in range(2):
+            left, jump, before = carry[h]
+            ahead = source[i + 1, h]
+            next_jump = source[i + 2, h] - ahead
+            half = 0.5 * limited(jump, next_jump)
+            flux = upwind(f1[i, h], left, ahead - half, jump)
+            total = change[h] + (flux - before) + row_divergence(here[h], f2[i, h])
+            fresh = here[h] - STEP_RATIO * total
+            if turn < NSUB - 1:
+                target[i, h] = fresh
+            else:
+                target[i - EDGE, :, h * 128 : h * 128 + 128] = fresh[8:40]
+            done.append((ahead + half, next_jump, flux))
+        return tuple(done)
+
+    lax.fori_loop(low, SLABS - low, step, tuple(begin))
+
+
+def early_kernel(
+    brick, velocity, vx_low, vx_high, vy_low, vy_high, rise, waited,
+    ta, f1, f2, f3,
+    vw, su, sf,
 ):
     for c in range(3):
         vw[c * PTS : c * PTS + 4, 8:24, :] = vx_low[c]
@@ -339,35 +376,12 @@
 
     lax.fori_loop(0, 21, first, 0)
 
-    for turn, (source, target) in enumerate(((brick, ta), (ta, tb), (tb, last))):
-        low = 2 + 2 * turn
-        begin = []
-        for h in range(2):
-            t0, t1, t2, t3 = (source[low - 2 + o, h] for o in range(4))
-            j0, j1, j2 = t1 - t0, t2 - t1, t3 - t2
-            h1, h2 = 0.5 * limited(j0, j1), 0.5 * limited(j1, j2)
-            begin.append((t2 + h2, j2, upwind(f1[low - 1, h], t1 + h1, t2 - h2, j1)))
-
-        def step(i, carry, source=source, target=target, turn=turn):
-            here = [source[i, h] for h in range(2)]
-            change = list(lane_divergence(*here, f3[i, 0], f3[i, 1]))
-            done = []
-            for h in range(2):
-                left, jump, before = carry[h]
-                ahead = source[i + 1, h]
-                next_jump = source[i + 2, h] - ahead
-                half = 0.5 * limited(jump, next_jump)
-                flux = upwind(f1[i, h], left, ahead - half, jump)
-                total = change[h] + (flux - before) + row_divergence(here[h], f2[i, h])
-                fresh = here[h] - STEP_RATIO * total
-                if turn < NSUB - 1:
-                    target[i, h] = fresh
-                else:
-                    target[i - EDGE, :, h * 128 : h * 128 + 128] = fresh[8:40]
-                done.append((ahead + half, next_jump, flux))
-            return tuple(done)
-
-        lax.fori_loop(low, SLABS - low, step, tuple(begin))
+    substep(brick, ta, 0, f1, f2, f3)
+
+
+def late_kernel(ta, f1, f2, f3, velocity, vorticity, join, th, tl, waited, advanced, out, tb, last, bs):
+    substep(ta, tb, 1, f1, f2, f3)
+    substep(tb, last, 2, f1, f2, f3)
 
     def finish(n, carry):
         lines = last[pl.ds(4 * n, 4)]
@@ -379,12 +393,14 @@
 
     lax.fori_loop(0, C1 // 2, finish, 0)
     buoyancy = bs[pl.ds(0, C1 * C2, stride=2), :] + bs[pl.ds(1, C1 * C2, stride=2), :]
-    force_lines(velocity, vorticity, buoyancy, th, tl, out)
+    u, w = flat_fields(velocity, vorticity)
+    send_lines([u[0] * w[1] - u[1] * w[0] + buoyancy], th, tl, out)
 
 
 def second_back_kernel(got, th, tl, out):
+    count = got.shape[1] // 64
     columns = []
-    for f in range(3):
+    for f in range(count):
         for h in range(2):
             parts = []
             for ri in range(2):
@@ -392,42 +408,62 @@
                 parts.append(got[:, at : at + 16, :].reshape(128, 128))
             columns.append(jnp.concatenate(parts, axis=0))
     z = dot3((th[...], tl[...]), split(jnp.concatenate(columns, axis=1)))
-    for f in range(3):
+    for f in range(count):
         for h in range(2):
             at = f * 16 + h * 8
             col = (f * 2 + h) * 128
             out[:, at : at + 8, :] = z[:, col : col + 128].reshape(GX, 8, 128)
 
 
-def first_back_kernel(got, th, tl, out, y):
-    rows = []
-    for f in range(3):
-        y[...] = got[:, 16 * f : 16 * f + 16, :].reshape(N1, 128)
-        w = swap_groups([y[pl.ds(g, N1 // 8, stride=8), :] for g in range(8)])
-        for i in range(8):
-            y[pl.ds(i, N1 // 8, stride=8), :] = w[i]
-        rows.append(y[...].T)
-    z = dot3(split(jnp.concatenate(rows, axis=0)), (th[...], tl[...]))
-    for f in range(3):
-        for r in range(Q2):
-            at = f * 128 + r * 32
-            cr, ci = z[at : at + 16, :N1], z[at + 16 : at + 32, :N1]
-            sr, si = z[at : at + 16, N1:], z[at + 16 : at + 32, N1:]
-            out[0, f, r] = cr + si
-            out[1, f, r] = ci - sr
-
-
-def call(kernel, out_shape, *args, scratch=(), late=0, hbm=False):
+def first_back_kernel(got, th, tl, *rest):
+    out, y = rest[-2:]
+    y[...] = got[...].reshape(N1, 128)
+    w = swap_groups([y[pl.ds(g, N1 // 8, stride=8), :] for g in range(8)])
+    for i in range(8):
+        y[pl.ds(i, N1 // 8, stride=8), :] = w[i]
+    z = dot3(split(y[...].T), (th[...], tl[...]))
+    for r in range(Q2):
+        at = r * 32
+        cr, ci = z[at : at + 16, :N1], z[at + 16 : at + 32, :N1]
+        sr, si = z[at : at + 16, N1:], z[at + 16 : at + 32, N1:]
+        out[0, 0, r] = cr + si
+        out[1, 0, r] = ci - sr
+
+
+def first_back(got, first, start, so_far=None):
+    count = got.shape[1] // 16
+    whole = pl.BlockSpec(memory_space=pltpu.VMEM)
+    args = [got, *first] + ([] if so_far is None else [so_far])
+    return pl.pallas_call(
+        first_back_kernel,
+        grid=(count,),
+        out_shape=shape(2, 3, Q2, Q3, N1),
+        in_specs=[pl.BlockSpec((GX, 16, 128), lambda f: (0, f, 0)), whole, whole]
+        + ([] if so_far is None else [pl.BlockSpec(memory_space=pl.ANY)]),
+        out_specs=pl.BlockSpec((2, 1, Q2, Q3, N1), lambda f: (0, f + start, 0, 0, 0)),
+        scratch_shapes=[pltpu.VMEM((N1, 128), F32)],
+        input_output_aliases={} if so_far is None else {3: 0},
+        interpret=INTERPRET,
+        name="first_back_kernel",
+        compiler_params=pltpu.CompilerParams(vmem_limit_bytes=48 * 1024 * 1024),
+    )(*args)
+
+
+def call(kernel, out_shape, *args, scratch=(), late=0, hbm=None):
     specs = [pl.BlockSpec(memory_space=pltpu.VMEM)] * (len(args) - late)
     specs += [pl.BlockSpec(memory_space=pl.ANY)] * late
+    single = not isinstance(out_shape, tuple)
+    outs = [out_shape] if single else list(out_shape)
+    if hbm is not None:
+        outs[int(hbm) if not single else 0] = pltpu.HBM(outs[-1].shape, outs[-1].dtype)
+    out_specs = [pl.BlockSpec(memory_space=pltpu.VMEM)] * len(outs)
     return pl.pallas_call(
         kernel,
         in_specs=specs,
-        out_shape=out_shape if not hbm else pltpu.HBM(out_shape.shape, out_shape.dtype),
-        out_specs=jax.tree.map(lambda _: pl.BlockSpec(memory_space=pltpu.VMEM), out_shape),
+        out_specs=out_specs[0] if single else out_specs,
+        out_shape=outs[0] if single else outs,
         scratch_shapes=list(scratch),
         interpret=INTERPRET,
-        name=kernel.__name__,
         compiler_params=pltpu.CompilerParams(vmem_limit_bytes=48 * 1024 * 1024),
     )(*args)
 
@@ -444,10 +480,15 @@
 
 def edges(axis, first, last):
     up, down = ring(axis)
-    return lax.ppermute(last, axis, up), lax.ppermute(first, axis, down)
-
-
-def body(spectrum, scalar):
+    low = lax.ppermute(last, axis, up)
+    return low, lax.ppermute(first, axis, down)
+
+
+def exchange(sent, axis):
+    return lax.all_to_all(sent, axis, split_axis=0, concat_axis=0, tiled=True)
+
+
+def step(spectrum, scalar):
     wave_first = np.tile(waves_np(N1).astype(np.float32), 2)[None]
     wave_second = np.repeat(waves_np(N2).astype(np.float32), 2)[:, None]
     blocks = np.tile(waves_np(N3).astype(np.float32).reshape(GY, 1, Q3), (1, 16, 1)).reshape(GY, 1, 256)
@@ -471,48 +512,53 @@
         first_kernel, shape(GX, 80, 128), spectrum, jnp.asarray(wave_first), *first,
         scratch=(pltpu.VMEM((5 * N1, 128), F32),),
     )
-    got = lax.all_to_all(sent, "px", split_axis=0, concat_axis=0, tiled=True)
+    got = exchange(sent, "px")
     sent = call(second_kernel, shape(GY, 384, 128), got, jnp.asarray(wave_second), wave_third, *second, x_low, x_high, late=2, hbm=True)
-    got = lax.all_to_all(sent, "py", split_axis=0, concat_axis=0, tiled=True)
+    got = exchange(sent, "py")
     velocity, vorticity = call(
         third_kernel, (shape(3, C1, C2, N3), shape(3, C1, C2, N3)), got, *third
     )
+    back3 = [jnp.asarray(t) for t in third_back()]
+    back2 = [jnp.asarray(t) for t in second_back()]
+    sent12 = call(force_kernel, shape(GY, 128, 128), velocity, vorticity, *back3, hbm=True)
     vx_low, vx_high = edges("px", velocity[:, :4], velocity[:, -4:])
     strips = [
         jnp.concatenate([part[:, :, cut] for part in (vx_low, velocity, vx_high)], axis=1)
         for cut in (slice(0, 4), slice(C2 - 4, C2))
     ]
     vy_low, vy_high = edges("py", *strips)
-    theta, sent = call(
-        scalar_kernel, (shape(2 * C1, 2 * C2, 2 * N3), shape(GY, 192, 128)),
-        brick, velocity, vx_low, vx_high, vy_low, vy_high, vorticity,
-        jnp.asarray(rise_tables()), join, *[jnp.asarray(t) for t in third_back()],
+    got12 = exchange(sent12, "py")
+    field = shape(SLABS, 2, ROWS, 128)
+    once, f1, f2, f3 = call(
+        early_kernel, (field, field, field, field),
+        brick, velocity, vx_low, vx_high, vy_low, vy_high, jnp.asarray(rise_tables()), sent12,
         scratch=(
-            pltpu.VMEM((SLABS, 2, ROWS, 128), F32),
-            pltpu.VMEM((SLABS, 2, ROWS, 128), F32),
-            pltpu.VMEM((2 * C1, 2 * C2, 256), F32),
             pltpu.VMEM((3 * PTS, PROWS, N3), F32),
             pltpu.VMEM((2 * 3 * PTS * PROWS, 128), F32),
             pltpu.VMEM((2 * 3 * PTS * ROWS, 128), F32),
+        ),
+        late=1,
+    )
+    sent12 = call(second_back_kernel, shape(GX, 32, 128), got12, *back2, hbm=True)
+    got12 = exchange(sent12, "px")
+    theta, sent3 = call(
+        late_kernel, (shape(2 * C1, 2 * C2, 2 * N3), shape(GY, 64, 128)),
+        once, f1, f2, f3, velocity, vorticity, join, *back3, sent12,
+        scratch=(
             pltpu.VMEM((SLABS, 2, ROWS, 128), F32),
-            pltpu.VMEM((SLABS, 2, ROWS, 128), F32),
-            pltpu.VMEM((SLABS, 2, ROWS, 128), F32),
+            pltpu.VMEM((2 * C1, 2 * C2, 256), F32),
             pltpu.VMEM((2 * C1 * C2, 128), F32),
         ),
+        late=1, hbm=1,
     )
-    got = lax.all_to_all(sent, "py", split_axis=0, concat_axis=0, tiled=True)
-    sent = call(
-        second_back_kernel, shape(GX, 48, 128), got, *[jnp.asarray(t) for t in second_back()]
-    )
-    got = lax.all_to_all(sent, "px", split_axis=0, concat_axis=0, tiled=True)
-    tendency = call(
-        first_back_kernel, shape(2, 3, Q2, Q3, N1), got, *first,
-        scratch=(pltpu.VMEM((N1, 128), F32),),
-    )
+    got3 = exchange(sent3, "py")
+    sent3 = call(second_back_kernel, shape(GX, 16, 128), got3, *back2, hbm=True)
+    got3 = exchange(sent3, "px")
+    tendency = first_back(got3, first, 2, first_back(got12, first, 0))
     return tendency, theta
 
 
 def solution(mesh):
     in_specs = (P(None, None, "px", "py", None), P("px", "py", None))
     out_specs = (P(None, None, "px", "py", None), P("px", "py", None))
-    return jax.shard_map(body, mesh=mesh, in_specs=in_specs, out_specs=out_specs, check_vma=False)
+    return jax.shard_map(step, mesh=mesh, in_specs=in_specs, out_specs=out_specs, check_vma=False)

time: 237 us -> 261 us (1.10)
  blocking collectives: 61.9 us -> 17 us
  waiting for transfers between devices: 78.7 us -> 108 us
  starting transfers between devices: 38.9 us -> 56.9 us
  Pallas kernels: 48.4 us -> 58.6 us
  local copies, waits for them, and re-layouts: 6.77 us -> 16.8 us
    all_to_all x2 -> x1, blocking collectives: 61.9 us -> 17 us  [exchange(): return lax.all_to_all(sent, axis, split_axis=0, concat_axis=0, tiled=True)]
    all_to_all x2 -> x5, waiting for transfers between devices: 49.5 us -> 73.4 us  [exchange(): return lax.all_to_all(sent, axis, split_axis=0, concat_axis=0, tiled=True)]
    all_to_all x2 -> x5, starting transfers between devices: 18.3 us -> 34.6 us  [exchange(): return lax.all_to_all(sent, axis, split_axis=0, concat_axis=0, tiled=True)]
    pallas_call x7 -> x11, Pallas kernels: 48.4 us -> 58.6 us  [the longest x9 54.4 us: call(): pl.pallas_call(kernel, in_specs=specs, out_specs=out_specs[0] if single e...]
    unnamed x38 -> x66, local copies, waits for them, and re-layouts: 5.17 us -> 15.2 us
    ppermute x8, waiting for transfers between devices: 29.2 us -> 34.9 us  [the longest x4 23.7 us: edges(): low = lax.ppermute(last, axis, up)]
  transfers between devices with their start and end apart: 10 -> 13, of which waited for: 7 -> 8; matrix products, arithmetic and copies ran while one was open for 1% -> 1% of each run, Pallas kernels for 3% -> 11%
where the time goes in v3:
time: 261 us; the launch traced here: 260 us
  waiting for transfers between devices  108 us (41%)
  Pallas kernels  58.6 us (22%)
  starting transfers between devices  56.9 us (22%)
  blocking collectives  17 us (7%)
  local copies, waits for them, and re-layouts  16.8 us (6%)
    all_to_all x5, waiting for transfers between devices, exchange(): return lax.all_to_all(sent, axis, split_axis=0, concat_axis=0, tiled=True)  73.4 us
    pallas_call x9, Pallas kernels, call(): pl.pallas_call(kernel, in_specs=specs, out_specs=out_specs[0] if single e...  54.4 us
    all_to_all x5, starting transfers between devices, exchange(): return lax.all_to_all(sent, axis, split_axis=0, concat_axis=0, tiled=True)  34.6 us
    ppermute x4, waiting for transfers between devices, edges(): low = lax.ppermute(last, axis, up)  23.7 us
    all_to_all x1, blocking collectives, exchange(): return lax.all_to_all(sent, axis, split_axis=0, concat_axis=0, tiled=True)  17 us
    unnamed x66, local copies, waits for them, and re-layouts  15.2 us
    ppermute x4, starting transfers between devices, edges(): low = lax.ppermute(last, axis, up)  14.1 us
    ppermute x4, waiting for transfers between devices, edges(): return (low, lax.ppermute(first, axis, down))  11.3 us
  transfers between devices with their start and end apart: 13, of which 8 were waited for; matrix products, arithmetic and copies ran while one was open for 1% of the time, Pallas kernels for 11%

profile of v3, /device:TPU:1, one launch (start us, length us, event | category | flops | bytes accessed | tf_op | source)
XLA Modules:
  0.0 259.7 jit_solution(17742369583706388924)
XLA Ops:
  0.6 1.2 copy-done
  1.9 1.2 copy-done.2
  3.1 1.1 copy-done.15
  4.2 0.7 copy-done.32
  4.9 4.4 %shard_map.186 = f32[32,80,128]{2,1,0:T(8,128)} custom-call(f32[2,3,4,16,512]{4,3,2,1,0:T(8,128)S(1)} %copy-done.15, f32[1,1024]{1,0:T(1,128)S(1)} %copy-done.32, bf16[512,1024]{1,0:T(8,128)(2,1)S(1)} %copy-done, bf16[512,1024]{1,0:T(8,128)(2,1)S(1)} %copy-done.2), custom_call_target="tpu_custom_call" | custom-call | tf_op jit(solution)/shard_map/pallas_call | solution.py:460
  9.3 10.3 %all-to-all-start = ((f32[32,80,128]{2,1,0:T(8,128)}), f32[32,80,128]{2,1,0:T(8,128)S(1)}, u32[]{:S(2)}, u32[]{:S(2)}) async-start(f32[32,80,128]{2,1,0:T(8,128)} %shard_map.186), calls=%async_computation | async-start | bytes 2621440 | tf_op jit(solution)/shard_map/all_to_all | solution.py:488
  19.7 0.8 fusion.5
  20.5 1.6 collective-permute-start
  22.1 0.7 dynamic-slice_bitcast_fusion.wave3
  22.8 22.6 %collective-permute-done.x_low = f32[6,32,256]{2,1,0:T(8,128)S(1)} collective-permute-done((f32[6,32,256]{2,1,0:T(8,128)}, f32[6,32,256]{2,1,0:T(8,128)S(1)}, u32[]{:S(2)}, u32[]{:S(2)}) %collective-permute-start) | collective-permute-done | bytes 196640 | tf_op jit(solution)/shard_map/ppermute | solution.py:483
  45.4 9.8 %all-to-all-done.got = f32[32,80,128]{2,1,0:T(8,128)S(1)} async-done(((f32[32,80,128]{2,1,0:T(8,128)}), f32[32,80,128]{2,1,0:T(8,128)S(1)}, u32[]{:S(2)}, u32[]{:S(2)}) %all-to-all-start) | async-done | bytes 1310752 | tf_op jit(solution)/shard_map/all_to_all | solution.py:488
  55.2 2.0 shard_map.187
  57.2 8.0 %all-to-all-start.1 = ((f32[8,384,128]{2,1,0:T(8,128)}), f32[8,384,128]{2,1,0:T(8,128)S(1)}, u32[]{:S(2)}, u32[]{:S(2)}) async-start(f32[8,384,128]{2,1,0:T(8,128)} %shard_map.187), calls=%async_computation.1 | async-start | bytes 3145728 | tf_op jit(solution)/shard_map/all_to_all | solution.py:488
  65.3 1.0 fusion.1
  66.3 5.4 %collective-permute-start.2 = (f32[108,2,256]{2,1,0:T(2,128)}, f32[108,2,256]{2,1,0:T(2,128)}, u32[]{:S(2)}, u32[]{:S(2)}) collective-permute-start(f32[108,2,256]{2,1,0:T(2,128)} %get-tuple-element.19), channel_id=1, source_target_pairs={{0,1},{1,2},{2,3},{3,4},{4,5},{5,6},{6,7},{7,0},{8,9},{9,10},{10,1... | collective-permute-start | bytes 663560 | tf_op jit(solution)/shard_map/ppermute | solution.py:483
  71.6 2.1 collective-permute-start.3
  73.7 39.2 %all-to-all-done.1.got = f32[8,384,128]{2,1,0:T(8,128)S(1)} async-done(((f32[8,384,128]{2,1,0:T(8,128)}), f32[8,384,128]{2,1,0:T(8,128)S(1)}, u32[]{:S(2)}, u32[]{:S(2)}) %all-to-all-start.1) | async-done | bytes 1572896 | tf_op jit(solution)/shard_map/all_to_all | solution.py:488
  113.0 0.8 copy-done.30
  113.8 0.8 copy-done.31
  114.7 3.0 %shard_map.188 = (f32[3,16,16,128]{3,2,1,0:T(8,128)S(1)}, f32[3,16,16,128]{3,2,1,0:T(8,128)S(1)}) custom-call(f32[8,384,128]{2,1,0:T(8,128)S(1)} %all-to-all-done.1.got, bf16[256,128]{1,0:T(8,128)(2,1)S(1)} %copy-done.30, bf16[256,128]{1,0:T(8,128)(2,1)S(1)} %copy-done.31), custom_call_target="tpu_custom_call" | custom-call | tf_op jit(solution)/shard_map/pallas_call | solution.py:460
  117.7 4.0 %collective-permute-start.4 = (f32[3,4,16,128]{3,2,1,0:T(8,128)S(1)}, f32[3,4,16,128]{3,2,1,0:T(8,128)S(1)}, u32[]{:S(2)}, u32[]{:S(2)}) collective-permute-start(f32[3,4,16,128]{3,2,1,0:T(8,128)S(1)} %get-tuple-element.27), channel_id=1, source_target_pairs={{0,8},{8,16},{16,24},{24,32},{32,40},{40,48},{48,56},{56,64},{64,7... | collective-permute-start | bytes 294920 | tf_op jit(solution)/shard_map/ppermute | solution.py:483
  121.7 1.6 shard_map.189.waited
  123.3 3.7 %all-to-all-start.2 = ((f32[8,128,128]{2,1,0:T(8,128)}), f32[8,128,128]{2,1,0:T(8,128)S(1)}, u32[]{:S(2)}, u32[]{:S(2)}) async-start(f32[8,128,128]{2,1,0:T(8,128)} %shard_map.189.waited), calls=%async_computation.2 | async-start | bytes 1048576 | tf_op jit(solution)/shard_map/all_to_all | solution.py:488
  127.0 0.3 collective-permute-start.5
  127.3 0.1 collective-permute-done.4.vx_low
  127.4 11.3 %collective-permute-done.5.vx_high = f32[3,4,16,128]{3,2,1,0:T(8,128)S(1)} collective-permute-done((f32[3,4,16,128]{3,2,1,0:T(8,128)S(1)}, f32[3,4,16,128]{3,2,1,0:T(8,128)S(1)}, u32[]{:S(2)}, u32[]{:S(2)}) %collective-permute-start.5) | collective-permute-done | bytes 98336 | tf_op jit(solution)/shard_map/ppermute | solution.py:484
  138.8 5.8 %collective-permute-start.7 = (f32[3,24,4,128]{3,2,1,0:T(4,128)S(1)}, f32[3,24,4,128]{3,2,1,0:T(4,128)S(1)}, u32[]{:S(2)}, u32[]{:S(2)}) collective-permute-start(f32[3,24,4,128]{3,2,1,0:T(4,128)S(1)} %pad_maximum_fusion.7), channel_id=1, source_target_pairs={{1,0},{2,1},{3,2},{4,3},{5,4},{6,5},{7,6},{0,7},{9,8},{10,9},{11,1... | collective-permute-start | bytes 442376 | tf_op jit(solution)/shard_map/ppermute | solution.py:484
  144.6 3.1 %collective-permute-start.6 = (f32[3,24,4,128]{3,2,1,0:T(4,128)S(1)}, f32[3,24,4,128]{3,2,1,0:T(4,128)S(1)}, u32[]{:S(2)}, u32[]{:S(2)}) collective-permute-start(f32[3,24,4,128]{3,2,1,0:T(4,128)S(1)} %pad_maximum_fusion.6), channel_id=1, source_target_pairs={{0,1},{1,2},{2,3},{3,4},{4,5},{5,6},{6,7},{7,0},{8,9},{9,10},{10,1... | collective-permute-start | bytes 442376 | tf_op jit(solution)/shard_map/ppermute | solution.py:483
  147.8 0.9 copy-done.28
  148.6 4.0 %shard_map.185.brick = f32[44,2,48,128]{3,2,1,0:T(8,128)S(1)} custom-call(f32[32,32,256]{2,1,0:T(8,128)S(1)} %copy-done.5, f32[6,32,256]{2,1,0:T(8,128)S(1)} %copy-done.12, f32[6,32,256]{2,1,0:T(8,128)S(1)} %copy-done.14, f32[108,2,256]{2,1,0:T(2,128)} %collective-permute-done.2.y_low, f32[108,2,256]{2,1,0:T(2,128)} %collective-permute-done.3.y_high, ...), custom_call_target="tpu_custom_call" | custom-call | tf_op jit(solution)/shard_map/pallas_call | solution.py:460
  152.6 1.4 copy-done.4
  154.0 0.9 collective-permute-done.6.vy_low
  154.9 0.9 copy-done.25
  155.8 16.9 %shard_map.190 = (f32[44,2,48,128]{3,2,1,0:T(8,128)S(1)}, f32[44,2,48,128]{3,2,1,0:T(8,128)S(1)}, f32[44,2,48,128]{3,2,1,0:T(8,128)}, f32[44,2,48,128]{3,2,1,0:T(8,128)}) custom-call(f32[44,2,48,128]{3,2,1,0:T(8,128)} %copy-done.4, f32[3,16,16,128]{3,2,1,0:T(8,128)S(1)} %get-tuple-element.10.velocity, f32[3,4,16,128]{3,2,1,0:T(8,128)S(1)} %copy-done.25, ...), custom_call_target="tpu_custom_call" | custom-call | tf_op jit(solution)/shard_map/pallas_call | solution.py:460
  172.7 1.4 copy-done.7
  174.1 1.4 copy-done.9
  175.5 1.2 shard_map.191.waited
  176.7 1.6 copy-done.8
  178.3 1.6 copy-done.10
  179.9 20.4 %shard_map.192 = (f32[32,32,256]{2,1,0:T(8,128)}, f32[8,64,128]{2,1,0:T(8,128)}) custom-call(f32[44,2,48,128]{3,2,1,0:T(8,128)S(1)} %copy-done.8, f32[44,2,48,128]{3,2,1,0:T(8,128)S(1)} %copy-done.10, f32[44,2,48,128]{3,2,1,0:T(8,128)} %get-tuple-element.14.f2, f32[44,2,48,128]{3,2,1,0:T(8,128)} %get-tuple-element.15.f3, ...), custom_call_target="tpu_custom_call" | custom-call | tf_op jit(solution)/shard_map/pallas_call | solution.py:460
  200.3 17.0 %all_to_all.30.got = f32[8,64,128]{2,1,0:T(8,128)S(1)} all-to-all(f32[8,64,128]{2,1,0:T(8,128)} %get-tuple-element.16), channel_id=1, replica_groups=mesh['px'=32,'py'=8] {'py'}, dimensions={0} | all-to-all | bytes 524288 | tf_op jit(solution)/shard_map/all_to_all | solution.py:488
  217.3 9.0 %all-to-all-start.5 = ((f32[32,32,128]{2,1,0:T(8,128)}), f32[32,32,128]{2,1,0:T(8,128)S(1)}, u32[]{:S(2)}, u32[]{:S(2)}) async-start(f32[32,32,128]{2,1,0:T(8,128)} %shard_map.191.waited), calls=%async_computation.5 | async-start | bytes 1048576 | tf_op jit(solution)/shard_map/all_to_all | solution.py:488
  226.3 1.0 shard_map.193
  227.3 15.8 %all-to-all-done.5.got = f32[32,32,128]{2,1,0:T(8,128)S(1)} async-done(((f32[32,32,128]{2,1,0:T(8,128)}), f32[32,32,128]{2,1,0:T(8,128)S(1)}, u32[]{:S(2)}, u32[]{:S(2)}) %all-to-all-start.5) | async-done | bytes 524320 | tf_op jit(solution)/shard_map/all_to_all | solution.py:488
  243.1 3.7 %all-to-all-start.4 = ((f32[32,16,128]{2,1,0:T(8,128)}), f32[32,16,128]{2,1,0:T(8,128)S(1)}, u32[]{:S(2)}, u32[]{:S(2)}) async-start(f32[32,16,128]{2,1,0:T(8,128)} %shard_map.193), calls=%async_computation.4 | async-start | bytes 524288 | tf_op jit(solution)/shard_map/all_to_all | solution.py:488
  246.8 2.6 %first_back_kernel.2.rest_0_ = f32[2,3,4,16,512]{4,3,2,1,0:T(8,128)} custom-call(f32[32,32,128]{2,1,0:T(8,128)S(1)} %all-to-all-done.5.got, bf16[512,1024]{1,0:T(8,128)(2,1)S(1)} %copy-done.1, bf16[512,1024]{1,0:T(8,128)(2,1)S(1)} %copy-done.3), custom_call_target="tpu_custom_call" | custom-call | tf_op jit(solution)/shard_map/first_back_kernel/pallas_call | solution.py:437
  249.5 8.6 %all-to-all-done.4.got = f32[32,16,128]{2,1,0:T(8,128)S(1)} async-done(((f32[32,16,128]{2,1,0:T(8,128)}), f32[32,16,128]{2,1,0:T(8,128)S(1)}, u32[]{:S(2)}, u32[]{:S(2)}) %all-to-all-start.4) | async-done | bytes 262176 | tf_op jit(solution)/shard_map/all_to_all | solution.py:488
  258.1 1.6 first_back_kernel.3
  (68 shorter events, 0.4 us)
Async XLA Ops:
  0.6 1.2 copy-start
  1.9 1.2 copy-start.2
  3.1 1.1 copy-start.15
  4.2 0.7 copy-start.32
  9.3 10.3 %copy-start.5 = (f32[32,32,256]{2,1,0:T(8,128)S(1)}, f32[32,32,256]{2,1,0:T(8,128)}, u32[]{:S(2)}) copy-start(f32[32,32,256]{2,1,0:T(8,128)} %scalar.1) | copy-start | bytes 3145732
  9.3 45.8 %copy-start.22 = (bf16[2,256,256]{2,1,0:T(8,128)(2,1)S(1)}, bf16[2,256,256]{2,1,0:T(8,128)(2,1)}, u32[]{:S(2)}) copy-start(bf16[2,256,256]{2,1,0:T(8,128)(2,1)} %constant.45.clone.th) | copy-start | bytes 786436
  9.3 45.8 %copy-start.23 = (bf16[2,256,256]{2,1,0:T(8,128)(2,1)S(1)}, bf16[2,256,256]{2,1,0:T(8,128)(2,1)}, u32[]{:S(2)}) copy-start(bf16[2,256,256]{2,1,0:T(8,128)(2,1)} %constant.46.clone.tl) | copy-start | bytes 786436
  9.3 45.8 %copy-start.29 = (f32[256,1]{1,0:T(8,128)S(1)}, f32[256,1]{1,0:T(8,128)}, u32[]{:S(2)}) copy-start(f32[256,1]{1,0:T(8,128)} %constant.52.clone.wave2) | copy-start | bytes 3076
  9.3 45.8 %all-to-all-start = ((f32[32,80,128]{2,1,0:T(8,128)}), f32[32,80,128]{2,1,0:T(8,128)S(1)}, u32[]{:S(2)}, u32[]{:S(2)}) async-start(f32[32,80,128]{2,1,0:T(8,128)} %shard_map.186), calls=%async_computation | async-start | bytes 2621440 | tf_op jit(solution)/shard_map/all_to_all | solution.py:488
  20.5 24.9 %collective-permute-start = (f32[6,32,256]{2,1,0:T(8,128)}, f32[6,32,256]{2,1,0:T(8,128)S(1)}, u32[]{:S(2)}, u32[]{:S(2)}) collective-permute-start(f32[6,32,256]{2,1,0:T(8,128)} %get-tuple-element.23), channel_id=1, source_target_pairs={{0,8},{8,16},{16,24},{24,32},{32,40},{40,48},{48,56},{56,64},{64,7... | collective-permute-start | bytes 589832 | tf_op jit(solution)/shard_map/ppermute | solution.py:483
  22.1 23.3 %collective-permute-start.1 = (f32[6,32,256]{2,1,0:T(8,128)}, f32[6,32,256]{2,1,0:T(8,128)S(1)}, u32[]{:S(2)}, u32[]{:S(2)}) collective-permute-start(f32[6,32,256]{2,1,0:T(8,128)} %get-tuple-element.22), channel_id=1, source_target_pairs={{8,0},{16,8},{24,16},{32,24},{40,32},{48,40},{56,48},{64,56},{72,6... | collective-permute-start | bytes 589832 | tf_op jit(solution)/shard_map/ppermute | solution.py:484
  45.4 19.8 %copy-start.11 = (f32[6,32,256]{2,1,0:T(8,128)}, f32[6,32,256]{2,1,0:T(8,128)S(1)}, u32[]{:S(2)}) copy-start(f32[6,32,256]{2,1,0:T(8,128)S(1)} %collective-permute-done.x_low) | copy-start | bytes 589828
  45.4 19.9 %copy-start.13 = (f32[6,32,256]{2,1,0:T(8,128)}, f32[6,32,256]{2,1,0:T(8,128)S(1)}, u32[]{:S(2)}) copy-start(f32[6,32,256]{2,1,0:T(8,128)S(1)} %collective-permute-done.1.x_high) | copy-start | bytes 589828
  57.2 55.8 %all-to-all-start.1 = ((f32[8,384,128]{2,1,0:T(8,128)}), f32[8,384,128]{2,1,0:T(8,128)S(1)}, u32[]{:S(2)}, u32[]{:S(2)}) async-start(f32[8,384,128]{2,1,0:T(8,128)} %shard_map.187), calls=%async_computation.1 | async-start | bytes 3145728 | tf_op jit(solution)/shard_map/all_to_all | solution.py:488
  65.3 56.5 %copy-start.18 = (bf16[128,256]{1,0:T(8,128)(2,1)S(1)}, bf16[128,256]{1,0:T(8,128)(2,1)}, u32[]{:S(2)}) copy-start(bf16[128,256]{1,0:T(8,128)(2,1)} %constant.53.clone.th) | copy-start | bytes 196612
  65.3 56.5 %copy-start.20 = (bf16[128,256]{1,0:T(8,128)(2,1)S(1)}, bf16[128,256]{1,0:T(8,128)(2,1)}, u32[]{:S(2)}) copy-start(bf16[128,256]{1,0:T(8,128)(2,1)} %constant.54.clone.tl) | copy-start | bytes 196612
  66.3 81.5 %collective-permute-start.2 = (f32[108,2,256]{2,1,0:T(2,128)}, f32[108,2,256]{2,1,0:T(2,128)}, u32[]{:S(2)}, u32[]{:S(2)}) collective-permute-start(f32[108,2,256]{2,1,0:T(2,128)} %get-tuple-element.19), channel_id=1, source_target_pairs={{0,1},{1,2},{2,3},{3,4},{4,5},{5,6},{6,7},{7,0},{8,9},{9,10},{10,1... | collective-permute-start | bytes 663560 | tf_op jit(solution)/shard_map/ppermute | solution.py:483
  71.6 76.1 %collective-permute-start.3 = (f32[108,2,256]{2,1,0:T(2,128)}, f32[108,2,256]{2,1,0:T(2,128)}, u32[]{:S(2)}, u32[]{:S(2)}) collective-permute-start(f32[108,2,256]{2,1,0:T(2,128)} %get-tuple-element.18), channel_id=1, source_target_pairs={{1,0},{2,1},{3,2},{4,3},{5,4},{6,5},{7,6},{0,7},{9,8},{10,9},{11,1... | collective-permute-start | bytes 663560 | tf_op jit(solution)/shard_map/ppermute | solution.py:484
  113.0 0.8 copy-start.30
  113.8 0.8 copy-start.31
  117.7 30.1 %copy-start.12 = (f32[6,32,256]{2,1,0:T(8,128)S(1)}, f32[6,32,256]{2,1,0:T(8,128)}, u32[]{:S(2)}) copy-start(f32[6,32,256]{2,1,0:T(8,128)} %copy-done.11) | copy-start | bytes 589828
  117.7 30.1 %copy-start.14 = (f32[6,32,256]{2,1,0:T(8,128)S(1)}, f32[6,32,256]{2,1,0:T(8,128)}, u32[]{:S(2)}) copy-start(f32[6,32,256]{2,1,0:T(8,128)} %copy-done.13) | copy-start | bytes 589828
  117.7 9.7 %collective-permute-start.4 = (f32[3,4,16,128]{3,2,1,0:T(8,128)S(1)}, f32[3,4,16,128]{3,2,1,0:T(8,128)S(1)}, u32[]{:S(2)}, u32[]{:S(2)}) collective-permute-start(f32[3,4,16,128]{3,2,1,0:T(8,128)S(1)} %get-tuple-element.27), channel_id=1, source_target_pairs={{0,8},{8,16},{16,24},{24,32},{32,40},{40,48},{48,56},{56,64},{64,7... | collective-permute-start | bytes 294920 | tf_op jit(solution)/shard_map/ppermute | solution.py:483
  123.3 52.2 %all-to-all-start.2 = ((f32[8,128,128]{2,1,0:T(8,128)}), f32[8,128,128]{2,1,0:T(8,128)S(1)}, u32[]{:S(2)}, u32[]{:S(2)}) async-start(f32[8,128,128]{2,1,0:T(8,128)} %shard_map.189.waited), calls=%async_computation.2 | async-start | bytes 1048576 | tf_op jit(solution)/shard_map/all_to_all | solution.py:488
  127.0 11.7 %collective-permute-start.5 = (f32[3,4,16,128]{3,2,1,0:T(8,128)S(1)}, f32[3,4,16,128]{3,2,1,0:T(8,128)S(1)}, u32[]{:S(2)}, u32[]{:S(2)}) collective-permute-start(f32[3,4,16,128]{3,2,1,0:T(8,128)S(1)} %get-tuple-element.26), channel_id=1, source_target_pairs={{8,0},{16,8},{24,16},{32,24},{40,32},{48,40},{56,48},{64,56},{72,6... | collective-permute-start | bytes 294920 | tf_op jit(solution)/shard_map/ppermute | solution.py:484
  127.4 20.3 %copy-start.24 = (f32[3,4,16,128]{3,2,1,0:T(8,128)}, f32[3,4,16,128]{3,2,1,0:T(8,128)S(1)}, u32[]{:S(2)}) copy-start(f32[3,4,16,128]{3,2,1,0:T(8,128)S(1)} %collective-permute-done.4.vx_low) | copy-start | bytes 294916
  138.8 15.2 %collective-permute-start.7 = (f32[3,24,4,128]{3,2,1,0:T(4,128)S(1)}, f32[3,24,4,128]{3,2,1,0:T(4,128)S(1)}, u32[]{:S(2)}, u32[]{:S(2)}) collective-permute-start(f32[3,24,4,128]{3,2,1,0:T(4,128)S(1)} %pad_maximum_fusion.7), channel_id=1, source_target_pairs={{1,0},{2,1},{3,2},{4,3},{5,4},{6,5},{7,6},{0,7},{9,8},{10,9},{11,1... | collective-permute-start | bytes 442376 | tf_op jit(solution)/shard_map/ppermute | solution.py:484
  144.6 10.4 %copy-start.6 = (f32[8,128,128]{2,1,0:T(8,128)S(1)}, f32[8,128,128]{2,1,0:T(8,128)}, u32[]{:S(2)}) copy-start(f32[8,128,128]{2,1,0:T(8,128)} %shard_map.189.waited) | copy-start | bytes 1572868
  144.6 10.4 %copy-start.27 = (bf16[2,128,256]{2,1,0:T(8,128)(2,1)S(1)}, bf16[2,128,256]{2,1,0:T(8,128)(2,1)}, u32[]{:S(2)}) copy-start(bf16[2,128,256]{2,1,0:T(8,128)(2,1)} %constant.57.clone.rise) | copy-start | bytes 393220
  144.6 10.3 %collective-permute-start.6 = (f32[3,24,4,128]{3,2,1,0:T(4,128)S(1)}, f32[3,24,4,128]{3,2,1,0:T(4,128)S(1)}, u32[]{:S(2)}, u32[]{:S(2)}) collective-permute-start(f32[3,24,4,128]{3,2,1,0:T(4,128)S(1)} %pad_maximum_fusion.6), channel_id=1, source_target_pairs={{0,1},{1,2},{2,3},{3,4},{4,5},{5,6},{6,7},{7,0},{8,9},{9,10},{10,1... | collective-permute-start | bytes 442376 | tf_op jit(solution)/shard_map/ppermute | solution.py:483
  147.7 0.9 copy-start.28
  152.6 1.4 copy-start.4
  154.0 21.5 %copy-start.16 = (bf16[256,256]{1,0:T(8,128)(2,1)S(1)}, bf16[256,256]{1,0:T(8,128)(2,1)}, u32[]{:S(2)}) copy-start(bf16[256,256]{1,0:T(8,128)(2,1)} %constant.55.clone.th) | copy-start | bytes 393220
  154.0 21.5 %copy-start.17 = (bf16[256,256]{1,0:T(8,128)(2,1)S(1)}, bf16[256,256]{1,0:T(8,128)(2,1)}, u32[]{:S(2)}) copy-start(bf16[256,256]{1,0:T(8,128)(2,1)} %constant.56.clone.tl) | copy-start | bytes 393220
  154.0 22.7 %copy-start.19 = (bf16[128,256]{1,0:T(8,128)(2,1)S(1)}, bf16[128,256]{1,0:T(8,128)(2,1)}, u32[]{:S(2)}) copy-start(bf16[128,256]{1,0:T(8,128)(2,1)} %constant.53.clone.th) | copy-start | bytes 196612
  154.0 22.7 %copy-start.21 = (bf16[128,256]{1,0:T(8,128)(2,1)S(1)}, bf16[128,256]{1,0:T(8,128)(2,1)}, u32[]{:S(2)}) copy-start(bf16[128,256]{1,0:T(8,128)(2,1)} %constant.54.clone.tl) | copy-start | bytes 196612
  154.9 0.9 copy-start.25
  155.8 20.8 %copy-start.26 = (bf16[256,256]{1,0:T(8,128)(2,1)S(1)}, bf16[256,256]{1,0:T(8,128)(2,1)}, u32[]{:S(2)}) copy-start(bf16[256,256]{1,0:T(8,128)(2,1)} %constant.50.clone.join) | copy-start | bytes 393220
  172.7 1.4 copy-start.7
  174.1 1.4 copy-start.9
  176.7 1.6 copy-start.8
  178.3 1.6 copy-start.10
  200.3 46.5 %copy-start.1 = (bf16[512,1024]{1,0:T(8,128)(2,1)S(1)}, bf16[512,1024]{1,0:T(8,128)(2,1)}, u32[]{:S(2)}) copy-start(bf16[512,1024]{1,0:T(8,128)(2,1)} %constant.43.clone.th) | copy-start | bytes 3145732
  200.3 46.6 %copy-start.3 = (bf16[512,1024]{1,0:T(8,128)(2,1)S(1)}, bf16[512,1024]{1,0:T(8,128)(2,1)}, u32[]{:S(2)}) copy-start(bf16[512,1024]{1,0:T(8,128)(2,1)} %constant.44.clone.tl) | copy-start | bytes 3145732
  217.3 25.8 %all-to-all-start.5 = ((f32[32,32,128]{2,1,0:T(8,128)}), f32[32,32,128]{2,1,0:T(8,128)S(1)}, u32[]{:S(2)}, u32[]{:S(2)}) async-start(f32[32,32,128]{2,1,0:T(8,128)} %shard_map.191.waited), calls=%async_computation.5 | async-start | bytes 1048576 | tf_op jit(solution)/shard_map/all_to_all | solution.py:488
  243.1 15.0 %all-to-all-start.4 = ((f32[32,16,128]{2,1,0:T(8,128)}), f32[32,16,128]{2,1,0:T(8,128)S(1)}, u32[]{:S(2)}, u32[]{:S(2)}) async-start(f32[32,16,128]{2,1,0:T(8,128)} %shard_map.193), calls=%async_computation.4 | async-start | bytes 524288 | tf_op jit(solution)/shard_map/all_to_all | solution.py:488

commit v4 on v2

--- a/solution.py
+++ b/solution.py
@@ -239,14 +239,20 @@
     return flux - pltpu.roll(flux, 1, 0)
 
 
-def lane_divergence(even, odd, face_even, face_odd):
+def lane_divergence(even, odd, face_even, face_odd, face_before):
+    even_before, odd_before = pltpu.roll(even, 1, 1), pltpu.roll(odd, 1, 1)
+    even_after, odd_after = pltpu.roll(even, N3 - 1, 1), pltpu.roll(odd, N3 - 1, 1)
     jump_even = odd - even
-    jump_odd = pltpu.roll(even, N3 - 1, 1) - odd
-    half_even = 0.5 * limited(even - pltpu.roll(odd, 1, 1), jump_even)
+    jump_odd = even_after - odd
+    jump_before = even - odd_before
+    half_even = 0.5 * limited(jump_before, jump_even)
     half_odd = 0.5 * limited(jump_even, jump_odd)
+    half_before = 0.5 * limited(odd_before - even_before, jump_before)
+    half_after = 0.5 * limited(jump_odd, odd_after - even_after)
     flux_even = upwind(face_even, even + half_even, odd - half_odd, jump_even)
-    flux_odd = upwind(face_odd, odd + half_odd, pltpu.roll(even - half_even, N3 - 1, 1), jump_odd)
-    return flux_even - pltpu.roll(flux_odd, 1, 1), flux_odd - flux_even
+    flux_odd = upwind(face_odd, odd + half_odd, even_after - half_after, jump_odd)
+    flux_before = upwind(face_before, odd_before + half_before, even - half_even, jump_before)
+    return flux_even - flux_before, flux_odd - flux_even
 
 
 EDGE = 6
@@ -335,6 +341,9 @@
                 else:
                     face[2 * k + 1, h] = odd
                     face[2 * k + 2, h] = cc
+                if c == 2 and h == 1:
+                    face[2 * k + 1, 2] = pltpu.roll(odd, 1, 1)
+                    face[2 * k + 2, 2] = pltpu.roll(cc, 1, 1)
         return carry
 
     lax.fori_loop(0, 21, first, 0)
@@ -350,7 +359,7 @@
 
         def step(i, carry, source=source, target=target, turn=turn):
             here = [source[i, h] for h in range(2)]
-            change = list(lane_divergence(*here, f3[i, 0], f3[i, 1]))
+            change = list(lane_divergence(*here, f3[i, 0], f3[i, 1], f3[i, 2]))
             done = []
             for h in range(2):
                 left, jump, before = carry[h]
@@ -496,7 +505,7 @@
             pltpu.VMEM((2 * 3 * PTS * ROWS, 128), F32),
             pltpu.VMEM((SLABS, 2, ROWS, 128), F32),
             pltpu.VMEM((SLABS, 2, ROWS, 128), F32),
-            pltpu.VMEM((SLABS, 2, ROWS, 128), F32),
+            pltpu.VMEM((SLABS, 3, ROWS, 128), F32),
             pltpu.VMEM((2 * C1 * C2, 128), F32),
         ),
     )

time: 237 us -> 228 us (0.962)
  Pallas kernels: 48.4 us -> 39 us
    pallas_call x7, Pallas kernels: 48.4 us -> 39 us  [call(): pl.pallas_call(kernel, in_specs=specs, out_shape=out_shape if not hbm els...]
where the time goes in v4:
time: 228 us; the launch traced here: 227 us
  waiting for transfers between devices  78.7 us (35%)
  blocking collectives  61.9 us (27%)
  Pallas kernels  39 us (17%)
  starting transfers between devices  38.9 us (17%)
  local copies, waits for them, and re-layouts  6.77 us (3%)
    all_to_all x1, waiting for transfers between devices, body(): got = lax.all_to_all(sent, 'py', split_axis=0, concat_axis=0, tiled=True)  39.7 us
    pallas_call x7, Pallas kernels, call(): pl.pallas_call(kernel, in_specs=specs, out_shape=out_shape if not hbm els...  39 us
    all_to_all x1, blocking collectives, body(): got = lax.all_to_all(sent, 'px', split_axis=0, concat_axis=0, tiled=True)  32 us
    all_to_all x1, blocking collectives, body(): got = lax.all_to_all(sent, 'py', split_axis=0, concat_axis=0, tiled=True)  29.9 us
    ppermute x8, waiting for transfers between devices, edges(): return (lax.ppermute(last, axis, up), lax.ppermute(first, axis, down))  29.2 us
    ppermute x8, starting transfers between devices, edges(): return (lax.ppermute(last, axis, up), lax.ppermute(first, axis, down))  20.6 us
    all_to_all x1, starting transfers between devices, body(): got = lax.all_to_all(sent, 'px', split_axis=0, concat_axis=0, tiled=True)  10.3 us
    all_to_all x1, waiting for transfers between devices, body(): got = lax.all_to_all(sent, 'px', split_axis=0, concat_axis=0, tiled=True)  9.78 us
  transfers between devices with their start and end apart: 10, of which 7 were waited for; matrix products, arithmetic and copies ran while one was open for 1% of the time, Pallas kernels for 3%

profile of v4, /device:TPU:1, one launch (start us, length us, event | category | flops | bytes accessed | tf_op | source)
XLA Modules:
  0.0 227.1 jit_solution(11157350464826199528)
XLA Ops:
  0.6 0.0 copy-start.1
  0.6 1.2 copy-done.1
  1.9 1.2 copy-done.3
  3.1 1.1 copy-done.5
  4.2 0.7 copy-done.18
  4.9 4.4 %first_kernel.1 = f32[32,80,128]{2,1,0:T(8,128)} custom-call(f32[2,3,4,16,512]{4,3,2,1,0:T(8,128)S(1)} %copy-done.5, f32[1,1024]{1,0:T(1,128)S(1)} %copy-done.18, bf16[512,1024]{1,0:T(8,128)(2,1)S(1)} %copy-done.3, bf16[512,1024]{1,0:T(8,128)(2,1)S(1)} %copy-done.1), custom_call_target="tpu_custom_call" | custom-call | tf_op jit(solution)/shard_map/first_kernel/pallas_call | solution.py:432
  9.3 10.3 %all-to-all-start = ((f32[32,80,128]{2,1,0:T(8,128)}), f32[32,80,128]{2,1,0:T(8,128)S(1)}, u32[]{:S(2)}, u32[]{:S(2)}) async-start(f32[32,80,128]{2,1,0:T(8,128)} %first_kernel.1), calls=%async_computation | async-start | bytes 2621440 | tf_op jit(solution)/shard_map/all_to_all | solution.py:483
  19.7 0.0 copy-done
  19.7 0.8 fusion.5
  20.4 0.2 collective-permute-start.1
  20.7 1.5 collective-permute-start
  22.2 0.7 dynamic-slice_bitcast_fusion.wave3
  22.9 14.9 %collective-permute-done.1.x_high = f32[6,32,256]{2,1,0:T(8,128)S(1)} collective-permute-done((f32[6,32,256]{2,1,0:T(8,128)}, f32[6,32,256]{2,1,0:T(8,128)S(1)}, u32[]{:S(2)}, u32[]{:S(2)}) %collective-permute-start.1) | collective-permute-done | bytes 196640 | tf_op jit(solution)/shard_map/ppermute | solution.py:456
  37.8 7.6 %collective-permute-done.x_low = f32[6,32,256]{2,1,0:T(8,128)S(1)} collective-permute-done((f32[6,32,256]{2,1,0:T(8,128)}, f32[6,32,256]{2,1,0:T(8,128)S(1)}, u32[]{:S(2)}, u32[]{:S(2)}) %collective-permute-start) | collective-permute-done | bytes 196640 | tf_op jit(solution)/shard_map/ppermute | solution.py:456
  45.4 9.8 %all-to-all-done.got = f32[32,80,128]{2,1,0:T(8,128)S(1)} async-done(((f32[32,80,128]{2,1,0:T(8,128)}), f32[32,80,128]{2,1,0:T(8,128)S(1)}, u32[]{:S(2)}, u32[]{:S(2)}) %all-to-all-start) | async-done | bytes 1310752 | tf_op jit(solution)/shard_map/all_to_all | solution.py:483
  55.1 0.0 copy-done.6
  55.1 0.0 copy-done.7
  55.1 2.1 second_kernel.1
  57.2 8.0 %all-to-all-start.1 = ((f32[8,384,128]{2,1,0:T(8,128)}), f32[8,384,128]{2,1,0:T(8,128)S(1)}, u32[]{:S(2)}, u32[]{:S(2)}) async-start(f32[8,384,128]{2,1,0:T(8,128)} %second_kernel.1), calls=%async_computation.1 | async-start | bytes 3145728 | tf_op jit(solution)/shard_map/all_to_all | solution.py:485
  65.2 0.1 fusion.4
  65.3 0.9 fusion.1
  66.2 7.5 %collective-permute-start.3 = (f32[108,2,256]{2,1,0:T(2,128)}, f32[108,2,256]{2,1,0:T(2,128)S(1)}, u32[]{:S(2)}, u32[]{:S(2)}) collective-permute-start(f32[108,2,256]{2,1,0:T(2,128)} %get-tuple-element.10), channel_id=1, source_target_pairs={{1,0},{2,1},{3,2},{4,3},{5,4},{6,5},{7,6},{0,7},{9,8},{10,9},{11,1... | collective-permute-start | bytes 663560 | tf_op jit(solution)/shard_map/ppermute | solution.py:456
  73.7 0.0 collective-permute-start.2
  73.7 39.7 %all-to-all-done.1.got = f32[8,384,128]{2,1,0:T(8,128)S(1)} async-done(((f32[8,384,128]{2,1,0:T(8,128)}), f32[8,384,128]{2,1,0:T(8,128)S(1)}, u32[]{:S(2)}, u32[]{:S(2)}) %all-to-all-start.1) | async-done | bytes 1572896 | tf_op jit(solution)/shard_map/all_to_all | solution.py:485
  113.4 0.8 copy-done.15
  114.2 3.0 %third_kernel.1 = (f32[3,16,16,128]{3,2,1,0:T(8,128)S(1)}, f32[3,16,16,128]{3,2,1,0:T(8,128)S(1)}) custom-call(f32[8,384,128]{2,1,0:T(8,128)S(1)} %all-to-all-done.1.got, bf16[256,128]{1,0:T(8,128)(2,1)S(1)} %copy-done.15, bf16[256,128]{1,0:T(8,128)(2,1)S(1)} %copy-done.14), custom_call_target="tpu_custom_call" | custom-call | tf_op jit(solution)/shard_map/third_kernel/pallas_call | solution.py:432
  117.2 2.5 %collective-permute-start.5 = (f32[3,4,16,128]{3,2,1,0:T(8,128)S(1)}, f32[3,4,16,128]{3,2,1,0:T(8,128)S(1)}, u32[]{:S(2)}, u32[]{:S(2)}) collective-permute-start(f32[3,4,16,128]{3,2,1,0:T(8,128)S(1)} %get-tuple-element.18), channel_id=1, source_target_pairs={{8,0},{16,8},{24,16},{32,24},{40,32},{48,40},{56,48},{64,56},{72,6... | collective-permute-start | bytes 294920 | tf_op jit(solution)/shard_map/ppermute | solution.py:456
  119.8 1.1 collective-permute-start.4
  120.9 2.5 %collective-permute-done.5.vx_high = f32[3,4,16,128]{3,2,1,0:T(8,128)S(1)} collective-permute-done((f32[3,4,16,128]{3,2,1,0:T(8,128)S(1)}, f32[3,4,16,128]{3,2,1,0:T(8,128)S(1)}, u32[]{:S(2)}, u32[]{:S(2)}) %collective-permute-start.5) | collective-permute-done | bytes 98336 | tf_op jit(solution)/shard_map/ppermute | solution.py:456
  123.3 0.0 collective-permute-done.4.vx_low
  123.4 4.3 %collective-permute-start.6 = (f32[3,24,4,128]{3,2,1,0:T(4,128)S(1)}, f32[3,24,4,128]{3,2,1,0:T(4,128)S(1)}, u32[]{:S(2)}, u32[]{:S(2)}) collective-permute-start(f32[3,24,4,128]{3,2,1,0:T(4,128)S(1)} %pad_maximum_fusion.6), channel_id=1, source_target_pairs={{0,1},{1,2},{2,3},{3,4},{4,5},{5,6},{6,7},{7,0},{8,9},{9,10},{10,1... | collective-permute-start | bytes 442376 | tf_op jit(solution)/shard_map/ppermute | solution.py:456
  127.7 0.0 copy-start.12
  127.7 0.0 copy-start.13
  127.8 0.0 copy-start.16
  127.8 0.0 copy-start.17
  127.8 3.5 %collective-permute-start.7 = (f32[3,24,4,128]{3,2,1,0:T(4,128)S(1)}, f32[3,24,4,128]{3,2,1,0:T(4,128)S(1)}, u32[]{:S(2)}, u32[]{:S(2)}) collective-permute-start(f32[3,24,4,128]{3,2,1,0:T(4,128)S(1)} %pad_maximum_fusion.7), channel_id=1, source_target_pairs={{1,0},{2,1},{3,2},{4,3},{5,4},{6,5},{7,6},{0,7},{9,8},{10,9},{11,1... | collective-permute-start | bytes 442376 | tf_op jit(solution)/shard_map/ppermute | solution.py:456
  131.3 0.0 collective-permute-done.3.y_high
  131.3 0.0 collective-permute-done.2.y_low
  131.3 2.9 %brick_kernel.1.brick = f32[44,2,48,128]{3,2,1,0:T(8,128)S(1)} custom-call(f32[32,32,256]{2,1,0:T(8,128)S(1)} %copy-done, f32[6,32,256]{2,1,0:T(8,128)S(1)} %collective-permute-done.x_low, f32[6,32,256]{2,1,0:T(8,128)S(1)} %collective-permute-done.1.x_high, f32[108,2,256]{2,1,0:T(2,128)S(1)} %collective-permute-done.2.y_low, ...), custom_call_target="tpu_custom_call" | custom-call | tf_op jit(solution)/shard_map/brick_kernel/pallas_call | solution.py:432
  134.3 1.1 collective-permute-done.6.vy_low
  135.3 3.2 %collective-permute-done.7.vy_high = f32[3,24,4,128]{3,2,1,0:T(4,128)S(1)} collective-permute-done((f32[3,24,4,128]{3,2,1,0:T(4,128)S(1)}, f32[3,24,4,128]{3,2,1,0:T(4,128)S(1)}, u32[]{:S(2)}, u32[]{:S(2)}) %collective-permute-start.7) | collective-permute-done | bytes 147488 | tf_op jit(solution)/shard_map/ppermute | solution.py:456
  138.5 0.0 copy-done.16
  138.5 22.8 %scalar_kernel.1 = (f32[32,32,256]{2,1,0:T(8,128)}, f32[8,192,128]{2,1,0:T(8,128)S(1)}) custom-call(f32[44,2,48,128]{3,2,1,0:T(8,128)S(1)} %brick_kernel.1.brick, f32[3,16,16,128]{3,2,1,0:T(8,128)S(1)} %get-tuple-element.6.velocity, f32[3,4,16,128]{3,2,1,0:T(8,128)S(1)} %collective-permute-done.4.vx_low, ...), custom_call_target="tpu_custom_call" | custom-call | tf_op jit(solution)/shard_map/scalar_kernel/pallas_call | solution.py:432
  161.4 29.9 %all_to_all.20.got = f32[8,192,128]{2,1,0:T(8,128)S(1)} all-to-all(f32[8,192,128]{2,1,0:T(8,128)S(1)} %get-tuple-element.8), channel_id=1, replica_groups=mesh['px'=32,'py'=8] {'py'}, dimensions={0} | all-to-all | bytes 1572864 | tf_op jit(solution)/shard_map/all_to_all | solution.py:512
  191.3 0.5 second_back_kernel.1
  191.8 32.0 %all_to_all.21.got = f32[32,48,128]{2,1,0:T(8,128)S(1)} all-to-all(f32[32,48,128]{2,1,0:T(8,128)S(1)} %second_back_kernel.1), channel_id=1, replica_groups=mesh['px'=32,'py'=8] {'px'}, dimensions={0} | all-to-all | bytes 1572864 | tf_op jit(solution)/shard_map/all_to_all | solution.py:516
  223.8 0.0 copy-done.4
  223.8 3.3 %first_back_kernel.1 = f32[2,3,4,16,512]{4,3,2,1,0:T(8,128)} custom-call(f32[32,48,128]{2,1,0:T(8,128)S(1)} %all_to_all.21.got, bf16[512,1024]{1,0:T(8,128)(2,1)S(1)} %copy-done.4, bf16[512,1024]{1,0:T(8,128)(2,1)S(1)} %copy-done.2), custom_call_target="tpu_custom_call" | custom-call | tf_op jit(solution)/shard_map/first_back_kernel/pallas_call | solution.py:432
  (31 shorter events, 0.2 us)
Async XLA Ops:
  0.6 1.2 copy-start.1
  1.9 1.2 copy-start.3
  3.1 1.1 copy-start.5
  4.2 0.7 copy-start.18
  9.3 10.3 %copy-start = (f32[32,32,256]{2,1,0:T(8,128)S(1)}, f32[32,32,256]{2,1,0:T(8,128)}, u32[]{:S(2)}) copy-start(f32[32,32,256]{2,1,0:T(8,128)} %scalar.1) | copy-start | bytes 3145732
  9.3 45.8 %copy-start.6 = (bf16[2,256,256]{2,1,0:T(8,128)(2,1)S(1)}, bf16[2,256,256]{2,1,0:T(8,128)(2,1)}, u32[]{:S(2)}) copy-start(bf16[2,256,256]{2,1,0:T(8,128)(2,1)} %constant.46.clone.tl) | copy-start | bytes 786436
  9.3 45.8 %copy-start.7 = (bf16[2,256,256]{2,1,0:T(8,128)(2,1)S(1)}, bf16[2,256,256]{2,1,0:T(8,128)(2,1)}, u32[]{:S(2)}) copy-start(bf16[2,256,256]{2,1,0:T(8,128)(2,1)} %constant.45.clone.th) | copy-start | bytes 786436
  9.3 45.8 %copy-start.11 = (f32[256,1]{1,0:T(8,128)S(1)}, f32[256,1]{1,0:T(8,128)}, u32[]{:S(2)}) copy-start(f32[256,1]{1,0:T(8,128)} %constant.52.clone.wave2) | copy-start | bytes 3076
  9.3 45.8 %all-to-all-start = ((f32[32,80,128]{2,1,0:T(8,128)}), f32[32,80,128]{2,1,0:T(8,128)S(1)}, u32[]{:S(2)}, u32[]{:S(2)}) async-start(f32[32,80,128]{2,1,0:T(8,128)} %first_kernel.1), calls=%async_computation | async-start | bytes 2621440 | tf_op jit(solution)/shard_map/all_to_all | solution.py:483
  20.4 17.3 %collective-permute-start.1 = (f32[6,32,256]{2,1,0:T(8,128)}, f32[6,32,256]{2,1,0:T(8,128)S(1)}, u32[]{:S(2)}, u32[]{:S(2)}) collective-permute-start(f32[6,32,256]{2,1,0:T(8,128)} %get-tuple-element.14), channel_id=1, source_target_pairs={{8,0},{16,8},{24,16},{32,24},{40,32},{48,40},{56,48},{64,56},{72,6... | collective-permute-start | bytes 589832 | tf_op jit(solution)/shard_map/ppermute | solution.py:456
  20.7 24.7 %collective-permute-start = (f32[6,32,256]{2,1,0:T(8,128)}, f32[6,32,256]{2,1,0:T(8,128)S(1)}, u32[]{:S(2)}, u32[]{:S(2)}) collective-permute-start(f32[6,32,256]{2,1,0:T(8,128)} %get-tuple-element.15), channel_id=1, source_target_pairs={{0,8},{8,16},{16,24},{24,32},{32,40},{40,48},{48,56},{56,64},{64,7... | collective-permute-start | bytes 589832 | tf_op jit(solution)/shard_map/ppermute | solution.py:456
  57.2 56.2 %all-to-all-start.1 = ((f32[8,384,128]{2,1,0:T(8,128)}), f32[8,384,128]{2,1,0:T(8,128)S(1)}, u32[]{:S(2)}, u32[]{:S(2)}) async-start(f32[8,384,128]{2,1,0:T(8,128)} %second_kernel.1), calls=%async_computation.1 | async-start | bytes 3145728 | tf_op jit(solution)/shard_map/all_to_all | solution.py:485
  65.2 48.2 %copy-start.14 = (bf16[256,128]{1,0:T(8,128)(2,1)S(1)}, bf16[256,128]{1,0:T(8,128)(2,1)}, u32[]{:S(2)}) copy-start(bf16[256,128]{1,0:T(8,128)(2,1)} %constant.48.clone.tl) | copy-start | bytes 196612
  66.2 65.1 %collective-permute-start.3 = (f32[108,2,256]{2,1,0:T(2,128)}, f32[108,2,256]{2,1,0:T(2,128)S(1)}, u32[]{:S(2)}, u32[]{:S(2)}) collective-permute-start(f32[108,2,256]{2,1,0:T(2,128)} %get-tuple-element.10), channel_id=1, source_target_pairs={{1,0},{2,1},{3,2},{4,3},{5,4},{6,5},{7,6},{0,7},{9,8},{10,9},{11,1... | collective-permute-start | bytes 663560 | tf_op jit(solution)/shard_map/ppermute | solution.py:456
  73.7 57.7 %collective-permute-start.2 = (f32[108,2,256]{2,1,0:T(2,128)}, f32[108,2,256]{2,1,0:T(2,128)S(1)}, u32[]{:S(2)}, u32[]{:S(2)}) collective-permute-start(f32[108,2,256]{2,1,0:T(2,128)} %get-tuple-element.11), channel_id=1, source_target_pairs={{0,1},{1,2},{2,3},{3,4},{4,5},{5,6},{6,7},{7,0},{8,9},{9,10},{10,1... | collective-permute-start | bytes 663560 | tf_op jit(solution)/shard_map/ppermute | solution.py:456
  113.4 0.8 copy-start.15
  114.2 17.1 %copy-start.10 = (bf16[256,256]{1,0:T(8,128)(2,1)S(1)}, bf16[256,256]{1,0:T(8,128)(2,1)}, u32[]{:S(2)}) copy-start(bf16[256,256]{1,0:T(8,128)(2,1)} %constant.49.clone.table) | copy-start | bytes 393220
  117.2 6.1 %collective-permute-start.5 = (f32[3,4,16,128]{3,2,1,0:T(8,128)S(1)}, f32[3,4,16,128]{3,2,1,0:T(8,128)S(1)}, u32[]{:S(2)}, u32[]{:S(2)}) collective-permute-start(f32[3,4,16,128]{3,2,1,0:T(8,128)S(1)} %get-tuple-element.18), channel_id=1, source_target_pairs={{8,0},{16,8},{24,16},{32,24},{40,32},{48,40},{56,48},{64,56},{72,6... | collective-permute-start | bytes 294920 | tf_op jit(solution)/shard_map/ppermute | solution.py:456
  119.8 3.6 %collective-permute-start.4 = (f32[3,4,16,128]{3,2,1,0:T(8,128)S(1)}, f32[3,4,16,128]{3,2,1,0:T(8,128)S(1)}, u32[]{:S(2)}, u32[]{:S(2)}) collective-permute-start(f32[3,4,16,128]{3,2,1,0:T(8,128)S(1)} %get-tuple-element.19), channel_id=1, source_target_pairs={{0,8},{8,16},{16,24},{24,32},{32,40},{40,48},{48,56},{56,64},{64,7... | collective-permute-start | bytes 294920 | tf_op jit(solution)/shard_map/ppermute | solution.py:456
  123.4 11.9 %collective-permute-start.6 = (f32[3,24,4,128]{3,2,1,0:T(4,128)S(1)}, f32[3,24,4,128]{3,2,1,0:T(4,128)S(1)}, u32[]{:S(2)}, u32[]{:S(2)}) collective-permute-start(f32[3,24,4,128]{3,2,1,0:T(4,128)S(1)} %pad_maximum_fusion.6), channel_id=1, source_target_pairs={{0,1},{1,2},{2,3},{3,4},{4,5},{5,6},{6,7},{7,0},{8,9},{9,10},{10,1... | collective-permute-start | bytes 442376 | tf_op jit(solution)/shard_map/ppermute | solution.py:456
  127.7 10.8 %copy-start.12 = (bf16[2,128,256]{2,1,0:T(8,128)(2,1)S(1)}, bf16[2,128,256]{2,1,0:T(8,128)(2,1)}, u32[]{:S(2)}) copy-start(bf16[2,128,256]{2,1,0:T(8,128)(2,1)} %constant.53.clone.rise) | copy-start | bytes 393220
  127.7 10.8 %copy-start.13 = (bf16[256,256]{1,0:T(8,128)(2,1)S(1)}, bf16[256,256]{1,0:T(8,128)(2,1)}, u32[]{:S(2)}) copy-start(bf16[256,256]{1,0:T(8,128)(2,1)} %constant.50.clone.join) | copy-start | bytes 393220
  127.8 10.8 %copy-start.16 = (bf16[128,256]{1,0:T(8,128)(2,1)S(1)}, bf16[128,256]{1,0:T(8,128)(2,1)}, u32[]{:S(2)}) copy-start(bf16[128,256]{1,0:T(8,128)(2,1)} %constant.55.clone.tl) | copy-start | bytes 196612
  127.8 10.8 %copy-start.17 = (bf16[128,256]{1,0:T(8,128)(2,1)S(1)}, bf16[128,256]{1,0:T(8,128)(2,1)}, u32[]{:S(2)}) copy-start(bf16[128,256]{1,0:T(8,128)(2,1)} %constant.54.clone.th) | copy-start | bytes 196612
  127.8 10.7 %collective-permute-start.7 = (f32[3,24,4,128]{3,2,1,0:T(4,128)S(1)}, f32[3,24,4,128]{3,2,1,0:T(4,128)S(1)}, u32[]{:S(2)}, u32[]{:S(2)}) collective-permute-start(f32[3,24,4,128]{3,2,1,0:T(4,128)S(1)} %pad_maximum_fusion.7), channel_id=1, source_target_pairs={{1,0},{2,1},{3,2},{4,3},{5,4},{6,5},{7,6},{0,7},{9,8},{10,9},{11,1... | collective-permute-start | bytes 442376 | tf_op jit(solution)/shard_map/ppermute | solution.py:456
  161.4 29.9 %copy-start.8 = (bf16[256,256]{1,0:T(8,128)(2,1)S(1)}, bf16[256,256]{1,0:T(8,128)(2,1)}, u32[]{:S(2)}) copy-start(bf16[256,256]{1,0:T(8,128)(2,1)} %constant.57.clone.tl) | copy-start | bytes 393220
  161.4 29.9 %copy-start.9 = (bf16[256,256]{1,0:T(8,128)(2,1)S(1)}, bf16[256,256]{1,0:T(8,128)(2,1)}, u32[]{:S(2)}) copy-start(bf16[256,256]{1,0:T(8,128)(2,1)} %constant.56.clone.th) | copy-start | bytes 393220
  191.3 32.5 %copy-start.2 = (bf16[512,1024]{1,0:T(8,128)(2,1)S(1)}, bf16[512,1024]{1,0:T(8,128)(2,1)}, u32[]{:S(2)}) copy-start(bf16[512,1024]{1,0:T(8,128)(2,1)} %constant.44.clone.tl) | copy-start | bytes 3145732
  191.3 32.5 %copy-start.4 = (bf16[512,1024]{1,0:T(8,128)(2,1)S(1)}, bf16[512,1024]{1,0:T(8,128)(2,1)}, u32[]{:S(2)}) copy-start(bf16[512,1024]{1,0:T(8,128)(2,1)} %constant.43.clone.th) | copy-start | bytes 3145732

commit v5 on v4

--- a/solution.py
+++ b/solution.py
@@ -39,42 +39,24 @@
 
 
 def first_table():
-    a = angles(N1)
-    return halves(np.concatenate([np.cos(a), np.sin(a)], axis=1))
+    a = angles(N1)[:, : N1 // 2]
+    rows = np.concatenate([a[0::2], a[1::2]], axis=0)
+    return halves(np.concatenate([np.cos(rows), np.sin(rows)], axis=1))
 
 
 def second_forward():
     a = angles(N2)
-    plain = np.zeros((2, N2, N2, 2))
-    plain[0, :, :, 0] = np.cos(a)
-    plain[0, :, :, 1] = -np.sin(a)
-    plain[1, :, :, 0] = np.sin(a)
-    plain[1, :, :, 1] = np.cos(a)
-    turned = np.zeros_like(plain)
-    turned[0] = -plain[1]
-    turned[1] = plain[0]
-    both = np.stack([plain, turned]).reshape(2, 2 * N2, 2 * N2)
-    return halves(both)
+    table = np.zeros((2, N2, N2, 2))
+    table[0, :, :, 0] = np.cos(a)
+    table[0, :, :, 1] = -np.sin(a)
+    table[1, :, :, 0] = np.sin(a)
+    table[1, :, :, 1] = np.cos(a)
+    return halves(table.reshape(2 * N2, 2 * N2))
 
 
 def third_forward():
     a = angles(N3)
     return halves(FACTOR * np.concatenate([np.cos(a), -np.sin(a)], axis=0))
-
-
-def third_back():
-    a = angles(N3)
-    return halves(FACTOR * np.concatenate([np.cos(a), -np.sin(a)], axis=1))
-
-
-def second_back():
-    a = angles(N2)
-    table = np.zeros((N2, 2, 2, N2))
-    table[:, 0, 0] = np.cos(a)
-    table[:, 0, 1] = np.sin(a)
-    table[:, 1, 0] = -np.sin(a)
-    table[:, 1, 1] = np.cos(a)
-    return halves(table.reshape(2 * N2, 2 * N2))
 
 
 def split(x):
@@ -111,24 +93,34 @@
     return v
 
 
+HALF = N1 // 2
+
+
+def point_row(i):
+    return HALF * (i % 2) + i // 2
+
+
 def first_kernel(spec, wave, th, tl, out, y):
-    rows = []
-    for f in (0, 1, 2, 1, 2):
+    even, odd = [], []
+    for n, f in enumerate((0, 1, 2, 1, 2)):
         plain, turned = [], []
         for r in range(Q2):
             re, im = spec[0, f, r], spec[1, f, r]
+            if n > 2:
+                re, im = re * wave[...], im * wave[...]
             plain += [re, im]
             turned += [-im, re]
-        piece = jnp.concatenate(
-            [jnp.concatenate(plain, axis=0), jnp.concatenate(turned, axis=0)], axis=1
-        )
-        rows.append(piece if len(rows) < 3 else piece * wave[...])
-    table = (th[...], tl[...])
-    z = dot3(table, split(jnp.concatenate(rows, axis=0)), ((1,), (1,)))
+        pieces = [jnp.concatenate(part, axis=0) for part in (plain, turned)]
+        even.append(jnp.concatenate([p[:, :HALF] + p[:, HALF:] for p in pieces], axis=1))
+        odd.append(jnp.concatenate([p[:, :HALF] - p[:, HALF:] for p in pieces], axis=1))
+    for n, rows in enumerate((even, odd)):
+        table = (th[HALF * n : HALF * n + HALF, :], tl[HALF * n : HALF * n + HALF, :])
+        z = dot3(table, split(jnp.concatenate(rows, axis=0)), ((1,), (1,)))
+        for f in range(5):
+            at = N1 * f + HALF * n
+            y[at : at + HALF, :] = z[:, 128 * f : 128 * f + 128]
     for f in range(5):
-        y[N1 * f : N1 * f + N1, :] = z[:, 128 * f : 128 * f + 128]
-    for f in range(5):
-        w = swap_groups([y[pl.ds(N1 * f + i, N1 // 8, stride=8), :] for i in range(8)])
+        w = swap_groups([y[pl.ds(N1 * f + point_row(i), N1 // 8, stride=4), :] for i in range(8)])
         for g in range(8):
             y[pl.ds(N1 * f + g, N1 // 8, stride=8), :] = w[g]
         out[:, 16 * f : 16 * f + 16, :] = y[N1 * f : N1 * f + N1, :].reshape(GX, 16, 128)
@@ -142,17 +134,14 @@
     k2 = wave2[...]
     k3 = wave3[...]
     curl = [k2 * c[2] - k3 * c[1], k3 * c[0] - c[4], c[3] - k2 * c[0]]
-    z = []
-    for group, fields in enumerate((c[:3], curl)):
-        data = split(jnp.concatenate(fields, axis=1))
-        z.append(dot3((th[group], tl[group]), data))
+    z = dot3((th[...], tl[...]), split(jnp.concatenate(c[:3] + curl, axis=1)))
     for f in range(6):
-        for ri in range(2):
+        real = z[:128, 256 * f : 256 * f + 256]
+        imag = z[128:, 256 * f : 256 * f + 256]
+        for ri, part in enumerate((real, imag) if f < 3 else (-imag, real)):
             for h in range(2):
                 at = ((f * 2 + ri) * 2 + h) * 16
-                col = (f % 3) * 256 + h * 128
-                piece = z[f // 3][ri * 128 : ri * 128 + 128, col : col + 128]
-                out[:, at : at + 16, :] = piece.reshape(GY, 16, 128)
+                out[:, at : at + 16, :] = part[:, h * 128 : h * 128 + 128].reshape(GY, 16, 128)
 
 
 def third_kernel(got, th, tl, velocity, vorticity):
@@ -174,7 +163,7 @@
     w = [vorticity[i].reshape(C1 * C2, N3) for i in range(3)]
     force = [u[1] * w[2] - u[2] * w[1], u[2] * w[0] - u[0] * w[2], u[0] * w[1] - u[1] * w[0] + b]
     for f in range(3):
-        lines = dot3(split(force[f]), (th[...], tl[...]))
+        lines = dot3(split(force[f]), (th[...], tl[...]), ((1,), (1,)))
         for ri in range(2):
             for h in range(2):
                 at = ((f * 2 + ri) * 2 + h) * 16
@@ -203,9 +192,8 @@
     return np.stack([parted(plain), parted(face)])
 
 
-def parity_tables():
-    part = parted(np.eye(2 * N3))
-    return part, np.ascontiguousarray(part.T)
+def parity_table():
+    return parted(np.eye(2 * N3))
 
 
 def three(x):
@@ -215,8 +203,8 @@
     return (rest - mid.astype(F32)).astype(BF), mid, high
 
 
-def permuted(x, table):
-    return dots([(part, table) for part in three(x)], ((1,), (0,)))
+def permuted(x, table, dims=((1,), (0,))):
+    return dots([(part, table) for part in three(x)], dims)
 
 
 def middle(a, b, c, d):
@@ -273,18 +261,18 @@
         raw[first : first + count, 40 + 2 * layer : 42 + 2 * layer, :] = y_high[at : at + count]
         at += count
 
-    def part(n, carry):
+    def sort(n, carry):
         z = permuted(raw[pl.ds(4 * n, 4)].reshape(4 * ROWS, 256), table[...])
         for h in range(2):
             brick[pl.ds(4 * n, 4), h] = z[:, h * 128 : h * 128 + 128].reshape(4, ROWS, 128)
         return carry
 
-    lax.fori_loop(0, SLABS // 4, part, 0)
+    lax.fori_loop(0, SLABS // 4, sort, 0)
 
 
 def scalar_kernel(
     brick, velocity, vx_low, vx_high, vy_low, vy_high, vorticity,
-    rise, join, th, tl,
+    rise, part, th, tl,
     advanced, out,
     ta, tb, last, vw, su, sf, f1, f2, f3, bs,
 ):
@@ -380,7 +368,7 @@
 
     def finish(n, carry):
         lines = last[pl.ds(4 * n, 4)]
-        advanced[pl.ds(4 * n, 4)] = permuted(lines.reshape(128, 256), join[...]).reshape(4, 32, 256)
+        advanced[pl.ds(4 * n, 4)] = permuted(lines.reshape(128, 256), part[...], ((1,), (1,))).reshape(4, 32, 256)
         both = lines[:, :, :128] + lines[:, :, 128:]
         bs[pl.ds(pl.multiple_of(64 * n, 8), 32), :] = 0.125 * (both[0] + both[1])
         bs[pl.ds(pl.multiple_of(64 * n + 32, 8), 32), :] = 0.125 * (both[2] + both[3])
@@ -400,7 +388,7 @@
                 at = ((f * 2 + ri) * 2 + h) * 16
                 parts.append(got[:, at : at + 16, :].reshape(128, 128))
             columns.append(jnp.concatenate(parts, axis=0))
-    z = dot3((th[...], tl[...]), split(jnp.concatenate(columns, axis=1)))
+    z = dot3((th[...], tl[...]), split(jnp.concatenate(columns, axis=1)), ((0,), (0,)))
     for f in range(3):
         for h in range(2):
             at = f * 16 + h * 8
@@ -409,21 +397,25 @@
 
 
 def first_back_kernel(got, th, tl, out, y):
-    rows = []
+    rows = ([], [])
     for f in range(3):
         y[...] = got[:, 16 * f : 16 * f + 16, :].reshape(N1, 128)
         w = swap_groups([y[pl.ds(g, N1 // 8, stride=8), :] for g in range(8)])
         for i in range(8):
-            y[pl.ds(i, N1 // 8, stride=8), :] = w[i]
-        rows.append(y[...].T)
-    z = dot3(split(jnp.concatenate(rows, axis=0)), (th[...], tl[...]))
+            y[pl.ds(point_row(i), N1 // 8, stride=4), :] = w[i]
+        for n in range(2):
+            rows[n].append(y[HALF * n : HALF * n + HALF, :].T)
+    z = []
+    for n in range(2):
+        table = (th[HALF * n : HALF * n + HALF, :], tl[HALF * n : HALF * n + HALF, :])
+        z.append(dot3(split(jnp.concatenate(rows[n], axis=0)), table))
     for f in range(3):
         for r in range(Q2):
             at = f * 128 + r * 32
-            cr, ci = z[at : at + 16, :N1], z[at + 16 : at + 32, :N1]
-            sr, si = z[at : at + 16, N1:], z[at + 16 : at + 32, N1:]
-            out[0, f, r] = cr + si
-            out[1, f, r] = ci - sr
+            real = [p[at : at + 16, :HALF] + p[at + 16 : at + 32, HALF:] for p in z]
+            imag = [p[at + 16 : at + 32, :HALF] - p[at : at + 16, HALF:] for p in z]
+            for ri, (e, o) in enumerate((real, imag)):
+                out[ri, f, r] = jnp.concatenate([e + o, e - o], axis=1)
 
 
 def call(kernel, out_shape, *args, scratch=(), late=0, hbm=False):
@@ -457,7 +449,7 @@
 
 
 def body(spectrum, scalar):
-    wave_first = np.tile(waves_np(N1).astype(np.float32), 2)[None]
+    wave_first = waves_np(N1).astype(np.float32)[None]
     wave_second = np.repeat(waves_np(N2).astype(np.float32), 2)[:, None]
     blocks = np.tile(waves_np(N3).astype(np.float32).reshape(GY, 1, Q3), (1, 16, 1)).reshape(GY, 1, 256)
     wave_third = lax.dynamic_index_in_dim(jnp.asarray(blocks), lax.axis_index("py"), 0, keepdims=False)
@@ -471,7 +463,7 @@
         for starts in ((0, 2, 4), (2 * C2 - 2, 2 * C2 - 4, 2 * C2 - 6))
     ]
     y_low, y_high = edges("py", *strips)
-    part, join = (jnp.asarray(t) for t in parity_tables())
+    part = jnp.asarray(parity_table())
     brick = call(
         brick_kernel, shape(SLABS, 2, ROWS, 128), scalar, x_low, x_high, y_low, y_high, part,
         scratch=(pltpu.VMEM((SLABS, ROWS, 256), F32),),
@@ -495,7 +487,7 @@
     theta, sent = call(
         scalar_kernel, (shape(2 * C1, 2 * C2, 2 * N3), shape(GY, 192, 128)),
         brick, velocity, vx_low, vx_high, vy_low, vy_high, vorticity,
-        jnp.asarray(rise_tables()), join, *[jnp.asarray(t) for t in third_back()],
+        jnp.asarray(rise_tables()), part, *third,
         scratch=(
             pltpu.VMEM((SLABS, 2, ROWS, 128), F32),
             pltpu.VMEM((SLABS, 2, ROWS, 128), F32),
@@ -511,7 +503,7 @@
     )
     got = lax.all_to_all(sent, "py", split_axis=0, concat_axis=0, tiled=True)
     sent = call(
-        second_back_kernel, shape(GX, 48, 128), got, *[jnp.asarray(t) for t in second_back()]
+        second_back_kernel, shape(GX, 48, 128), got, *second
     )
     got = lax.all_to_all(sent, "px", split_axis=0, concat_axis=0, tiled=True)
     tendency = call(

time: 228 us -> 226 us (level)
    all_to_all x1, blocking collectives: 29.9 us -> 32.8 us  [body(): got = lax.all_to_all(sent, 'py', split_axis=0, concat_axis=0, tiled=True)]
    unnamed x38 -> x30, local copies, waits for them, and re-layouts: 5.17 us -> 5.01 us
where the time goes in v5:
time: 226 us; the launch traced here: 225 us
  waiting for transfers between devices  76.7 us (34%)
  blocking collectives  63.7 us (28%)
  starting transfers between devices  38.9 us (17%)
  Pallas kernels  37.8 us (17%)
  local copies, waits for them, and re-layouts  6.55 us (3%)
    all_to_all x1, waiting for transfers between devices, body(): got = lax.all_to_all(sent, 'py', split_axis=0, concat_axis=0, tiled=True)  39.7 us
    pallas_call x7, Pallas kernels, call(): pl.pallas_call(kernel, in_specs=specs, out_shape=out_shape if not hbm els...  37.8 us
    all_to_all x1, blocking collectives, body(): got = lax.all_to_all(sent, 'py', split_axis=0, concat_axis=0, tiled=True)  32.8 us
    all_to_all x1, blocking collectives, body(): got = lax.all_to_all(sent, 'px', split_axis=0, concat_axis=0, tiled=True)  30.8 us
    ppermute x8, waiting for transfers between devices, edges(): return (lax.ppermute(last, axis, up), lax.ppermute(first, axis, down))  27.1 us
    ppermute x8, starting transfers between devices, edges(): return (lax.ppermute(last, axis, up), lax.ppermute(first, axis, down))  20.7 us
    all_to_all x1, starting transfers between devices, body(): got = lax.all_to_all(sent, 'px', split_axis=0, concat_axis=0, tiled=True)  10.3 us
    all_to_all x1, waiting for transfers between devices, body(): got = lax.all_to_all(sent, 'px', split_axis=0, concat_axis=0, tiled=True)  9.88 us
  transfers between devices with their start and end apart: 10, of which 7 were waited for; matrix products, arithmetic and copies ran while one was open for 1% of the time, Pallas kernels for 3%

profile of v5, /device:TPU:1, one launch (start us, length us, event | category | flops | bytes accessed | tf_op | source)
XLA Modules:
  0.0 225.4 jit_solution(16166470316939614096)
XLA Ops:
  0.6 0.0 copy-start.2
  0.6 1.0 copy-done.2
  1.7 1.0 copy-done.4
  2.7 1.1 copy-done.6
  3.9 0.7 copy-done.14
  4.5 2.3 %first_kernel.1 = f32[32,80,128]{2,1,0:T(8,128)S(1)} custom-call(f32[2,3,4,16,512]{4,3,2,1,0:T(8,128)S(1)} %copy-done.6, f32[1,512]{1,0:T(1,128)S(1)} %copy-done.14, bf16[512,512]{1,0:T(8,128)(2,1)S(1)} %copy-done.4, bf16[512,512]{1,0:T(8,128)(2,1)S(1)} %copy-done.2), custom_call_target="tpu_custom_call" | custom-call | tf_op jit(solution)/shard_map/first_kernel/pallas_call | solution.py:424
  6.8 0.0 copy-start.1
  6.8 1.1 copy-done.1
  7.9 10.3 %all-to-all-start = ((f32[32,80,128]{2,1,0:T(8,128)}), f32[32,80,128]{2,1,0:T(8,128)S(1)}, u32[]{:S(2)}, u32[]{:S(2)}) async-start(f32[32,80,128]{2,1,0:T(8,128)} %copy-done.1), calls=%async_computation | async-start | bytes 2621440 | tf_op jit(solution)/shard_map/all_to_all | solution.py:475
  18.2 0.0 copy-done
  18.2 0.7 fusion.5
  18.9 0.2 collective-permute-start.1
  19.2 1.5 collective-permute-start
  20.7 0.7 dynamic-slice_bitcast_fusion.wave3
  21.4 15.0 %collective-permute-done.1.x_high = f32[6,32,256]{2,1,0:T(8,128)S(1)} collective-permute-done((f32[6,32,256]{2,1,0:T(8,128)}, f32[6,32,256]{2,1,0:T(8,128)S(1)}, u32[]{:S(2)}, u32[]{:S(2)}) %collective-permute-start.1) | collective-permute-done | bytes 196640 | tf_op jit(solution)/shard_map/ppermute | solution.py:448
  36.3 7.5 %collective-permute-done.x_low = f32[6,32,256]{2,1,0:T(8,128)S(1)} collective-permute-done((f32[6,32,256]{2,1,0:T(8,128)S(1)}, f32[6,32,256]{2,1,0:T(8,128)S(1)}, u32[]{:S(2)}, u32[]{:S(2)}) %collective-permute-start) | collective-permute-done | bytes 196640 | tf_op jit(solution)/shard_map/ppermute | solution.py:448
  43.8 9.9 %all-to-all-done.got = f32[32,80,128]{2,1,0:T(8,128)S(1)} async-done(((f32[32,80,128]{2,1,0:T(8,128)}), f32[32,80,128]{2,1,0:T(8,128)S(1)}, u32[]{:S(2)}, u32[]{:S(2)}) %all-to-all-start) | async-done | bytes 1310752 | tf_op jit(solution)/shard_map/all_to_all | solution.py:475
  53.7 0.0 copy-done.7
  53.7 0.0 copy-done.8
  53.7 0.0 copy-done.12
  53.7 2.0 second_kernel.1
  55.7 7.9 %all-to-all-start.1 = ((f32[8,384,128]{2,1,0:T(8,128)}), f32[8,384,128]{2,1,0:T(8,128)S(1)}, u32[]{:S(2)}, u32[]{:S(2)}) async-start(f32[8,384,128]{2,1,0:T(8,128)} %second_kernel.1), calls=%async_computation.1 | async-start | bytes 3145728 | tf_op jit(solution)/shard_map/all_to_all | solution.py:477
  63.7 0.0 copy-start.11
  63.7 0.1 fusion.4
  63.8 0.9 fusion.1
  64.7 7.5 %collective-permute-start.3 = (f32[108,2,256]{2,1,0:T(2,128)}, f32[108,2,256]{2,1,0:T(2,128)}, u32[]{:S(2)}, u32[]{:S(2)}) collective-permute-start(f32[108,2,256]{2,1,0:T(2,128)} %get-tuple-element.10), channel_id=1, source_target_pairs={{1,0},{2,1},{3,2},{4,3},{5,4},{6,5},{7,6},{0,7},{9,8},{10,9},{11,1... | collective-permute-start | bytes 663560 | tf_op jit(solution)/shard_map/ppermute | solution.py:448
  72.2 0.0 collective-permute-start.2
  72.2 39.7 %all-to-all-done.1.got = f32[8,384,128]{2,1,0:T(8,128)S(1)} async-done(((f32[8,384,128]{2,1,0:T(8,128)}), f32[8,384,128]{2,1,0:T(8,128)S(1)}, u32[]{:S(2)}, u32[]{:S(2)}) %all-to-all-start.1) | async-done | bytes 1572896 | tf_op jit(solution)/shard_map/all_to_all | solution.py:477
  111.9 0.0 copy-done.10
  111.9 3.0 %third_kernel.1 = (f32[3,16,16,128]{3,2,1,0:T(8,128)S(1)}, f32[3,16,16,128]{3,2,1,0:T(8,128)S(1)}) custom-call(f32[8,384,128]{2,1,0:T(8,128)S(1)} %all-to-all-done.1.got, bf16[256,128]{1,0:T(8,128)(2,1)S(1)} %copy-done.11, bf16[256,128]{1,0:T(8,128)(2,1)S(1)} %copy-done.10), custom_call_target="tpu_custom_call" | custom-call | tf_op jit(solution)/shard_map/third_kernel/pallas_call | solution.py:424
  114.9 2.5 %collective-permute-start.5 = (f32[3,4,16,128]{3,2,1,0:T(8,128)S(1)}, f32[3,4,16,128]{3,2,1,0:T(8,128)S(1)}, u32[]{:S(2)}, u32[]{:S(2)}) collective-permute-start(f32[3,4,16,128]{3,2,1,0:T(8,128)S(1)} %get-tuple-element.18), channel_id=1, source_target_pairs={{8,0},{16,8},{24,16},{32,24},{40,32},{48,40},{56,48},{64,56},{72,6... | collective-permute-start | bytes 294920 | tf_op jit(solution)/shard_map/ppermute | solution.py:448
  117.5 1.1 collective-permute-start.4
  118.6 2.6 %collective-permute-done.5.vx_high = f32[3,4,16,128]{3,2,1,0:T(8,128)S(1)} collective-permute-done((f32[3,4,16,128]{3,2,1,0:T(8,128)S(1)}, f32[3,4,16,128]{3,2,1,0:T(8,128)S(1)}, u32[]{:S(2)}, u32[]{:S(2)}) %collective-permute-start.5) | collective-permute-done | bytes 98336 | tf_op jit(solution)/shard_map/ppermute | solution.py:448
  121.2 0.0 collective-permute-done.4.vx_low
  121.3 4.8 %collective-permute-start.6 = (f32[3,24,4,128]{3,2,1,0:T(4,128)S(1)}, f32[3,24,4,128]{3,2,1,0:T(4,128)S(1)}, u32[]{:S(2)}, u32[]{:S(2)}) collective-permute-start(f32[3,24,4,128]{3,2,1,0:T(4,128)S(1)} %pad_maximum_fusion.6), channel_id=1, source_target_pairs={{0,1},{1,2},{2,3},{3,4},{4,5},{5,6},{6,7},{7,0},{8,9},{9,10},{10,1... | collective-permute-start | bytes 442376 | tf_op jit(solution)/shard_map/ppermute | solution.py:448
  126.1 0.0 copy-start.13
  126.1 3.1 %collective-permute-start.7 = (f32[3,24,4,128]{3,2,1,0:T(4,128)S(1)}, f32[3,24,4,128]{3,2,1,0:T(4,128)S(1)}, u32[]{:S(2)}, u32[]{:S(2)}) collective-permute-start(f32[3,24,4,128]{3,2,1,0:T(4,128)S(1)} %pad_maximum_fusion.7), channel_id=1, source_target_pairs={{1,0},{2,1},{3,2},{4,3},{5,4},{6,5},{7,6},{0,7},{9,8},{10,9},{11,1... | collective-permute-start | bytes 442376 | tf_op jit(solution)/shard_map/ppermute | solution.py:448
  129.1 0.0 collective-permute-done.3.y_high
  129.1 0.0 collective-permute-done.2.y_low
  129.1 4.0 %brick_kernel.1.brick = f32[44,2,48,128]{3,2,1,0:T(8,128)S(1)} custom-call(f32[32,32,256]{2,1,0:T(8,128)S(1)} %copy-done, f32[6,32,256]{2,1,0:T(8,128)S(1)} %collective-permute-done.x_low, f32[6,32,256]{2,1,0:T(8,128)S(1)} %collective-permute-done.1.x_high, f32[108,2,256]{2,1,0:T(2,128)} %collective-permute-done.2.y_low, ...), custom_call_target="tpu_custom_call" | custom-call | tf_op jit(solution)/shard_map/brick_kernel/pallas_call | solution.py:424
  133.1 1.7 collective-permute-done.6.vy_low
  134.8 0.4 collective-permute-done.7.vy_high
  135.2 23.4 %scalar_kernel.1 = (f32[32,32,256]{2,1,0:T(8,128)}, f32[8,192,128]{2,1,0:T(8,128)S(1)}) custom-call(f32[44,2,48,128]{3,2,1,0:T(8,128)S(1)} %brick_kernel.1.brick, f32[3,16,16,128]{3,2,1,0:T(8,128)S(1)} %get-tuple-element.6.velocity, f32[3,4,16,128]{3,2,1,0:T(8,128)S(1)} %collective-permute-done.4.vx_low, ...), custom_call_target="tpu_custom_call" | custom-call | tf_op jit(solution)/shard_map/scalar_kernel/pallas_call | solution.py:424
  158.5 32.8 %all_to_all.20.got = f32[8,192,128]{2,1,0:T(8,128)S(1)} all-to-all(f32[8,192,128]{2,1,0:T(8,128)S(1)} %get-tuple-element.8), channel_id=1, replica_groups=mesh['px'=32,'py'=8] {'py'}, dimensions={0} | all-to-all | bytes 1572864 | tf_op jit(solution)/shard_map/all_to_all | solution.py:504
  191.4 0.5 second_back_kernel.1
  191.9 30.8 %all_to_all.21.got = f32[32,48,128]{2,1,0:T(8,128)S(1)} all-to-all(f32[32,48,128]{2,1,0:T(8,128)S(1)} %second_back_kernel.1), channel_id=1, replica_groups=mesh['px'=32,'py'=8] {'px'}, dimensions={0} | all-to-all | bytes 1572864 | tf_op jit(solution)/shard_map/all_to_all | solution.py:508
  222.7 0.0 copy-done.3
  222.7 2.6 %first_back_kernel.1 = f32[2,3,4,16,512]{4,3,2,1,0:T(8,128)} custom-call(f32[32,48,128]{2,1,0:T(8,128)S(1)} %all_to_all.21.got, bf16[512,512]{1,0:T(8,128)(2,1)S(1)} %copy-done.5, bf16[512,512]{1,0:T(8,128)(2,1)S(1)} %copy-done.3), custom_call_target="tpu_custom_call" | custom-call | tf_op jit(solution)/shard_map/first_back_kernel/pallas_call | solution.py:424
  (23 shorter events, 0.2 us)
Async XLA Ops:
  0.6 1.0 copy-start.2
  1.7 1.0 copy-start.4
  2.7 1.1 copy-start.6
  3.9 0.7 copy-start.14
  6.8 1.1 copy-start.1
  7.9 10.3 %copy-start = (f32[32,32,256]{2,1,0:T(8,128)S(1)}, f32[32,32,256]{2,1,0:T(8,128)}, u32[]{:S(2)}) copy-start(f32[32,32,256]{2,1,0:T(8,128)} %scalar.1) | copy-start | bytes 3145732
  7.9 45.8 %copy-start.7 = (bf16[256,256]{1,0:T(8,128)(2,1)S(1)}, bf16[256,256]{1,0:T(8,128)(2,1)}, u32[]{:S(2)}) copy-start(bf16[256,256]{1,0:T(8,128)(2,1)} %constant.36.clone.tl) | copy-start | bytes 393220
  7.9 45.8 %copy-start.8 = (bf16[256,256]{1,0:T(8,128)(2,1)S(1)}, bf16[256,256]{1,0:T(8,128)(2,1)}, u32[]{:S(2)}) copy-start(bf16[256,256]{1,0:T(8,128)(2,1)} %constant.35.clone.th) | copy-start | bytes 393220
  7.9 45.8 %copy-start.12 = (f32[256,1]{1,0:T(8,128)S(1)}, f32[256,1]{1,0:T(8,128)}, u32[]{:S(2)}) copy-start(f32[256,1]{1,0:T(8,128)} %constant.41.clone.wave2) | copy-start | bytes 3076
  7.9 45.8 %all-to-all-start = ((f32[32,80,128]{2,1,0:T(8,128)}), f32[32,80,128]{2,1,0:T(8,128)S(1)}, u32[]{:S(2)}, u32[]{:S(2)}) async-start(f32[32,80,128]{2,1,0:T(8,128)} %copy-done.1), calls=%async_computation | async-start | bytes 2621440 | tf_op jit(solution)/shard_map/all_to_all | solution.py:475
  18.9 17.4 %collective-permute-start.1 = (f32[6,32,256]{2,1,0:T(8,128)}, f32[6,32,256]{2,1,0:T(8,128)S(1)}, u32[]{:S(2)}, u32[]{:S(2)}) collective-permute-start(f32[6,32,256]{2,1,0:T(8,128)} %get-tuple-element.14), channel_id=1, source_target_pairs={{8,0},{16,8},{24,16},{32,24},{40,32},{48,40},{56,48},{64,56},{72,6... | collective-permute-start | bytes 589832 | tf_op jit(solution)/shard_map/ppermute | solution.py:448
  19.2 24.6 %collective-permute-start = (f32[6,32,256]{2,1,0:T(8,128)S(1)}, f32[6,32,256]{2,1,0:T(8,128)S(1)}, u32[]{:S(2)}, u32[]{:S(2)}) collective-permute-start(f32[6,32,256]{2,1,0:T(8,128)S(1)} %get-tuple-element.15), channel_id=1, source_target_pairs={{0,8},{8,16},{16,24},{24,32},{32,40},{40,48},{48,56},{56,64},{64,7... | collective-permute-start | bytes 589832 | tf_op jit(solution)/shard_map/ppermute | solution.py:448
  55.7 56.2 %all-to-all-start.1 = ((f32[8,384,128]{2,1,0:T(8,128)}), f32[8,384,128]{2,1,0:T(8,128)S(1)}, u32[]{:S(2)}, u32[]{:S(2)}) async-start(f32[8,384,128]{2,1,0:T(8,128)} %second_kernel.1), calls=%async_computation.1 | async-start | bytes 3145728 | tf_op jit(solution)/shard_map/all_to_all | solution.py:477
  63.7 48.2 %copy-start.10 = (bf16[256,128]{1,0:T(8,128)(2,1)S(1)}, bf16[256,128]{1,0:T(8,128)(2,1)}, u32[]{:S(2)}) copy-start(bf16[256,128]{1,0:T(8,128)(2,1)} %constant.38.clone.tl) | copy-start | bytes 196612
  63.7 48.2 %copy-start.11 = (bf16[256,128]{1,0:T(8,128)(2,1)S(1)}, bf16[256,128]{1,0:T(8,128)(2,1)}, u32[]{:S(2)}) copy-start(bf16[256,128]{1,0:T(8,128)(2,1)} %constant.37.clone.th) | copy-start | bytes 196612
  64.7 64.4 %collective-permute-start.3 = (f32[108,2,256]{2,1,0:T(2,128)}, f32[108,2,256]{2,1,0:T(2,128)}, u32[]{:S(2)}, u32[]{:S(2)}) collective-permute-start(f32[108,2,256]{2,1,0:T(2,128)} %get-tuple-element.10), channel_id=1, source_target_pairs={{1,0},{2,1},{3,2},{4,3},{5,4},{6,5},{7,6},{0,7},{9,8},{10,9},{11,1... | collective-permute-start | bytes 663560 | tf_op jit(solution)/shard_map/ppermute | solution.py:448
  72.2 57.0 %copy-start.9 = (bf16[256,256]{1,0:T(8,128)(2,1)S(1)}, bf16[256,256]{1,0:T(8,128)(2,1)}, u32[]{:S(2)}) copy-start(bf16[256,256]{1,0:T(8,128)(2,1)} %constant.39.clone.table.part) | copy-start | bytes 393220
  72.2 57.0 %collective-permute-start.2 = (f32[108,2,256]{2,1,0:T(2,128)}, f32[108,2,256]{2,1,0:T(2,128)}, u32[]{:S(2)}, u32[]{:S(2)}) collective-permute-start(f32[108,2,256]{2,1,0:T(2,128)} %get-tuple-element.11), channel_id=1, source_target_pairs={{0,1},{1,2},{2,3},{3,4},{4,5},{5,6},{6,7},{7,0},{8,9},{9,10},{10,1... | collective-permute-start | bytes 663560 | tf_op jit(solution)/shard_map/ppermute | solution.py:448
  114.9 6.2 %collective-permute-start.5 = (f32[3,4,16,128]{3,2,1,0:T(8,128)S(1)}, f32[3,4,16,128]{3,2,1,0:T(8,128)S(1)}, u32[]{:S(2)}, u32[]{:S(2)}) collective-permute-start(f32[3,4,16,128]{3,2,1,0:T(8,128)S(1)} %get-tuple-element.18), channel_id=1, source_target_pairs={{8,0},{16,8},{24,16},{32,24},{40,32},{48,40},{56,48},{64,56},{72,6... | collective-permute-start | bytes 294920 | tf_op jit(solution)/shard_map/ppermute | solution.py:448
  117.5 3.7 %collective-permute-start.4 = (f32[3,4,16,128]{3,2,1,0:T(8,128)S(1)}, f32[3,4,16,128]{3,2,1,0:T(8,128)S(1)}, u32[]{:S(2)}, u32[]{:S(2)}) collective-permute-start(f32[3,4,16,128]{3,2,1,0:T(8,128)S(1)} %get-tuple-element.19), channel_id=1, source_target_pairs={{0,8},{8,16},{16,24},{24,32},{32,40},{40,48},{48,56},{56,64},{64,7... | collective-permute-start | bytes 294920 | tf_op jit(solution)/shard_map/ppermute | solution.py:448
  121.3 13.5 %collective-permute-start.6 = (f32[3,24,4,128]{3,2,1,0:T(4,128)S(1)}, f32[3,24,4,128]{3,2,1,0:T(4,128)S(1)}, u32[]{:S(2)}, u32[]{:S(2)}) collective-permute-start(f32[3,24,4,128]{3,2,1,0:T(4,128)S(1)} %pad_maximum_fusion.6), channel_id=1, source_target_pairs={{0,1},{1,2},{2,3},{3,4},{4,5},{5,6},{6,7},{7,0},{8,9},{9,10},{10,1... | collective-permute-start | bytes 442376 | tf_op jit(solution)/shard_map/ppermute | solution.py:448
  126.1 9.1 %copy-start.13 = (bf16[2,128,256]{2,1,0:T(8,128)(2,1)S(1)}, bf16[2,128,256]{2,1,0:T(8,128)(2,1)}, u32[]{:S(2)}) copy-start(bf16[2,128,256]{2,1,0:T(8,128)(2,1)} %constant.42.clone.rise) | copy-start | bytes 393220
  126.1 9.1 %collective-permute-start.7 = (f32[3,24,4,128]{3,2,1,0:T(4,128)S(1)}, f32[3,24,4,128]{3,2,1,0:T(4,128)S(1)}, u32[]{:S(2)}, u32[]{:S(2)}) collective-permute-start(f32[3,24,4,128]{3,2,1,0:T(4,128)S(1)} %pad_maximum_fusion.7), channel_id=1, source_target_pairs={{1,0},{2,1},{3,2},{4,3},{5,4},{6,5},{7,6},{0,7},{9,8},{10,9},{11,1... | collective-permute-start | bytes 442376 | tf_op jit(solution)/shard_map/ppermute | solution.py:448
  191.4 31.4 %copy-start.3 = (bf16[512,512]{1,0:T(8,128)(2,1)S(1)}, bf16[512,512]{1,0:T(8,128)(2,1)}, u32[]{:S(2)}) copy-start(bf16[512,512]{1,0:T(8,128)(2,1)} %constant.34.clone.tl) | copy-start | bytes 1572868
  191.4 31.4 %copy-start.5 = (bf16[512,512]{1,0:T(8,128)(2,1)S(1)}, bf16[512,512]{1,0:T(8,128)(2,1)}, u32[]{:S(2)}) copy-start(bf16[512,512]{1,0:T(8,128)(2,1)} %constant.33.clone.th) | copy-start | bytes 1572868

commit v6 on v5

--- a/solution.py
+++ b/solution.py
@@ -7,6 +7,7 @@
 from jax.experimental import pallas as pl
 from jax.experimental.pallas import tpu as pltpu
 from jax.sharding import PartitionSpec as P
+
 
 NSUB = 3
 STEP_RATIO = 0.08
@@ -100,7 +101,13 @@
     return HALF * (i % 2) + i // 2
 
 
-def first_kernel(spec, wave, th, tl, out, y):
+def first_kernel(spec_far, wave_far, th_far, tl_far, out, y, spec, wave, th, tl, landed):
+    far, near = (spec_far, wave_far, th_far, tl_far), (spec, wave, th, tl)
+    copies = [pltpu.make_async_copy(a, b, landed.at[n]) for n, (a, b) in enumerate(zip(far, near))]
+    for copy in copies:
+        copy.start()
+    for copy in copies:
+        copy.wait()
     even, odd = [], []
     for n, f in enumerate((0, 1, 2, 1, 2)):
         plain, turned = [], []
@@ -418,8 +425,10 @@
                 out[ri, f, r] = jnp.concatenate([e + o, e - o], axis=1)
 
 
-def call(kernel, out_shape, *args, scratch=(), late=0, hbm=False):
-    specs = [pl.BlockSpec(memory_space=pltpu.VMEM)] * (len(args) - late)
+def call(kernel, out_shape, *args, scratch=(), late=0, hbm=False, far=False):
+    if far:
+        args = [pltpu.with_memory_space_constraint(a, pltpu.HBM) for a in args]
+    specs = [pl.BlockSpec(memory_space=pltpu.HBM if far else pltpu.VMEM)] * (len(args) - late)
     specs += [pl.BlockSpec(memory_space=pl.ANY)] * late
     return pl.pallas_call(
         kernel,
@@ -428,7 +437,6 @@
         out_specs=jax.tree.map(lambda _: pl.BlockSpec(memory_space=pltpu.VMEM), out_shape),
         scratch_shapes=list(scratch),
         interpret=INTERPRET,
-        name=kernel.__name__,
         compiler_params=pltpu.CompilerParams(vmem_limit_bytes=48 * 1024 * 1024),
     )(*args)
 
@@ -445,10 +453,11 @@
 
 def edges(axis, first, last):
     up, down = ring(axis)
-    return lax.ppermute(last, axis, up), lax.ppermute(first, axis, down)
-
-
-def body(spectrum, scalar):
+    low = lax.ppermute(last, axis, up)
+    return low, lax.ppermute(first, axis, down)
+
+
+def step(spectrum, scalar):
     wave_first = waves_np(N1).astype(np.float32)[None]
     wave_second = np.repeat(waves_np(N2).astype(np.float32), 2)[:, None]
     blocks = np.tile(waves_np(N3).astype(np.float32).reshape(GY, 1, Q3), (1, 16, 1)).reshape(GY, 1, 256)
@@ -470,7 +479,15 @@
     )
     sent = call(
         first_kernel, shape(GX, 80, 128), spectrum, jnp.asarray(wave_first), *first,
-        scratch=(pltpu.VMEM((5 * N1, 128), F32),),
+        scratch=(
+            pltpu.VMEM((5 * N1, 128), F32),
+            pltpu.VMEM((2, 3, Q2, Q3, N1), F32),
+            pltpu.VMEM((1, N1), F32),
+            pltpu.VMEM((N1, N1), BF),
+            pltpu.VMEM((N1, N1), BF),
+            pltpu.SemaphoreType.DMA((4,)),
+        ),
+        far=True, hbm=True,
     )
     got = lax.all_to_all(sent, "px", split_axis=0, concat_axis=0, tiled=True)
     sent = call(second_kernel, shape(GY, 384, 128), got, jnp.asarray(wave_second), wave_third, *second, x_low, x_high, late=2, hbm=True)
@@ -516,4 +533,4 @@
 def solution(mesh):
     in_specs = (P(None, None, "px", "py", None), P("px", "py", None))
     out_specs = (P(None, None, "px", "py", None), P("px", "py", None))
-    return jax.shard_map(body, mesh=mesh, in_specs=in_specs, out_specs=out_specs, check_vma=False)
+    return jax.shard_map(step, mesh=mesh, in_specs=in_specs, out_specs=out_specs, check_vma=False)

time: 226 us -> 223 us (0.987)
  local copies, waits for them, and re-layouts: 6.55 us -> 1.6 us
  Pallas kernels: 37.8 us -> 40.4 us
    unnamed x30 -> x20, local copies, waits for them, and re-layouts: 5.01 us -> 0.06 us
    pallas_call x7, Pallas kernels: 37.8 us -> 40.4 us  [call(): pl.pallas_call(kernel, in_specs=specs, out_shape=out_shape if not hbm els...]
where the time goes in v6:
time: 223 us
  waiting for transfers between devices  76.7 us (34%)
  blocking collectives  63.7 us (29%)
  Pallas kernels  40.4 us (18%)
  starting transfers between devices  38.9 us (17%)
    pallas_call x7, Pallas kernels, call(): pl.pallas_call(kernel, in_specs=specs, out_shape=out_shape if not hbm els...  40.4 us
    all_to_all x1, waiting for transfers between devices, step(): got = lax.all_to_all(sent, 'py', split_axis=0, concat_axis=0, tiled=True)  39.7 us
    all_to_all x1, blocking collectives, step(): got = lax.all_to_all(sent, 'py', split_axis=0, concat_axis=0, tiled=True)  32.8 us
    all_to_all x1, blocking collectives, step(): got = lax.all_to_all(sent, 'px', split_axis=0, concat_axis=0, tiled=True)  30.8 us
    ppermute x4, waiting for transfers between devices, edges(): return (low, lax.ppermute(first, axis, down))  17.9 us
    ppermute x4, starting transfers between devices, edges(): return (low, lax.ppermute(first, axis, down))  13.3 us
    all_to_all x1, starting transfers between devices, step(): got = lax.all_to_all(sent, 'px', split_axis=0, concat_axis=0, tiled=True)  10.3 us
    all_to_all x1, waiting for transfers between devices, step(): got = lax.all_to_all(sent, 'px', split_axis=0, concat_axis=0, tiled=True)  9.88 us
  transfers between devices with their start and end apart: 10, of which 7 were waited for; matrix products, arithmetic and copies ran while one was open for 1% of the time, Pallas kernels for 3%

profile of v6, /device:TPU:1, one launch (start us, length us, event | category | flops | bytes accessed | tf_op | source)
XLA Modules:
  0.0 223.1 jit_solution(4251386314984554888)
XLA Ops:
  0.6 4.9 %shard_map.141 = f32[32,80,128]{2,1,0:T(8,128)} custom-call(f32[2,3,4,16,512]{4,3,2,1,0:T(8,128)} %spec_far.1, f32[1,512]{1,0:T(1,128)} %constant.40.clone.wave_far, bf16[512,512]{1,0:T(8,128)(2,1)} %constant.33.clone.th_far.th, bf16[512,512]{1,0:T(8,128)(2,1)} %constant.34.clone.tl_far.tl), custom_call_target="tpu_custom_call" | custom-call | tf_op jit(solution)/shard_map/pallas_call | solution.py:433
  5.5 0.0 copy-start
  5.5 0.0 copy-start.3
  5.5 0.0 copy-start.4
  5.5 0.0 copy-start.8
  5.6 10.3 %all-to-all-start = ((f32[32,80,128]{2,1,0:T(8,128)}), f32[32,80,128]{2,1,0:T(8,128)S(1)}, u32[]{:S(2)}, u32[]{:S(2)}) async-start(f32[32,80,128]{2,1,0:T(8,128)} %shard_map.141), calls=%async_computation | async-start | bytes 2621440 | tf_op jit(solution)/shard_map/all_to_all | solution.py:492
  15.9 0.0 copy-done
  15.9 0.7 fusion.5
  16.6 0.2 collective-permute-start.1
  16.8 1.5 collective-permute-start
  18.3 0.7 dynamic-slice_bitcast_fusion.wave3
  19.0 15.0 %collective-permute-done.1.x_high = f32[6,32,256]{2,1,0:T(8,128)S(1)} collective-permute-done((f32[6,32,256]{2,1,0:T(8,128)}, f32[6,32,256]{2,1,0:T(8,128)S(1)}, u32[]{:S(2)}, u32[]{:S(2)}) %collective-permute-start.1) | collective-permute-done | bytes 196640 | tf_op jit(solution)/shard_map/ppermute | solution.py:457
  34.0 7.5 %collective-permute-done.x_low = f32[6,32,256]{2,1,0:T(8,128)S(1)} collective-permute-done((f32[6,32,256]{2,1,0:T(8,128)S(1)}, f32[6,32,256]{2,1,0:T(8,128)S(1)}, u32[]{:S(2)}, u32[]{:S(2)}) %collective-permute-start) | collective-permute-done | bytes 196640 | tf_op jit(solution)/shard_map/ppermute | solution.py:456
  41.5 9.9 %all-to-all-done.got = f32[32,80,128]{2,1,0:T(8,128)S(1)} async-done(((f32[32,80,128]{2,1,0:T(8,128)}), f32[32,80,128]{2,1,0:T(8,128)S(1)}, u32[]{:S(2)}, u32[]{:S(2)}) %all-to-all-start) | async-done | bytes 1310752 | tf_op jit(solution)/shard_map/all_to_all | solution.py:492
  51.3 0.0 copy-done.3
  51.3 0.0 copy-done.4
  51.4 0.0 copy-done.8
  51.4 2.0 shard_map.142
  53.4 8.0 %all-to-all-start.1 = ((f32[8,384,128]{2,1,0:T(8,128)}), f32[8,384,128]{2,1,0:T(8,128)S(1)}, u32[]{:S(2)}, u32[]{:S(2)}) async-start(f32[8,384,128]{2,1,0:T(8,128)} %shard_map.142), calls=%async_computation.1 | async-start | bytes 3145728 | tf_op jit(solution)/shard_map/all_to_all | solution.py:494
  61.4 0.0 copy-start.7
  61.4 0.1 fusion.4
  61.5 0.9 fusion.1
  62.4 7.5 %collective-permute-start.3 = (f32[108,2,256]{2,1,0:T(2,128)}, f32[108,2,256]{2,1,0:T(2,128)}, u32[]{:S(2)}, u32[]{:S(2)}) collective-permute-start(f32[108,2,256]{2,1,0:T(2,128)} %get-tuple-element.10), channel_id=1, source_target_pairs={{1,0},{2,1},{3,2},{4,3},{5,4},{6,5},{7,6},{0,7},{9,8},{10,9},{11,1... | collective-permute-start | bytes 663560 | tf_op jit(solution)/shard_map/ppermute | solution.py:457
  69.9 0.0 collective-permute-start.2
  69.9 39.7 %all-to-all-done.1.got = f32[8,384,128]{2,1,0:T(8,128)S(1)} async-done(((f32[8,384,128]{2,1,0:T(8,128)}), f32[8,384,128]{2,1,0:T(8,128)S(1)}, u32[]{:S(2)}, u32[]{:S(2)}) %all-to-all-start.1) | async-done | bytes 1572896 | tf_op jit(solution)/shard_map/all_to_all | solution.py:494
  109.6 0.0 copy-done.6
  109.6 0.0 copy-done.7
  109.6 3.0 %shard_map.143 = (f32[3,16,16,128]{3,2,1,0:T(8,128)S(1)}, f32[3,16,16,128]{3,2,1,0:T(8,128)S(1)}) custom-call(f32[8,384,128]{2,1,0:T(8,128)S(1)} %all-to-all-done.1.got, bf16[256,128]{1,0:T(8,128)(2,1)S(1)} %copy-done.7, bf16[256,128]{1,0:T(8,128)(2,1)S(1)} %copy-done.6), custom_call_target="tpu_custom_call" | custom-call | tf_op jit(solution)/shard_map/pallas_call | solution.py:433
  112.6 2.5 %collective-permute-start.5 = (f32[3,4,16,128]{3,2,1,0:T(8,128)S(1)}, f32[3,4,16,128]{3,2,1,0:T(8,128)S(1)}, u32[]{:S(2)}, u32[]{:S(2)}) collective-permute-start(f32[3,4,16,128]{3,2,1,0:T(8,128)S(1)} %get-tuple-element.18), channel_id=1, source_target_pairs={{8,0},{16,8},{24,16},{32,24},{40,32},{48,40},{56,48},{64,56},{72,6... | collective-permute-start | bytes 294920 | tf_op jit(solution)/shard_map/ppermute | solution.py:457
  115.2 1.1 collective-permute-start.4
  116.3 2.6 %collective-permute-done.5.vx_high = f32[3,4,16,128]{3,2,1,0:T(8,128)S(1)} collective-permute-done((f32[3,4,16,128]{3,2,1,0:T(8,128)S(1)}, f32[3,4,16,128]{3,2,1,0:T(8,128)S(1)}, u32[]{:S(2)}, u32[]{:S(2)}) %collective-permute-start.5) | collective-permute-done | bytes 98336 | tf_op jit(solution)/shard_map/ppermute | solution.py:457
  118.9 0.0 collective-permute-done.4.vx_low
  119.0 4.8 %collective-permute-start.6 = (f32[3,24,4,128]{3,2,1,0:T(4,128)S(1)}, f32[3,24,4,128]{3,2,1,0:T(4,128)S(1)}, u32[]{:S(2)}, u32[]{:S(2)}) collective-permute-start(f32[3,24,4,128]{3,2,1,0:T(4,128)S(1)} %pad_maximum_fusion.6), channel_id=1, source_target_pairs={{0,1},{1,2},{2,3},{3,4},{4,5},{5,6},{6,7},{7,0},{8,9},{9,10},{10,1... | collective-permute-start | bytes 442376 | tf_op jit(solution)/shard_map/ppermute | solution.py:456
  123.7 0.0 copy-start.9
  123.8 3.1 %collective-permute-start.7 = (f32[3,24,4,128]{3,2,1,0:T(4,128)S(1)}, f32[3,24,4,128]{3,2,1,0:T(4,128)S(1)}, u32[]{:S(2)}, u32[]{:S(2)}) collective-permute-start(f32[3,24,4,128]{3,2,1,0:T(4,128)S(1)} %pad_maximum_fusion.7), channel_id=1, source_target_pairs={{1,0},{2,1},{3,2},{4,3},{5,4},{6,5},{7,6},{0,7},{9,8},{10,9},{11,1... | collective-permute-start | bytes 442376 | tf_op jit(solution)/shard_map/ppermute | solution.py:457
  126.8 0.0 collective-permute-done.3.y_high
  126.8 0.0 collective-permute-done.2.y_low
  126.8 0.0 copy-done.5
  126.8 4.0 %shard_map.140.brick = f32[44,2,48,128]{3,2,1,0:T(8,128)S(1)} custom-call(f32[32,32,256]{2,1,0:T(8,128)S(1)} %copy-done, f32[6,32,256]{2,1,0:T(8,128)S(1)} %collective-permute-done.x_low, f32[6,32,256]{2,1,0:T(8,128)S(1)} %collective-permute-done.1.x_high, f32[108,2,256]{2,1,0:T(2,128)} %collective-permute-done.2.y_low, ...), custom_call_target="tpu_custom_call" | custom-call | tf_op jit(solution)/shard_map/pallas_call | solution.py:433
  130.8 1.7 collective-permute-done.6.vy_low
  132.5 0.4 collective-permute-done.7.vy_high
  132.9 0.0 copy-done.9
  132.9 23.4 %shard_map.144 = (f32[32,32,256]{2,1,0:T(8,128)}, f32[8,192,128]{2,1,0:T(8,128)S(1)}) custom-call(f32[44,2,48,128]{3,2,1,0:T(8,128)S(1)} %shard_map.140.brick, f32[3,16,16,128]{3,2,1,0:T(8,128)S(1)} %get-tuple-element.6.velocity, f32[3,4,16,128]{3,2,1,0:T(8,128)S(1)} %collective-permute-done.4.vx_low, f32[3,4,16,128]{3,2,1,0:T(8,128)S(1)} %collective-permute-done.5.vx_high, ...), custom_call_target="tpu_custom_call" | custom-call | tf_op jit(solution)/shard_map/pallas_call | solution.py:433
  156.2 32.8 %all_to_all.20.got = f32[8,192,128]{2,1,0:T(8,128)S(1)} all-to-all(f32[8,192,128]{2,1,0:T(8,128)S(1)} %get-tuple-element.8), channel_id=1, replica_groups=mesh['px'=32,'py'=8] {'py'}, dimensions={0} | all-to-all | bytes 1572864 | tf_op jit(solution)/shard_map/all_to_all | solution.py:521
  189.1 0.5 shard_map.145
  189.6 30.8 %all_to_all.21.got = f32[32,48,128]{2,1,0:T(8,128)S(1)} all-to-all(f32[32,48,128]{2,1,0:T(8,128)S(1)} %shard_map.145), channel_id=1, replica_groups=mesh['px'=32,'py'=8] {'px'}, dimensions={0} | all-to-all | bytes 1572864 | tf_op jit(solution)/shard_map/all_to_all | solution.py:525
  220.4 0.0 copy-done.2
  220.4 2.6 %shard_map.146 = f32[2,3,4,16,512]{4,3,2,1,0:T(8,128)} custom-call(f32[32,48,128]{2,1,0:T(8,128)S(1)} %all_to_all.21.got, bf16[512,512]{1,0:T(8,128)(2,1)S(1)} %copy-done.2, bf16[512,512]{1,0:T(8,128)(2,1)S(1)} %copy-done.1), custom_call_target="tpu_custom_call" | custom-call | tf_op jit(solution)/shard_map/pallas_call | solution.py:433
  (13 shorter events, 0.2 us)
Async XLA Ops:
  5.5 10.4 %copy-start = (f32[32,32,256]{2,1,0:T(8,128)S(1)}, f32[32,32,256]{2,1,0:T(8,128)}, u32[]{:S(2)}) copy-start(f32[32,32,256]{2,1,0:T(8,128)} %scalar.1) | copy-start | bytes 3145732
  5.5 45.8 %copy-start.3 = (bf16[256,256]{1,0:T(8,128)(2,1)S(1)}, bf16[256,256]{1,0:T(8,128)(2,1)}, u32[]{:S(2)}) copy-start(bf16[256,256]{1,0:T(8,128)(2,1)} %constant.36.clone.tl) | copy-start | bytes 393220
  5.5 45.8 %copy-start.4 = (bf16[256,256]{1,0:T(8,128)(2,1)S(1)}, bf16[256,256]{1,0:T(8,128)(2,1)}, u32[]{:S(2)}) copy-start(bf16[256,256]{1,0:T(8,128)(2,1)} %constant.35.clone.th) | copy-start | bytes 393220
  5.5 45.8 %copy-start.8 = (f32[256,1]{1,0:T(8,128)S(1)}, f32[256,1]{1,0:T(8,128)}, u32[]{:S(2)}) copy-start(f32[256,1]{1,0:T(8,128)} %constant.41.clone.wave2) | copy-start | bytes 3076
  5.6 45.8 %all-to-all-start = ((f32[32,80,128]{2,1,0:T(8,128)}), f32[32,80,128]{2,1,0:T(8,128)S(1)}, u32[]{:S(2)}, u32[]{:S(2)}) async-start(f32[32,80,128]{2,1,0:T(8,128)} %shard_map.141), calls=%async_computation | async-start | bytes 2621440 | tf_op jit(solution)/shard_map/all_to_all | solution.py:492
  16.6 17.4 %collective-permute-start.1 = (f32[6,32,256]{2,1,0:T(8,128)}, f32[6,32,256]{2,1,0:T(8,128)S(1)}, u32[]{:S(2)}, u32[]{:S(2)}) collective-permute-start(f32[6,32,256]{2,1,0:T(8,128)} %get-tuple-element.14), channel_id=1, source_target_pairs={{8,0},{16,8},{24,16},{32,24},{40,32},{48,40},{56,48},{64,56},{72,6... | collective-permute-start | bytes 589832 | tf_op jit(solution)/shard_map/ppermute | solution.py:457
  16.8 24.6 %collective-permute-start = (f32[6,32,256]{2,1,0:T(8,128)S(1)}, f32[6,32,256]{2,1,0:T(8,128)S(1)}, u32[]{:S(2)}, u32[]{:S(2)}) collective-permute-start(f32[6,32,256]{2,1,0:T(8,128)S(1)} %get-tuple-element.15), channel_id=1, source_target_pairs={{0,8},{8,16},{16,24},{24,32},{32,40},{40,48},{48,56},{56,64},{64,7... | collective-permute-start | bytes 589832 | tf_op jit(solution)/shard_map/ppermute | solution.py:456
  53.4 56.2 %all-to-all-start.1 = ((f32[8,384,128]{2,1,0:T(8,128)}), f32[8,384,128]{2,1,0:T(8,128)S(1)}, u32[]{:S(2)}, u32[]{:S(2)}) async-start(f32[8,384,128]{2,1,0:T(8,128)} %shard_map.142), calls=%async_computation.1 | async-start | bytes 3145728 | tf_op jit(solution)/shard_map/all_to_all | solution.py:494
  61.3 48.2 %copy-start.6 = (bf16[256,128]{1,0:T(8,128)(2,1)S(1)}, bf16[256,128]{1,0:T(8,128)(2,1)}, u32[]{:S(2)}) copy-start(bf16[256,128]{1,0:T(8,128)(2,1)} %constant.38.clone.tl) | copy-start | bytes 196612
  61.4 48.2 %copy-start.7 = (bf16[256,128]{1,0:T(8,128)(2,1)S(1)}, bf16[256,128]{1,0:T(8,128)(2,1)}, u32[]{:S(2)}) copy-start(bf16[256,128]{1,0:T(8,128)(2,1)} %constant.37.clone.th) | copy-start | bytes 196612
  62.4 64.4 %collective-permute-start.3 = (f32[108,2,256]{2,1,0:T(2,128)}, f32[108,2,256]{2,1,0:T(2,128)}, u32[]{:S(2)}, u32[]{:S(2)}) collective-permute-start(f32[108,2,256]{2,1,0:T(2,128)} %get-tuple-element.10), channel_id=1, source_target_pairs={{1,0},{2,1},{3,2},{4,3},{5,4},{6,5},{7,6},{0,7},{9,8},{10,9},{11,1... | collective-permute-start | bytes 663560 | tf_op jit(solution)/shard_map/ppermute | solution.py:457
  69.9 57.0 %copy-start.5 = (bf16[256,256]{1,0:T(8,128)(2,1)S(1)}, bf16[256,256]{1,0:T(8,128)(2,1)}, u32[]{:S(2)}) copy-start(bf16[256,256]{1,0:T(8,128)(2,1)} %constant.39.clone.table.part) | copy-start | bytes 393220
  69.9 57.0 %collective-permute-start.2 = (f32[108,2,256]{2,1,0:T(2,128)}, f32[108,2,256]{2,1,0:T(2,128)}, u32[]{:S(2)}, u32[]{:S(2)}) collective-permute-start(f32[108,2,256]{2,1,0:T(2,128)} %get-tuple-element.11), channel_id=1, source_target_pairs={{0,1},{1,2},{2,3},{3,4},{4,5},{5,6},{6,7},{7,0},{8,9},{9,10},{10,1... | collective-permute-start | bytes 663560 | tf_op jit(solution)/shard_map/ppermute | solution.py:456
  112.6 6.3 %collective-permute-start.5 = (f32[3,4,16,128]{3,2,1,0:T(8,128)S(1)}, f32[3,4,16,128]{3,2,1,0:T(8,128)S(1)}, u32[]{:S(2)}, u32[]{:S(2)}) collective-permute-start(f32[3,4,16,128]{3,2,1,0:T(8,128)S(1)} %get-tuple-element.18), channel_id=1, source_target_pairs={{8,0},{16,8},{24,16},{32,24},{40,32},{48,40},{56,48},{64,56},{72,6... | collective-permute-start | bytes 294920 | tf_op jit(solution)/shard_map/ppermute | solution.py:457
  115.2 3.7 %collective-permute-start.4 = (f32[3,4,16,128]{3,2,1,0:T(8,128)S(1)}, f32[3,4,16,128]{3,2,1,0:T(8,128)S(1)}, u32[]{:S(2)}, u32[]{:S(2)}) collective-permute-start(f32[3,4,16,128]{3,2,1,0:T(8,128)S(1)} %get-tuple-element.19), channel_id=1, source_target_pairs={{0,8},{8,16},{16,24},{24,32},{32,40},{40,48},{48,56},{56,64},{64,7... | collective-permute-start | bytes 294920 | tf_op jit(solution)/shard_map/ppermute | solution.py:456
  119.0 13.5 %collective-permute-start.6 = (f32[3,24,4,128]{3,2,1,0:T(4,128)S(1)}, f32[3,24,4,128]{3,2,1,0:T(4,128)S(1)}, u32[]{:S(2)}, u32[]{:S(2)}) collective-permute-start(f32[3,24,4,128]{3,2,1,0:T(4,128)S(1)} %pad_maximum_fusion.6), channel_id=1, source_target_pairs={{0,1},{1,2},{2,3},{3,4},{4,5},{5,6},{6,7},{7,0},{8,9},{9,10},{10,1... | collective-permute-start | bytes 442376 | tf_op jit(solution)/shard_map/ppermute | solution.py:456
  123.7 9.1 %copy-start.9 = (bf16[2,128,256]{2,1,0:T(8,128)(2,1)S(1)}, bf16[2,128,256]{2,1,0:T(8,128)(2,1)}, u32[]{:S(2)}) copy-start(bf16[2,128,256]{2,1,0:T(8,128)(2,1)} %constant.42.clone.rise) | copy-start | bytes 393220
  123.8 9.1 %collective-permute-start.7 = (f32[3,24,4,128]{3,2,1,0:T(4,128)S(1)}, f32[3,24,4,128]{3,2,1,0:T(4,128)S(1)}, u32[]{:S(2)}, u32[]{:S(2)}) collective-permute-start(f32[3,24,4,128]{3,2,1,0:T(4,128)S(1)} %pad_maximum_fusion.7), channel_id=1, source_target_pairs={{1,0},{2,1},{3,2},{4,3},{5,4},{6,5},{7,6},{0,7},{9,8},{10,9},{11,1... | collective-permute-start | bytes 442376 | tf_op jit(solution)/shard_map/ppermute | solution.py:457
  189.1 31.4 %copy-start.1 = (bf16[512,512]{1,0:T(8,128)(2,1)S(1)}, bf16[512,512]{1,0:T(8,128)(2,1)}, u32[]{:S(2)}) copy-start(bf16[512,512]{1,0:T(8,128)(2,1)} %constant.34.clone.tl_far.tl) | copy-start | bytes 1572868
  189.1 31.4 %copy-start.2 = (bf16[512,512]{1,0:T(8,128)(2,1)S(1)}, bf16[512,512]{1,0:T(8,128)(2,1)}, u32[]{:S(2)}) copy-start(bf16[512,512]{1,0:T(8,128)(2,1)} %constant.33.clone.th_far.th) | copy-start | bytes 1572868
